TPU v7x, 32 devices: a whole 2x2x4 slice. The times are simulated.
32 devices in a mesh: row: 4 (over z), col: 4 (over x, core), mp: 2 (over y).
Axes of the slice: x: 2, y: 2, z: 4, core: 2. Of those that a mesh axis runs over, the one named last changes fastest.
Arguments:
- weights: bfloat16 [4, 4, 5, 2304, 1024], P('row', 'col', None, None, 'mp'), may hold values from -6 to 6
- warm_down: bfloat16 [4, 4, 5, 4, 1024], P('row', 'col', None, None, 'mp'), may hold values from -6 to 6
- warm_right: bfloat16 [4, 4, 5, 4, 1024], P('row', 'col', None, None, 'mp'), may hold values from -6 to 6
Outputs:
- new_weights: bfloat16 [4, 4, 5, 2304, 1024], P('row', 'col', None, None, 'mp')
- next_down: float32 [4, 4, 5, 4, 1024], P('row', 'col', None, None, 'mp')
- next_right: float32 [4, 4, 5, 4, 1024], P('row', 'col', None, None, 'mp')
All inputs are finite; a program needn't handle non-finite values.
Results may differ from a plain program's by a relative error of at most 0.0085.
Values may be sent and summed in bfloat16 or wider, within the bound.
No kernel may reach another device: no remote copies, remote signals or barrier semaphores. Data moves between devices by JAX's collectives and lax.ppermute only.
A program may use at most 128 MiB of HBM per device.

v0:
```python
import jax
import jax.numpy as jnp
from jax import lax
from jax.sharding import PartitionSpec as P

ROUNDS = 2


step_size = 0.2
epsilon = 1e-06


def passed_along(value, axis, by):
    devices = lax.axis_size(axis)
    return lax.ppermute(value, axis, [(i, (i + by) % devices) for i in range(devices)])


def orthonormal(vectors):
    basis = []
    for column in range(vectors.shape[-2]):
        source = vectors[..., column, :]
        update = source
        for earlier in basis:
            update = update - jnp.sum(source * earlier, axis=-1, keepdims=True) * earlier
        basis.append(update / jnp.sqrt(jnp.sum(update * update, axis=-1, keepdims=True) + epsilon))
    return jnp.stack(basis, axis=-2)


def neighbours(payload):
    from_above = passed_along(payload[:, 1].astype(jnp.bfloat16), "row", 1).astype(jnp.float32)
    from_below = passed_along(payload[:, 0], "row", -1)
    from_left = passed_along(payload[:, 3].astype(jnp.bfloat16), "col", 1).astype(jnp.float32)
    from_right = passed_along(payload[:, 2].astype(jnp.bfloat16), "col", -1).astype(jnp.float32)
    return jnp.stack([from_above, from_below, from_left, from_right], 1)


def gossip_round(layers, factors):
    partial_rows = jnp.einsum("lerk,ldk->lerd", factors, layers, preferred_element_type=jnp.float32)
    totals = lax.psum(partial_rows, "mp")
    difference = totals - neighbours(totals)
    basis = orthonormal(difference).astype(jnp.bfloat16)
    own_back = jnp.einsum("lerd,ldk->lerk", basis, layers, preferred_element_type=jnp.float32)
    combined = own_back + neighbours(own_back)
    next_factors = combined.astype(jnp.bfloat16)
    count_layers = layers.shape[0]
    flat_basis = basis.reshape(count_layers, -1, basis.shape[-1])
    flat_factors = next_factors.reshape(count_layers, -1, next_factors.shape[-1])
    correction = jnp.einsum(
        "lsd,lsk->ldk", flat_basis, flat_factors, preferred_element_type=jnp.float32
    )
    updated = (layers.astype(jnp.float32) - step_size * correction).astype(jnp.bfloat16)
    return (updated, next_factors, combined)


def body(weights, warm_down, warm_right):
    above = passed_along(warm_down, "row", 1)
    beside = passed_along(warm_right, "col", 1)
    layers = weights[0, 0]
    factors = jnp.stack([above[0, 0], warm_down[0, 0], beside[0, 0], warm_right[0, 0]], axis=1)
    combined = jnp.zeros(factors.shape, jnp.float32)
    for repeat in range(ROUNDS):
        layers, factors, combined = gossip_round(layers, factors)
    return (layers[None, None], combined[:, 1][None, None], combined[:, 3][None, None])


def solution(mesh):
    placed = (
        P("row", "col", None, None, "mp"),
        P("row", "col", None, None, "mp"),
        P("row", "col", None, None, "mp"),
    )
    return jax.shard_map(
        body,
        mesh=mesh,
        in_specs=placed,
        out_specs=(
            P("row", "col", None, None, "mp"),
            P("row", "col", None, None, "mp"),
            P("row", "col", None, None, "mp"),
        ),
        check_vma=False,
    )
```

profile of v0, /device:TPU:0, one launch (start us, length us, event | category | flops | bytes accessed | tf_op | source)
XLA Modules:
  0.0 180.7 jit_solution(14943097519896180930)
XLA Ops:
  7.2 3.1 %collective-permute-start = (bf16[1,1,5,4,512]{4,3,2,1,0:T(4,128)(2,1)}, bf16[1,1,5,4,512]{4,3,2,1,0:T(4,128)(2,1)S(1)}, u32[]{:S(2)}, u32[]{:S(2)}) collective-permute-start(bf16[1,1,5,4,512]{4,3,2,1,0:T(4,128)(2,1)} %param.4), channel_id=1, source_target_pairs={{0,8},{8,16},{16,24},{24,0},{1,9},{9,17},{17,25},{25,1},{2,10},{10... | collective-permute-start | bytes 61448 | tf_op jit(solution)/shard_map/ppermute | solution.py:15
  10.3 4.0 %collective-permute-done = bf16[1,1,5,4,512]{4,3,2,1,0:T(4,128)(2,1)S(1)} collective-permute-done((bf16[1,1,5,4,512]{4,3,2,1,0:T(4,128)(2,1)}, bf16[1,1,5,4,512]{4,3,2,1,0:T(4,128)(2,1)S(1)}, u32[]{:S(2)}, u32[]{:S(2)}) %collective-permute-start) | collective-permute-done | bytes 20512 | tf_op jit(solution)/shard_map/ppermute | solution.py:15
  14.3 8.5 %fusion.6 = f32[5,4,4,2304]{3,2,1,0:T(4,128)} fusion(bf16[1,1,5,2304,512]{4,3,2,1,0:T(8,128)(2,1)} %param.3, bf16[5,1,4,512]{3,2,1,0:T(4,128)(2,1)} %bitcast.260, bf16[5,1,4,512]{3,2,1,0:T(4,128)(2,1)S(1)} %bitcast.263, bf16[5,1,4,512]{3,2,1,0:T(4,128)(2,1)} %bitcast.261, bf16[5,1,4,512]{3,2,1,0:T(4,128)(2,1)S(1)} %bitcast.262), kind=kOutput, calls=%fused_computation.8 | convolution fusion | flops 189071360 | bytes 12615680 | tf_op jit(solution)/shard_map/lerk,ldk->lerd/dot_general | solution.py:38
  22.9 33.1 %all-reduce.3.cloned.1.call-done = f32[5,4,4,2304]{3,2,1,0:T(4,128)} async-done(((f32[5,4,4,2304]{3,2,1,0:T(4,128)}), f32[5,4,4,2304]{3,2,1,0:T(4,128)}) %all-reduce.3.cloned.1.call-update) | async-done | bytes 737296 | tf_op jit(solution)/shard_map/psum | solution.py:39
  56.0 1.2 slice_bitcast_fusion.7
  57.2 1.5 collective-permute-start.2
  58.7 0.9 slice_bitcast_fusion.1
  59.6 2.4 %collective-permute-start.3 = (f32[5,4,2304]{2,1,0:T(4,128)S(1)}, f32[5,4,2304]{2,1,0:T(4,128)S(1)}, u32[]{:S(2)}, u32[]{:S(2)}) collective-permute-start(f32[5,4,2304]{2,1,0:T(4,128)S(1)} %slice_bitcast_fusion.1), channel_id=1, source_target_pairs={{0,24},{8,0},{16,8},{24,16},{1,25},{9,1},{17,9},{25,17},{2,26},{10... | collective-permute-start | bytes 552968 | tf_op jit(solution)/shard_map/ppermute | solution.py:15
  62.2 0.3 collective-permute-start.4
  62.5 1.1 collective-permute-done.2
  63.7 0.9 collective-permute-done.5
  64.6 2.4 %collective-permute-done.4 = bf16[5,4,2304]{2,1,0:T(4,128)(2,1)S(1)} collective-permute-done((bf16[5,4,2304]{2,1,0:T(4,128)(2,1)S(1)}, bf16[5,4,2304]{2,1,0:T(4,128)(2,1)S(1)}, u32[]{:S(2)}, u32[]{:S(2)}) %collective-permute-start.4) | collective-permute-done | bytes 92192 | tf_op jit(solution)/shard_map/ppermute | solution.py:15
  67.2 1.4 maximum_subtract_fusion
  68.6 0.5 fusion.44
  69.5 0.3 fusion.19
  70.6 0.3 fusion.25
  70.9 1.7 subtract_divide_fusion.3
  72.6 0.9 maximum_convert_fusion
  73.5 6.1 %fusion.4 = f32[5,4,4,512]{3,2,1,0:T(4,128)S(1)} fusion(bf16[5,4,4,2304]{3,2,1,0:T(4,128)(2,1)S(1)} %maximum_convert_fusion, bf16[1,1,5,2304,512]{4,3,2,1,0:T(8,128)(2,1)} %param.3), kind=kOutput, calls=%fused_computation.6 | convolution fusion | flops 188743680 | bytes 12328960 | tf_op jit(solution)/shard_map/lerd,ldk->lerk/dot_general | solution.py:42
  79.6 0.9 collective-permute-start.6
  80.6 3.0 %collective-permute-start.7 = (f32[5,4,512]{2,1,0:T(4,128)S(1)}, f32[5,4,512]{2,1,0:T(4,128)S(1)}, u32[]{:S(2)}, u32[]{:S(2)}) collective-permute-start(f32[5,4,512]{2,1,0:T(4,128)S(1)} %slice_bitcast_fusion.11), channel_id=1, source_target_pairs={{0,24},{8,0},{16,8},{24,16},{1,25},{9,1},{17,9},{25,17},{2,26},{10... | collective-permute-start | bytes 122888 | tf_op jit(solution)/shard_map/ppermute | solution.py:15
  84.2 1.1 collective-permute-done.6
  85.4 1.7 collective-permute-done.8
  87.2 8.9 %subtract_convert_fusion.1 = bf16[5,2304,512]{2,1,0:T(8,128)(2,1)} fusion(bf16[5,16,2304]{2,1,0:T(8,128)(2,1)S(1)} %convert_element_type.97, bf16[5,16,512]{2,1,0:T(8,128)(2,1)S(1)} %reshape.90, bf16[1,1,5,2304,512]{4,3,2,1,0:T(8,128)(2,1)} %param.3), kind=kOutput, calls=%fused_computation.1 | convolution fusion | flops 212336640 | bytes 24043520 | tf_op jit(solution)/shard_map/lsd,lsk->ldk/dot_general | solution.py:48
  96.2 8.5 %fusion.2 = f32[5,4,4,2304]{3,2,1,0:T(4,128)} fusion(bf16[5,4,4,512]{3,2,1,0:T(4,128)(2,1)S(1)} %fusion.29, bf16[5,2304,512]{2,1,0:T(8,128)(2,1)} %subtract_convert_fusion.1), kind=kOutput, calls=%fused_computation.4 | convolution fusion | flops 188743680 | bytes 12615680 | tf_op jit(solution)/shard_map/lerk,ldk->lerd/dot_general | solution.py:38
  104.6 32.4 %all-reduce.5.cloned.1.call-done = f32[5,4,4,2304]{3,2,1,0:T(4,128)} async-done(((f32[5,4,4,2304]{3,2,1,0:T(4,128)}), f32[5,4,4,2304]{3,2,1,0:T(4,128)}) %all-reduce.5.cloned.1.call-update) | async-done | bytes 737296 | tf_op jit(solution)/shard_map/psum | solution.py:39
  137.1 1.3 slice_bitcast_fusion.4
  138.4 1.5 collective-permute-start.10
  140.0 1.7 slice_bitcast_fusion
  141.6 2.1 %collective-permute-start.11 = (f32[5,4,2304]{2,1,0:T(4,128)S(1)}, f32[5,4,2304]{2,1,0:T(4,128)S(1)}, u32[]{:S(2)}, u32[]{:S(2)}) collective-permute-start(f32[5,4,2304]{2,1,0:T(4,128)S(1)} %slice_bitcast_fusion), channel_id=1, source_target_pairs={{0,24},{8,0},{16,8},{24,16},{1,25},{9,1},{17,9},{25,17},{2,26},{10... | collective-permute-start | bytes 552968 | tf_op jit(solution)/shard_map/ppermute | solution.py:15
  143.8 0.4 collective-permute-start.12
  144.3 0.7 collective-permute-done.10
  145.0 1.1 collective-permute-done.13
  146.1 2.7 %collective-permute-done.12 = bf16[5,4,2304]{2,1,0:T(4,128)(2,1)S(1)} collective-permute-done((bf16[5,4,2304]{2,1,0:T(4,128)(2,1)S(1)}, bf16[5,4,2304]{2,1,0:T(4,128)(2,1)S(1)}, u32[]{:S(2)}, u32[]{:S(2)}) %collective-permute-start.12) | collective-permute-done | bytes 92192 | tf_op jit(solution)/shard_map/ppermute | solution.py:15
  148.8 1.4 maximum_subtract_fusion.1
  150.1 0.5 fusion.43
  151.0 0.3 fusion.9
  152.1 0.3 fusion.15
  152.5 1.7 subtract_divide_fusion
  154.2 0.9 maximum_convert_fusion.1
  155.1 1.8 fusion
  156.9 0.6 collective-permute-start.14
  157.6 3.3 %collective-permute-start.15 = (f32[5,4,512]{2,1,0:T(4,128)S(1)}, f32[5,4,512]{2,1,0:T(4,128)S(1)}, u32[]{:S(2)}, u32[]{:S(2)}) collective-permute-start(f32[5,4,512]{2,1,0:T(4,128)S(1)} %slice_bitcast_fusion.10), channel_id=1, source_target_pairs={{0,24},{8,0},{16,8},{24,16},{1,25},{9,1},{17,9},{25,17},{2,26},{10... | collective-permute-start | bytes 122888 | tf_op jit(solution)/shard_map/ppermute | solution.py:15
  160.9 0.5 collective-permute-start.16
  161.4 1.2 collective-permute-done.14
  162.6 1.6 collective-permute-done.16
  164.3 0.6 slice_bitcast_fusion.8
  164.9 8.9 %fusion.8 = bf16[1,1,5,2304,512]{4,3,2,1,0:T(8,128)(2,1)} fusion(bf16[5,16,2304]{2,1,0:T(8,128)(2,1)S(1)} %convert_element_type.108, bf16[5,16,512]{2,1,0:T(8,128)(2,1)S(1)} %reshape.91, bf16[5,2304,512]{2,1,0:T(8,128)(2,1)} %subtract_convert_fusion.1), kind=kOutput, calls=%fused_computation.10 | convolution fusion | flops 212336640 | bytes 24043520 | tf_op jit(solution)/shard_map/lsd,lsk->ldk/dot_general | solution.py:48
  (59 shorter events, 4.0 us)
Async XLA Ops:
  7.2 48.8 %all-reduce.3.cloned.1.call-start = ((), (), s32[]{:S(2)}) async-start(), calls=%async_computation | async-start | bytes 1474560 | tf_op jit(solution)/shard_map/psum | solution.py:39
  7.2 7.1 %collective-permute-start = (bf16[1,1,5,4,512]{4,3,2,1,0:T(4,128)(2,1)}, bf16[1,1,5,4,512]{4,3,2,1,0:T(4,128)(2,1)S(1)}, u32[]{:S(2)}, u32[]{:S(2)}) collective-permute-start(bf16[1,1,5,4,512]{4,3,2,1,0:T(4,128)(2,1)} %param.4), channel_id=1, source_target_pairs={{0,8},{8,16},{16,24},{24,0},{1,9},{9,17},{17,25},{25,1},{2,10},{10... | collective-permute-start | bytes 61448 | tf_op jit(solution)/shard_map/ppermute | solution.py:15
  10.3 4.0 %collective-permute-start.1 = (bf16[1,1,5,4,512]{4,3,2,1,0:T(4,128)(2,1)}, bf16[1,1,5,4,512]{4,3,2,1,0:T(4,128)(2,1)S(1)}, u32[]{:S(2)}, u32[]{:S(2)}) collective-permute-start(bf16[1,1,5,4,512]{4,3,2,1,0:T(4,128)(2,1)} %param.5), channel_id=1, source_target_pairs={{0,2},{2,4},{4,6},{6,0},{1,3},{3,5},{5,7},{7,1},{8,10},{10,12},{12... | collective-permute-start | bytes 61448 | tf_op jit(solution)/shard_map/ppermute | solution.py:15
  22.8 114.2 %all-reduce.5.cloned.1.call-start = ((), (), s32[]{:S(2)}) async-start(), calls=%async_computation.1 | async-start | bytes 1474560 | tf_op jit(solution)/shard_map/psum | solution.py:39
  57.2 6.5 %collective-permute-start.2 = (bf16[5,4,2304]{2,1,0:T(4,128)(2,1)S(1)}, bf16[5,4,2304]{2,1,0:T(4,128)(2,1)S(1)}, u32[]{:S(2)}, u32[]{:S(2)}) collective-permute-start(bf16[5,4,2304]{2,1,0:T(4,128)(2,1)S(1)} %get-tuple-element.42), channel_id=1, source_target_pairs={{0,8},{8,16},{16,24},{24,0},{1,9},{9,17},{17,25},{25,1},{2,10},{10... | collective-permute-start | bytes 276488 | tf_op jit(solution)/shard_map/ppermute | solution.py:15
  59.6 7.6 %collective-permute-start.3 = (f32[5,4,2304]{2,1,0:T(4,128)S(1)}, f32[5,4,2304]{2,1,0:T(4,128)S(1)}, u32[]{:S(2)}, u32[]{:S(2)}) collective-permute-start(f32[5,4,2304]{2,1,0:T(4,128)S(1)} %slice_bitcast_fusion.1), channel_id=1, source_target_pairs={{0,24},{8,0},{16,8},{24,16},{1,25},{9,1},{17,9},{25,17},{2,26},{10... | collective-permute-start | bytes 552968 | tf_op jit(solution)/shard_map/ppermute | solution.py:15
  62.0 2.5 %collective-permute-start.5 = (bf16[5,4,2304]{2,1,0:T(4,128)(2,1)S(1)}, bf16[5,4,2304]{2,1,0:T(4,128)(2,1)S(1)}, u32[]{:S(2)}, u32[]{:S(2)}) collective-permute-start(bf16[5,4,2304]{2,1,0:T(4,128)(2,1)S(1)} %get-tuple-element.43), channel_id=1, source_target_pairs={{0,6},{2,0},{4,2},{6,4},{1,7},{3,1},{5,3},{7,5},{8,14},{10,8},{12,... | collective-permute-start | bytes 276488 | tf_op jit(solution)/shard_map/ppermute | solution.py:15
  62.2 4.8 %collective-permute-start.4 = (bf16[5,4,2304]{2,1,0:T(4,128)(2,1)S(1)}, bf16[5,4,2304]{2,1,0:T(4,128)(2,1)S(1)}, u32[]{:S(2)}, u32[]{:S(2)}) collective-permute-start(bf16[5,4,2304]{2,1,0:T(4,128)(2,1)S(1)} %get-tuple-element.44), channel_id=1, source_target_pairs={{0,2},{2,4},{4,6},{6,0},{1,3},{3,5},{5,7},{7,1},{8,10},{10,12},{12... | collective-permute-start | bytes 276488 | tf_op jit(solution)/shard_map/ppermute | solution.py:15
  79.6 5.6 %collective-permute-start.6 = (bf16[5,4,512]{2,1,0:T(4,128)(2,1)S(1)}, bf16[5,4,512]{2,1,0:T(4,128)(2,1)S(1)}, u32[]{:S(2)}, u32[]{:S(2)}) collective-permute-start(bf16[5,4,512]{2,1,0:T(4,128)(2,1)S(1)} %get-tuple-element.50), channel_id=1, source_target_pairs={{0,8},{8,16},{16,24},{24,0},{1,9},{9,17},{17,25},{25,1},{2,10},{10... | collective-permute-start | bytes 61448 | tf_op jit(solution)/shard_map/ppermute | solution.py:15
  80.6 6.5 %collective-permute-start.7 = (f32[5,4,512]{2,1,0:T(4,128)S(1)}, f32[5,4,512]{2,1,0:T(4,128)S(1)}, u32[]{:S(2)}, u32[]{:S(2)}) collective-permute-start(f32[5,4,512]{2,1,0:T(4,128)S(1)} %slice_bitcast_fusion.11), channel_id=1, source_target_pairs={{0,24},{8,0},{16,8},{24,16},{1,25},{9,1},{17,9},{25,17},{2,26},{10... | collective-permute-start | bytes 122888 | tf_op jit(solution)/shard_map/ppermute | solution.py:15
  83.6 1.7 collective-permute-start.9
  83.9 3.2 %collective-permute-start.8 = (bf16[5,4,512]{2,1,0:T(4,128)(2,1)S(1)}, bf16[5,4,512]{2,1,0:T(4,128)(2,1)S(1)}, u32[]{:S(2)}, u32[]{:S(2)}) collective-permute-start(bf16[5,4,512]{2,1,0:T(4,128)(2,1)S(1)} %get-tuple-element.52), channel_id=1, source_target_pairs={{0,2},{2,4},{4,6},{6,0},{1,3},{3,5},{5,7},{7,1},{8,10},{10,12},{12... | collective-permute-start | bytes 61448 | tf_op jit(solution)/shard_map/ppermute | solution.py:15
  137.1 18.0 %copy-start = (bf16[5,2304,512]{2,1,0:T(8,128)(2,1)S(1)}, bf16[5,2304,512]{2,1,0:T(8,128)(2,1)}, u32[]{:S(2)}) copy-start(bf16[5,2304,512]{2,1,0:T(8,128)(2,1)} %subtract_convert_fusion.1) | copy-start | bytes 35389444
  138.4 6.5 %collective-permute-start.10 = (bf16[5,4,2304]{2,1,0:T(4,128)(2,1)S(1)}, bf16[5,4,2304]{2,1,0:T(4,128)(2,1)S(1)}, u32[]{:S(2)}, u32[]{:S(2)}) collective-permute-start(bf16[5,4,2304]{2,1,0:T(4,128)(2,1)S(1)} %get-tuple-element.39), channel_id=1, source_target_pairs={{0,8},{8,16},{16,24},{24,0},{1,9},{9,17},{17,25},{25,1},{2,10},{10... | collective-permute-start | bytes 276488 | tf_op jit(solution)/shard_map/ppermute | solution.py:15
  141.6 7.1 %collective-permute-start.11 = (f32[5,4,2304]{2,1,0:T(4,128)S(1)}, f32[5,4,2304]{2,1,0:T(4,128)S(1)}, u32[]{:S(2)}, u32[]{:S(2)}) collective-permute-start(f32[5,4,2304]{2,1,0:T(4,128)S(1)} %slice_bitcast_fusion), channel_id=1, source_target_pairs={{0,24},{8,0},{16,8},{24,16},{1,25},{9,1},{17,9},{25,17},{2,26},{10... | collective-permute-start | bytes 552968 | tf_op jit(solution)/shard_map/ppermute | solution.py:15
  143.8 2.3 %collective-permute-start.13 = (bf16[5,4,2304]{2,1,0:T(4,128)(2,1)S(1)}, bf16[5,4,2304]{2,1,0:T(4,128)(2,1)S(1)}, u32[]{:S(2)}, u32[]{:S(2)}) collective-permute-start(bf16[5,4,2304]{2,1,0:T(4,128)(2,1)S(1)} %get-tuple-element.40), channel_id=1, source_target_pairs={{0,6},{2,0},{4,2},{6,4},{1,7},{3,1},{5,3},{7,5},{8,14},{10,8},{12,... | collective-permute-start | bytes 276488 | tf_op jit(solution)/shard_map/ppermute | solution.py:15
  143.8 4.9 %collective-permute-start.12 = (bf16[5,4,2304]{2,1,0:T(4,128)(2,1)S(1)}, bf16[5,4,2304]{2,1,0:T(4,128)(2,1)S(1)}, u32[]{:S(2)}, u32[]{:S(2)}) collective-permute-start(bf16[5,4,2304]{2,1,0:T(4,128)(2,1)S(1)} %get-tuple-element.41), channel_id=1, source_target_pairs={{0,2},{2,4},{4,6},{6,0},{1,3},{3,5},{5,7},{7,1},{8,10},{10,12},{12... | collective-permute-start | bytes 276488 | tf_op jit(solution)/shard_map/ppermute | solution.py:15
  156.9 5.7 %collective-permute-start.14 = (bf16[5,4,512]{2,1,0:T(4,128)(2,1)S(1)}, bf16[5,4,512]{2,1,0:T(4,128)(2,1)S(1)}, u32[]{:S(2)}, u32[]{:S(2)}) collective-permute-start(bf16[5,4,512]{2,1,0:T(4,128)(2,1)S(1)} %get-tuple-element.47), channel_id=1, source_target_pairs={{0,8},{8,16},{16,24},{24,0},{1,9},{9,17},{17,25},{25,1},{2,10},{10... | collective-permute-start | bytes 61448 | tf_op jit(solution)/shard_map/ppermute | solution.py:15
  157.6 6.6 %collective-permute-start.15 = (f32[5,4,512]{2,1,0:T(4,128)S(1)}, f32[5,4,512]{2,1,0:T(4,128)S(1)}, u32[]{:S(2)}, u32[]{:S(2)}) collective-permute-start(f32[5,4,512]{2,1,0:T(4,128)S(1)} %slice_bitcast_fusion.10), channel_id=1, source_target_pairs={{0,24},{8,0},{16,8},{24,16},{1,25},{9,1},{17,9},{25,17},{2,26},{10... | collective-permute-start | bytes 122888 | tf_op jit(solution)/shard_map/ppermute | solution.py:15
  160.9 1.7 collective-permute-start.17
  160.9 3.3 %collective-permute-start.16 = (bf16[5,4,512]{2,1,0:T(4,128)(2,1)S(1)}, bf16[5,4,512]{2,1,0:T(4,128)(2,1)S(1)}, u32[]{:S(2)}, u32[]{:S(2)}) collective-permute-start(bf16[5,4,512]{2,1,0:T(4,128)(2,1)S(1)} %get-tuple-element.49), channel_id=1, source_target_pairs={{0,2},{2,4},{4,6},{6,0},{1,3},{3,5},{5,7},{7,1},{8,10},{10,12},{12... | collective-permute-start | bytes 61448 | tf_op jit(solution)/shard_map/ppermute | solution.py:15
Sparse Core Ops, SparseCore 0:
  23.0 32.9 all-reduce.2
  104.8 32.2 all-reduce.4
where the time goes:
time: 181 us
  waiting for transfers between devices  84.3 us (47%)
  matrix products  42.7 us (24%)
  starting transfers between devices  20.7 us (11%)
  between operations  14.2 us (8%)
  other arithmetic  11.7 us (6%)
  local copies, waits for them, and re-layouts  7.13 us (4%)
    psum x2, waiting for transfers between devices, gossip_round(): totals = lax.psum(partial_rows, 'mp')  65.5 us
    ppermute x18, starting transfers between devices, passed_along(): lax.ppermute(value, axis, [(i, (i + by) % devices) for i in range(devices)])  20.6 us
    ppermute x18, waiting for transfers between devices, passed_along(): lax.ppermute(value, axis, [(i, (i + by) % devices) for i in range(devices)])  18.8 us
    dot_general x2, matrix products, gossip_round(): jnp.einsum('lsd,lsk->ldk', flat_basis, flat_factors, preferred_element_ty...  17.9 us
    dot_general x2, matrix products, gossip_round(): jnp.einsum('lerk,ldk->lerd', factors, layers, preferred_element_type=jnp....  16.9 us
    dot_general x2, matrix products, gossip_round(): jnp.einsum('lerd,ldk->lerk', basis, layers, preferred_element_type=jnp.fl...  7.88 us
  transfers between devices with their start and end apart: 20, of which 15 were waited for; matrix products, arithmetic and copies ran while one was open for 2% of the time, Pallas kernels for 0%

commit v1 on v0

v1 whole, which is shorter than its diff:
```python
import functools

import jax
import jax.numpy as jnp
from jax import lax
from jax.experimental import pallas as pl
from jax.experimental.pallas import tpu as pltpu
from jax.sharding import PartitionSpec as P

ROUNDS = 2
step_size = 0.2
epsilon = 1e-06

BF16 = jnp.bfloat16
F32 = jnp.float32
MIB = 1024 * 1024


def passed_along(value, axis, by):
    devices = lax.axis_size(axis)
    return lax.ppermute(value, axis, [(i, (i + by) % devices) for i in range(devices)])


def from_partners(value, axis):
    return [passed_along(value, axis, by) for by in range(1, lax.axis_size(axis))]


def rows_by_features(left, right):
    return lax.dot_general(left, right, (((1,), (1,)), ((), ())), preferred_element_type=F32)


def in_two_parts(value):
    high = value.astype(BF16)
    low = (value - high.astype(F32)).astype(BF16)
    return jnp.concatenate([high, low], axis=0)


def small_times(small, wide):
    rows = small.shape[0]
    both = jnp.dot(in_two_parts(small), wide, preferred_element_type=F32)
    return both[:rows] + both[rows:]


def call(kernel, outs, args, arg_spaces, scratch=(), limit=16, flops=1_000_000, name=None):
    return pl.pallas_call(
        kernel,
        out_shape=[jax.ShapeDtypeStruct(shape, dtype) for shape, dtype, _ in outs],
        in_specs=[pl.BlockSpec(memory_space=space) for space in arg_spaces],
        out_specs=[pl.BlockSpec(memory_space=space) for _, _, space in outs],
        scratch_shapes=list(scratch),
        compiler_params=pltpu.CompilerParams(vmem_limit_bytes=limit * MIB),
        cost_estimate=pl.CostEstimate(flops=flops, bytes_accessed=0, transcendentals=0),
        name=name,
    )(*args)


def load_kernel(w_hbm, down_ref, right_ref, w_ref, own_ref, sems):
    count = w_ref.shape[0]
    copies = [pltpu.make_async_copy(w_hbm.at[l], w_ref.at[l], sems.at[l]) for l in range(count)]
    for copy in copies:
        copy.start()
    for l in range(count):
        copies[l].wait()
        factors = jnp.concatenate([down_ref[l], right_ref[l]], axis=0)
        own_ref[l] = rows_by_features(factors, w_ref[l])


def store_products(l, row, col, row_keep, row_send, col_keep, left_send, right_send):
    row_keep[l] = row
    row_send[l] = row.astype(BF16)
    col_keep[l] = col
    left_send[l] = col[:4].astype(BF16)
    right_send[l] = col[4:].astype(BF16)


def first_products_kernel(w_ref, up_ref, left_ref, own_ref, *outs):
    for l in range(w_ref.shape[0]):
        factors = jnp.concatenate([up_ref[l], left_ref[l]], axis=0)
        theirs = rows_by_features(factors, w_ref[l])
        own = own_ref[l]
        row = jnp.concatenate([theirs[:4], own[:4]], axis=0)
        col = jnp.concatenate([theirs[4:], own[4:]], axis=0)
        store_products(l, row, col, *outs)


def middle_kernel(partners, row_keep, col_keep, from_left, from_right, *refs):
    received, (row_total, up_send, down_send, col_diff, col_send) = refs[:partners], refs[partners:]
    for l in range(row_keep.shape[0]):
        row = row_keep[l]
        for other in received:
            row = row + other[l].astype(F32)
        row_total[l] = row
        up_send[l] = row[:4].astype(BF16)
        down_send[l] = row[4:].astype(BF16)
        col = col_keep[l] - jnp.concatenate([from_left[l], from_right[l]], axis=0).astype(F32)
        col_diff[l] = col
        col_send[l] = col.astype(BF16)


def orthonormal(vectors):
    rank = vectors.shape[0] // 2
    row = lax.broadcasted_iota(jnp.int32, (vectors.shape[0], 1), 0)
    first = row < rank
    place = jnp.where(first, row, row - rank)
    rest, basis = vectors, None
    for k in range(rank):
        current = jnp.where(first, rest[k : k + 1], rest[rank + k : rank + k + 1])
        square = jnp.sum(current * current, axis=1, keepdims=True)
        unit = current * (1.0 / jnp.sqrt(square + epsilon))
        basis = unit if basis is None else jnp.where(place == k, unit, basis)
        if k + 1 < rank:
            along = jnp.sum(vectors * unit, axis=1, keepdims=True)
            rest = rest - along * unit
    return basis


def back_kernel(partners, earlier, w_ref, row_total, from_above, from_below, col_diff, *refs):
    received, refs = refs[:partners], refs[partners:]
    pairs, refs = refs[: 2 * earlier], refs[2 * earlier :]
    basis_ref, back_ref, up_send, down_send, left_send, right_send = refs
    for l in range(w_ref.shape[0]):
        row = row_total[l] - jnp.concatenate([from_above[l], from_below[l]], axis=0).astype(F32)
        col = col_diff[l]
        for other in received:
            col = col + other[l].astype(F32)
        basis = jnp.concatenate([orthonormal(row), orthonormal(col)], axis=0).astype(BF16)
        basis_ref[l] = basis
        back = jnp.dot(basis, w_ref[l], preferred_element_type=F32)
        for e in range(earlier):
            mixing = rows_by_features(basis, pairs[2 * e][l])
            back = back + small_times(-step_size * mixing, pairs[2 * e + 1][l])
        back_ref[l] = back
        for i, send in enumerate((up_send, down_send, left_send, right_send)):
            send[l] = back[4 * i : 4 * i + 4].astype(BF16)


def combined_of(l, back_ref, above, below, left, right):
    theirs = jnp.concatenate([above[l], below[l], left[l], right[l]], axis=0)
    return back_ref[l] + theirs.astype(F32)


def next_products_kernel(earlier, w_ref, back_ref, above, below, left, right, *refs):
    bases, refs = refs[: earlier + 1], refs[earlier + 1 :]
    old_factors, refs = refs[:earlier], refs[earlier:]
    factors_ref, outs = refs[0], refs[1:]
    for l in range(w_ref.shape[0]):
        factors = combined_of(l, back_ref, above, below, left, right).astype(BF16)
        factors_ref[l] = factors
        products = rows_by_features(factors, w_ref[l])
        for e in range(earlier + 1):
            base_factors = old_factors[e][l] if e < earlier else factors
            mixing = rows_by_features(factors, base_factors)
            products = products + small_times(-step_size * mixing, bases[e][l])
        store_products(l, products[:8], products[8:], *outs)


def finish_kernel(earlier, chunk, w_ref, back_ref, above, below, left, right, *refs):
    bases, refs = refs[: earlier + 1], refs[earlier + 1 :]
    old_factors, refs = refs[:earlier], refs[earlier:]
    w_out, down_out, right_out, staged, sems = refs
    count, depth, _ = w_ref.shape
    copies = []
    for l in range(count):
        combined = combined_of(l, back_ref, above, below, left, right)
        down_out[l] = combined[4:8]
        right_out[l] = combined[12:]
        factors = jnp.concatenate([f[l] for f in old_factors] + [combined.astype(BF16)], axis=0)
        for c in range(depth // chunk):
            part = pl.ds(c * chunk, chunk)
            basis = jnp.concatenate([b[l, :, part] for b in bases], axis=0)
            correction = lax.dot_general(
                basis, factors, (((0,), (0,)), ((), ())), preferred_element_type=F32
            )
            staged[l, part] = (w_ref[l, part].astype(F32) - step_size * correction).astype(BF16)
            copy = pltpu.make_async_copy(
                staged.at[l, part], w_out.at[l, part], sems.at[l, c]
            )
            copy.start()
            copies.append(copy)
    for copy in copies:
        copy.wait()


def body(weights, warm_down, warm_right):
    vmem, hbm = pltpu.VMEM, pltpu.HBM
    w_hbm, down, right = weights[0, 0], warm_down[0, 0], warm_right[0, 0]
    w_hbm = pltpu.with_memory_space_constraint(w_hbm, pltpu.HBM)
    count, depth, width = w_hbm.shape
    rank = down.shape[1]
    partners = lax.axis_size("mp") - 1
    pair, every = 2 * rank, 4 * rank
    work = 2 * count * depth * width * every

    above = passed_along(down, "row", 1)
    beside = passed_along(right, "col", 1)
    w, own = call(
        load_kernel,
        [((count, depth, width), BF16, vmem), ((count, pair, depth), F32, vmem)],
        (w_hbm, down, right),
        (hbm, vmem, vmem),
        [pltpu.SemaphoreType.DMA((count,))],
        flops=10 * work,
        name="load",
    )
    product_outs = [
        ((count, pair, depth), F32, vmem),
        ((count, pair, depth), BF16, vmem),
        ((count, pair, depth), F32, vmem),
        ((count, rank, depth), BF16, vmem),
        ((count, rank, depth), BF16, vmem),
    ]
    products = call(
        first_products_kernel, product_outs, (w, above, beside, own), [vmem] * 4, name="first"
    )
    bases, factors = [], []
    for repeat in range(ROUNDS):
        row_keep, row_send, col_keep, left_send, right_send = products
        received = from_partners(row_send, "mp")
        from_left = passed_along(right_send, "col", 1)
        from_right = passed_along(left_send, "col", -1)
        args = (row_keep, col_keep, from_left, from_right, *received)
        row_total, up_send, down_send, col_diff, col_send = call(
            functools.partial(middle_kernel, partners),
            [
                ((count, pair, depth), F32, vmem),
                ((count, rank, depth), BF16, vmem),
                ((count, rank, depth), BF16, vmem),
                ((count, pair, depth), F32, vmem),
                ((count, pair, depth), BF16, vmem),
            ],
            args,
            [vmem] * len(args),
            name=f"middle_{repeat}",
        )
        from_above = passed_along(down_send, "row", 1)
        from_below = passed_along(up_send, "row", -1)
        received = from_partners(col_send, "mp")
        pairs = [x for both in zip(bases, factors) for x in both]
        args = (w, row_total, from_above, from_below, col_diff, *received, *pairs)
        basis, back, up_send, down_send, left_send, right_send = call(
            functools.partial(back_kernel, partners, repeat),
            [((count, every, depth), BF16, vmem), ((count, every, width), F32, vmem)]
            + [((count, rank, width), BF16, vmem)] * 4,
            args,
            [vmem] * len(args),
            name=f"back_{repeat}",
        )
        bases = bases + [basis]
        from_above = passed_along(down_send, "row", 1)
        from_below = passed_along(up_send, "row", -1)
        from_left = passed_along(right_send, "col", 1)
        from_right = passed_along(left_send, "col", -1)
        args = (w, back, from_above, from_below, from_left, from_right, *bases, *factors)
        if repeat + 1 < ROUNDS:
            out = call(
                functools.partial(next_products_kernel, repeat),
                [((count, every, width), BF16, vmem)] + product_outs,
                args,
                [vmem] * len(args),
                name=f"next_{repeat}",
            )
            factors, products = factors + [out[0]], out[1:]
    chunk = depth // 3 if depth % 384 == 0 else depth
    new_w, next_down, next_right = call(
        functools.partial(finish_kernel, ROUNDS - 1, chunk),
        [
            ((count, depth, width), BF16, hbm),
            ((count, rank, width), F32, vmem),
            ((count, rank, width), F32, vmem),
        ],
        args,
        [vmem] * len(args),
        [
            pltpu.VMEM((count, depth, width), BF16),
            pltpu.SemaphoreType.DMA((count, depth // chunk)),
        ],
        limit=28,
        name="finish",
    )
    return new_w[None, None], next_down[None, None], next_right[None, None]


def solution(mesh):
    placed = (P("row", "col", None, None, "mp"),) * 3
    return jax.shard_map(
        body, mesh=mesh, in_specs=placed, out_specs=placed, check_vma=False
    )
```

time: 181 us -> 77.6 us (0.43)
  waiting for transfers between devices: 84.3 us -> 19.2 us
  matrix products: 42.7 us -> 0 us
  Pallas kernels: 0 us -> 25.4 us
  between operations: 14.2 us -> 0.85 us
  other arithmetic: 11.7 us -> 0 us
  starting transfers between devices: 20.7 us -> 29.6 us
  local copies, waits for them, and re-layouts: 7.13 us -> 1.48 us
    psum x2 -> x0, waiting for transfers between devices: 65.5 us -> none  [gossip_round(): totals = lax.psum(partial_rows, 'mp')]
    dot_general x6 -> x0, matrix products: 42.7 us -> none  [the longest x2 17.9 us: gossip_round(): jnp.einsum('lsd,lsk->ldk', flat_basis, flat_factors, preferred_element_ty...]
    pallas_call x0 -> x8, Pallas kernels: none -> 25.4 us  [call(): pl.pallas_call(kernel, out_shape=[jax.ShapeDtypeStruct(shape, dtype) for...]
    ppermute x18 -> x22, starting transfers between devices: 20.6 us -> 29.6 us  [passed_along(): lax.ppermute(value, axis, [(i, (i + by) % devices) for i in range(devices)])]
    reduce_sum x14 -> x0, other arithmetic: 3.45 us -> none  [the longest x8 2.08 us: orthonormal(): jnp.sum(source * earlier, axis=-1, keepdims=True) * earlier]
    div x2 -> x0, other arithmetic: 3.42 us -> none  [orthonormal(): update / jnp.sqrt(jnp.sum(update * update, axis=-1, keepdims=True) + epsi...]
    convert_element_type x6 -> x0, local copies, waits for them, and re-layouts: 2.76 us -> none  [the longest x4 2.59 us: neighbours(): payload[:, 1].astype(jnp.bfloat16)]
    sub x2 -> x0, other arithmetic: 2.75 us -> none  [gossip_round(): difference = totals - neighbours(totals)]
  transfers between devices with their start and end apart: 20 -> 22, of which waited for: 15 -> 9; matrix products, arithmetic and copies ran while one was open for 2% -> 0% of each run, Pallas kernels for 0% -> 7%
where the time goes in v1:
time: 77.6 us; the launch traced here: 76.6 us
  starting transfers between devices  29.6 us (38%)
  Pallas kernels  25.4 us (33%)
  waiting for transfers between devices  19.2 us (25%)
  local copies, waits for them, and re-layouts  1.48 us (2%)
  between operations  0.85 us (1%)
    ppermute x22, starting transfers between devices, passed_along(): lax.ppermute(value, axis, [(i, (i + by) % devices) for i in range(devices)])  29.6 us
    pallas_call x8, Pallas kernels, call(): pl.pallas_call(kernel, out_shape=[jax.ShapeDtypeStruct(shape, dtype) for...  25.4 us
    ppermute x22, waiting for transfers between devices, passed_along(): lax.ppermute(value, axis, [(i, (i + by) % devices) for i in range(devices)])  19.2 us
  transfers between devices with their start and end apart: 22, of which 9 were waited for; matrix products, arithmetic and copies ran while one was open for 0% of the time, Pallas kernels for 7%

profile of v1, /device:TPU:0, one launch (start us, length us, event | category | flops | bytes accessed | tf_op | source)
XLA Modules:
  0.0 76.6 jit_solution(11097621897899173552)
XLA Ops:
  0.6 3.1 %collective-permute-start = (bf16[5,4,512]{2,1,0:T(4,128)(2,1)}, bf16[5,4,512]{2,1,0:T(4,128)(2,1)S(1)}, u32[]{:S(2)}, u32[]{:S(2)}) collective-permute-start(bf16[5,4,512]{2,1,0:T(4,128)(2,1)} %bitcast.6), channel_id=1, source_target_pairs={{0,8},{8,16},{16,24},{24,0},{1,9},{9,17},{17,25},{25,1},{2,10},{10... | collective-permute-start | bytes 61448 | tf_op jit(solution)/shard_map/ppermute | solution.py:21
  3.7 0.0 collective-permute-start.1
  3.7 0.8 copy-done
  4.5 0.7 copy-done.1
  5.2 5.6 %load.1 = (bf16[5,2304,512]{2,1,0:T(8,128)(2,1)S(1)}, f32[5,8,2304]{2,1,0:T(8,128)S(1)}) custom-call(bf16[5,2304,512]{2,1,0:T(8,128)(2,1)} %bitcast.10, bf16[5,4,512]{2,1,0:T(4,128)(2,1)S(1)} %bitcast.7, bf16[5,4,512]{2,1,0:T(4,128)(2,1)S(1)} %bitcast.9), custom_call_target="tpu_custom_call" | custom-call | flops 1887436800 | tf_op jit(solution)/shard_map/load/pallas_call | solution.py:45
  10.9 0.0 collective-permute-done.up_ref
  10.9 0.0 collective-permute-done.1.left_ref
  10.9 3.2 %first.1 = (f32[5,8,2304]{2,1,0:T(8,128)S(1)}, bf16[5,8,2304]{2,1,0:T(8,128)(2,1)S(1)}, f32[5,8,2304]{2,1,0:T(8,128)S(1)}, bf16[5,4,2304]{2,1,0:T(4,128)(2,1)S(1)}, bf16[5,4,2304]{2,1,0:T(4,128)(2,1)S(1)}) custom-call(bf16[5,2304,512]{2,1,0:T(8,128)(2,1)S(1)} %get-tuple-element.41.w_ref, bf16[5,4,512]{2,1,0:T(4,128)(2,1)S(1)} %collective-permute-done.up_ref, ...), custom_call_target="tpu_custom_call" | custom-call | flops 1000000 | tf_op jit(solution)/shard_map/first/pallas_call | solution.py:45
  14.0 1.5 %collective-permute-start.4 = (bf16[5,8,2304]{2,1,0:T(8,128)(2,1)S(1)}, bf16[5,8,2304]{2,1,0:T(8,128)(2,1)S(1)}, u32[]{:S(2)}, u32[]{:S(2)}) collective-permute-start(bf16[5,8,2304]{2,1,0:T(8,128)(2,1)S(1)} %get-tuple-element.47), channel_id=1, source_target_pairs={{0,1},{1,0},{2,3},{3,2},{4,5},{5,4},{6,7},{7,6},{8,9},{9,8},{10,11... | collective-permute-start | bytes 552968 | tf_op jit(solution)/shard_map/ppermute | solution.py:21
  15.6 1.3 %collective-permute-start.2 = (bf16[5,4,2304]{2,1,0:T(4,128)(2,1)S(1)}, bf16[5,4,2304]{2,1,0:T(4,128)(2,1)S(1)}, u32[]{:S(2)}, u32[]{:S(2)}) collective-permute-start(bf16[5,4,2304]{2,1,0:T(4,128)(2,1)S(1)} %get-tuple-element.45), channel_id=1, source_target_pairs={{0,2},{2,4},{4,6},{6,0},{1,3},{3,5},{5,7},{7,1},{8,10},{10,12},{12... | collective-permute-start | bytes 276488 | tf_op jit(solution)/shard_map/ppermute | solution.py:21
  16.9 0.5 collective-permute-start.3
  17.3 2.2 %collective-permute-done.2.from_left = bf16[5,4,2304]{2,1,0:T(4,128)(2,1)S(1)} collective-permute-done((bf16[5,4,2304]{2,1,0:T(4,128)(2,1)S(1)}, bf16[5,4,2304]{2,1,0:T(4,128)(2,1)S(1)}, u32[]{:S(2)}, u32[]{:S(2)}) %collective-permute-start.2) | collective-permute-done | bytes 92192 | tf_op jit(solution)/shard_map/ppermute | solution.py:21
  19.6 0.0 collective-permute-done.3.from_right
  19.6 1.4 %collective-permute-done.4.refs_0_ = bf16[5,8,2304]{2,1,0:T(8,128)(2,1)S(1)} collective-permute-done((bf16[5,8,2304]{2,1,0:T(8,128)(2,1)S(1)}, bf16[5,8,2304]{2,1,0:T(8,128)(2,1)S(1)}, u32[]{:S(2)}, u32[]{:S(2)}) %collective-permute-start.4) | collective-permute-done | bytes 184352 | tf_op jit(solution)/shard_map/ppermute | solution.py:21
  21.0 0.1 middle_0.1
  21.1 1.6 %collective-permute-start.7 = (bf16[5,8,2304]{2,1,0:T(8,128)(2,1)S(1)}, bf16[5,8,2304]{2,1,0:T(8,128)(2,1)S(1)}, u32[]{:S(2)}, u32[]{:S(2)}) collective-permute-start(bf16[5,8,2304]{2,1,0:T(8,128)(2,1)S(1)} %get-tuple-element.52), channel_id=1, source_target_pairs={{0,1},{1,0},{2,3},{3,2},{4,5},{5,4},{6,7},{7,6},{8,9},{9,8},{10,11... | collective-permute-start | bytes 552968 | tf_op jit(solution)/shard_map/ppermute | solution.py:21
  22.7 1.6 %collective-permute-start.5 = (bf16[5,4,2304]{2,1,0:T(4,128)(2,1)S(1)}, bf16[5,4,2304]{2,1,0:T(4,128)(2,1)S(1)}, u32[]{:S(2)}, u32[]{:S(2)}) collective-permute-start(bf16[5,4,2304]{2,1,0:T(4,128)(2,1)S(1)} %get-tuple-element.49), channel_id=1, source_target_pairs={{0,8},{8,16},{16,24},{24,0},{1,9},{9,17},{17,25},{25,1},{2,10},{10... | collective-permute-start | bytes 276488 | tf_op jit(solution)/shard_map/ppermute | solution.py:21
  24.3 2.2 %collective-permute-start.6 = (bf16[5,4,2304]{2,1,0:T(4,128)(2,1)S(1)}, bf16[5,4,2304]{2,1,0:T(4,128)(2,1)S(1)}, u32[]{:S(2)}, u32[]{:S(2)}) collective-permute-start(bf16[5,4,2304]{2,1,0:T(4,128)(2,1)S(1)} %get-tuple-element.50), channel_id=1, source_target_pairs={{0,24},{8,0},{16,8},{24,16},{1,25},{9,1},{17,9},{25,17},{2,26},{10... | collective-permute-start | bytes 276488 | tf_op jit(solution)/shard_map/ppermute | solution.py:21
  26.5 3.5 %collective-permute-done.5.from_above = bf16[5,4,2304]{2,1,0:T(4,128)(2,1)S(1)} collective-permute-done((bf16[5,4,2304]{2,1,0:T(4,128)(2,1)S(1)}, bf16[5,4,2304]{2,1,0:T(4,128)(2,1)S(1)}, u32[]{:S(2)}, u32[]{:S(2)}) %collective-permute-start.5) | collective-permute-done | bytes 92192 | tf_op jit(solution)/shard_map/ppermute | solution.py:21
  30.0 0.6 collective-permute-done.6.from_below
  30.7 3.1 %back_0.1 = (bf16[5,16,2304]{2,1,0:T(8,128)(2,1)S(1)}, f32[5,16,512]{2,1,0:T(8,128)S(1)}, bf16[5,4,512]{2,1,0:T(4,128)(2,1)S(1)}, bf16[5,4,512]{2,1,0:T(4,128)(2...) custom-call(bf16[5,2304,512]{2,1,0:T(8,128)(2,1)S(1)} %get-tuple-element.41.w_ref, ...), custom_call_target="tpu_custom_call" | custom-call | flops 1000000 | tf_op jit(solution)/shard_map/back_0/pallas_call | solution.py:45
  33.8 1.1 %collective-permute-start.8 = (bf16[5,4,512]{2,1,0:T(4,128)(2,1)S(1)}, bf16[5,4,512]{2,1,0:T(4,128)(2,1)S(1)}, u32[]{:S(2)}, u32[]{:S(2)}) collective-permute-start(bf16[5,4,512]{2,1,0:T(4,128)(2,1)S(1)} %get-tuple-element.54), channel_id=1, source_target_pairs={{0,8},{8,16},{16,24},{24,0},{1,9},{9,17},{17,25},{25,1},{2,10},{10... | collective-permute-start | bytes 61448 | tf_op jit(solution)/shard_map/ppermute | solution.py:21
  34.8 2.8 %collective-permute-start.9 = (bf16[5,4,512]{2,1,0:T(4,128)(2,1)S(1)}, bf16[5,4,512]{2,1,0:T(4,128)(2,1)S(1)}, u32[]{:S(2)}, u32[]{:S(2)}) collective-permute-start(bf16[5,4,512]{2,1,0:T(4,128)(2,1)S(1)} %get-tuple-element.55), channel_id=1, source_target_pairs={{0,24},{8,0},{16,8},{24,16},{1,25},{9,1},{17,9},{25,17},{2,26},{10... | collective-permute-start | bytes 61448 | tf_op jit(solution)/shard_map/ppermute | solution.py:21
  37.6 1.7 %collective-permute-start.11 = (bf16[5,4,512]{2,1,0:T(4,128)(2,1)S(1)}, bf16[5,4,512]{2,1,0:T(4,128)(2,1)S(1)}, u32[]{:S(2)}, u32[]{:S(2)}) collective-permute-start(bf16[5,4,512]{2,1,0:T(4,128)(2,1)S(1)} %get-tuple-element.57), channel_id=1, source_target_pairs={{0,6},{2,0},{4,2},{6,4},{1,7},{3,1},{5,3},{7,5},{8,14},{10,8},{12,... | collective-permute-start | bytes 61448 | tf_op jit(solution)/shard_map/ppermute | solution.py:21
  39.3 0.0 collective-permute-done.8.above
  39.4 0.0 collective-permute-done.9.below
  39.4 1.4 %collective-permute-done.10.left = bf16[5,4,512]{2,1,0:T(4,128)(2,1)S(1)} collective-permute-done((bf16[5,4,512]{2,1,0:T(4,128)(2,1)S(1)}, bf16[5,4,512]{2,1,0:T(4,128)(2,1)S(1)}, u32[]{:S(2)}, u32[]{:S(2)}) %collective-permute-start.10) | collective-permute-done | bytes 20512 | tf_op jit(solution)/shard_map/ppermute | solution.py:21
  40.8 0.0 collective-permute-done.11.right
  40.8 3.8 %next_0.1 = (bf16[5,16,512]{2,1,0:T(8,128)(2,1)S(1)}, f32[5,8,2304]{2,1,0:T(8,128)S(1)}, bf16[5,8,2304]{2,1,0:T(8,128)(2,1)S(1)}, f32[5,8,2304]{2,1,0:T(8,128)S(...) custom-call(bf16[5,2304,512]{2,1,0:T(8,128)(2,1)S(1)} %get-tuple-element.41.w_ref, ...), custom_call_target="tpu_custom_call" | custom-call | flops 1000000 | tf_op jit(solution)/shard_map/next_0/pallas_call | solution.py:45
  44.6 0.5 collective-permute-start.14
  45.1 0.9 %collective-permute-start.12 = (bf16[5,4,2304]{2,1,0:T(4,128)(2,1)S(1)}, bf16[5,4,2304]{2,1,0:T(4,128)(2,1)S(1)}, u32[]{:S(2)}, u32[]{:S(2)}) collective-permute-start(bf16[5,4,2304]{2,1,0:T(4,128)(2,1)S(1)} %get-tuple-element.61), channel_id=1, source_target_pairs={{0,2},{2,4},{4,6},{6,0},{1,3},{3,5},{5,7},{7,1},{8,10},{10,12},{12... | collective-permute-start | bytes 276488 | tf_op jit(solution)/shard_map/ppermute | solution.py:21
  46.0 0.9 %collective-permute-start.13 = (bf16[5,4,2304]{2,1,0:T(4,128)(2,1)S(1)}, bf16[5,4,2304]{2,1,0:T(4,128)(2,1)S(1)}, u32[]{:S(2)}, u32[]{:S(2)}) collective-permute-start(bf16[5,4,2304]{2,1,0:T(4,128)(2,1)S(1)} %get-tuple-element.62), channel_id=1, source_target_pairs={{0,6},{2,0},{4,2},{6,4},{1,7},{3,1},{5,3},{7,5},{8,14},{10,8},{12,... | collective-permute-start | bytes 276488 | tf_op jit(solution)/shard_map/ppermute | solution.py:21
  46.9 2.2 %collective-permute-done.12.from_left = bf16[5,4,2304]{2,1,0:T(4,128)(2,1)S(1)} collective-permute-done((bf16[5,4,2304]{2,1,0:T(4,128)(2,1)S(1)}, bf16[5,4,2304]{2,1,0:T(4,128)(2,1)S(1)}, u32[]{:S(2)}, u32[]{:S(2)}) %collective-permute-start.12) | collective-permute-done | bytes 92192 | tf_op jit(solution)/shard_map/ppermute | solution.py:21
  49.1 2.8 %collective-permute-done.14.refs_0_ = bf16[5,8,2304]{2,1,0:T(8,128)(2,1)S(1)} collective-permute-done((bf16[5,8,2304]{2,1,0:T(8,128)(2,1)S(1)}, bf16[5,8,2304]{2,1,0:T(8,128)(2,1)S(1)}, u32[]{:S(2)}, u32[]{:S(2)}) %collective-permute-start.14) | collective-permute-done | bytes 184352 | tf_op jit(solution)/shard_map/ppermute | solution.py:21
  51.9 0.1 middle_1.1
  52.1 0.6 collective-permute-start.17
  52.6 3.8 %collective-permute-start.16 = (bf16[5,4,2304]{2,1,0:T(4,128)(2,1)S(1)}, bf16[5,4,2304]{2,1,0:T(4,128)(2,1)S(1)}, u32[]{:S(2)}, u32[]{:S(2)}) collective-permute-start(bf16[5,4,2304]{2,1,0:T(4,128)(2,1)S(1)} %get-tuple-element.66), channel_id=1, source_target_pairs={{0,24},{8,0},{16,8},{24,16},{1,25},{9,1},{17,9},{25,17},{2,26},{10... | collective-permute-start | bytes 276488 | tf_op jit(solution)/shard_map/ppermute | solution.py:21
  56.5 3.4 %collective-permute-done.15.from_above = bf16[5,4,2304]{2,1,0:T(4,128)(2,1)S(1)} collective-permute-done((bf16[5,4,2304]{2,1,0:T(4,128)(2,1)S(1)}, bf16[5,4,2304]{2,1,0:T(4,128)(2,1)S(1)}, u32[]{:S(2)}, u32[]{:S(2)}) %collective-permute-start.15) | collective-permute-done | bytes 92192 | tf_op jit(solution)/shard_map/ppermute | solution.py:21
  59.9 0.0 collective-permute-done.16.from_below
  59.9 0.0 collective-permute-done.17.refs_0_
  59.9 4.0 %back_1.1 = (bf16[5,16,2304]{2,1,0:T(8,128)(2,1)S(1)}, f32[5,16,512]{2,1,0:T(8,128)S(1)}, bf16[5,4,512]{2,1,0:T(4,128)(2,1)S(1)}, bf16[5,4,512]{2,1,0:T(4,128)(2...) custom-call(bf16[5,2304,512]{2,1,0:T(8,128)(2,1)S(1)} %get-tuple-element.41.w_ref, ...), custom_call_target="tpu_custom_call" | custom-call | flops 1000000 | tf_op jit(solution)/shard_map/back_1/pallas_call | solution.py:45
  63.9 3.8 %collective-permute-start.19 = (bf16[5,4,512]{2,1,0:T(4,128)(2,1)S(1)}, bf16[5,4,512]{2,1,0:T(4,128)(2,1)S(1)}, u32[]{:S(2)}, u32[]{:S(2)}) collective-permute-start(bf16[5,4,512]{2,1,0:T(4,128)(2,1)S(1)} %get-tuple-element.72), channel_id=1, source_target_pairs={{0,24},{8,0},{16,8},{24,16},{1,25},{9,1},{17,9},{25,17},{2,26},{10... | collective-permute-start | bytes 61448 | tf_op jit(solution)/shard_map/ppermute | solution.py:21
  67.7 1.7 %collective-permute-start.21 = (bf16[5,4,512]{2,1,0:T(4,128)(2,1)S(1)}, bf16[5,4,512]{2,1,0:T(4,128)(2,1)S(1)}, u32[]{:S(2)}, u32[]{:S(2)}) collective-permute-start(bf16[5,4,512]{2,1,0:T(4,128)(2,1)S(1)} %get-tuple-element.74), channel_id=1, source_target_pairs={{0,6},{2,0},{4,2},{6,4},{1,7},{3,1},{5,3},{7,5},{8,14},{10,8},{12,... | collective-permute-start | bytes 61448 | tf_op jit(solution)/shard_map/ppermute | solution.py:21
  69.5 0.0 collective-permute-done.18.above
  69.5 0.0 collective-permute-done.19.below
  69.5 1.4 %collective-permute-done.20.left = bf16[5,4,512]{2,1,0:T(4,128)(2,1)S(1)} collective-permute-done((bf16[5,4,512]{2,1,0:T(4,128)(2,1)S(1)}, bf16[5,4,512]{2,1,0:T(4,128)(2,1)S(1)}, u32[]{:S(2)}, u32[]{:S(2)}) %collective-permute-start.20) | collective-permute-done | bytes 20512 | tf_op jit(solution)/shard_map/ppermute | solution.py:21
  70.9 0.0 collective-permute-done.21.right
  70.9 5.5 %finish.1 = (bf16[5,2304,512]{2,1,0:T(8,128)(2,1)}, f32[5,4,512]{2,1,0:T(4,128)}, f32[5,4,512]{2,1,0:T(4,128)}) custom-call(bf16[5,2304,512]{2,1,0:T(8,128)(2,1)S(1)} %get-tuple-element.41.w_ref, f32[5,16,512]{2,1,0:T(8,128)S(1)} %get-tuple-element.70.back_ref, bf16[5,4,512]{2,1,0:T(4,128)(2,1)S(1)} %collective-permute-done.18.above, ...), custom_call_target="tpu_custom_call" | custom-call | flops 1000000 | tf_op jit(solution)/shard_map/finish/pallas_call | solution.py:45
  (8 shorter events, 0.0 us)
Async XLA Ops:
  0.6 10.2 %collective-permute-start = (bf16[5,4,512]{2,1,0:T(4,128)(2,1)}, bf16[5,4,512]{2,1,0:T(4,128)(2,1)S(1)}, u32[]{:S(2)}, u32[]{:S(2)}) collective-permute-start(bf16[5,4,512]{2,1,0:T(4,128)(2,1)} %bitcast.6), channel_id=1, source_target_pairs={{0,8},{8,16},{16,24},{24,0},{1,9},{9,17},{17,25},{25,1},{2,10},{10... | collective-permute-start | bytes 61448 | tf_op jit(solution)/shard_map/ppermute | solution.py:21
  3.7 7.1 %collective-permute-start.1 = (bf16[5,4,512]{2,1,0:T(4,128)(2,1)}, bf16[5,4,512]{2,1,0:T(4,128)(2,1)S(1)}, u32[]{:S(2)}, u32[]{:S(2)}) collective-permute-start(bf16[5,4,512]{2,1,0:T(4,128)(2,1)} %bitcast.8), channel_id=1, source_target_pairs={{0,2},{2,4},{4,6},{6,0},{1,3},{3,5},{5,7},{7,1},{8,10},{10,12},{12... | collective-permute-start | bytes 61448 | tf_op jit(solution)/shard_map/ppermute | solution.py:21
  3.7 0.8 copy-start
  4.5 0.7 copy-start.1
  14.0 6.9 %collective-permute-start.4 = (bf16[5,8,2304]{2,1,0:T(8,128)(2,1)S(1)}, bf16[5,8,2304]{2,1,0:T(8,128)(2,1)S(1)}, u32[]{:S(2)}, u32[]{:S(2)}) collective-permute-start(bf16[5,8,2304]{2,1,0:T(8,128)(2,1)S(1)} %get-tuple-element.47), channel_id=1, source_target_pairs={{0,1},{1,0},{2,3},{3,2},{4,5},{5,4},{6,7},{7,6},{8,9},{9,8},{10,11... | collective-permute-start | bytes 552968 | tf_op jit(solution)/shard_map/ppermute | solution.py:21
  15.6 4.0 %collective-permute-start.2 = (bf16[5,4,2304]{2,1,0:T(4,128)(2,1)S(1)}, bf16[5,4,2304]{2,1,0:T(4,128)(2,1)S(1)}, u32[]{:S(2)}, u32[]{:S(2)}) collective-permute-start(bf16[5,4,2304]{2,1,0:T(4,128)(2,1)S(1)} %get-tuple-element.45), channel_id=1, source_target_pairs={{0,2},{2,4},{4,6},{6,0},{1,3},{3,5},{5,7},{7,1},{8,10},{10,12},{12... | collective-permute-start | bytes 276488 | tf_op jit(solution)/shard_map/ppermute | solution.py:21
  16.9 2.7 %collective-permute-start.3 = (bf16[5,4,2304]{2,1,0:T(4,128)(2,1)S(1)}, bf16[5,4,2304]{2,1,0:T(4,128)(2,1)S(1)}, u32[]{:S(2)}, u32[]{:S(2)}) collective-permute-start(bf16[5,4,2304]{2,1,0:T(4,128)(2,1)S(1)} %get-tuple-element.46), channel_id=1, source_target_pairs={{0,6},{2,0},{4,2},{6,4},{1,7},{3,1},{5,3},{7,5},{8,14},{10,8},{12,... | collective-permute-start | bytes 276488 | tf_op jit(solution)/shard_map/ppermute | solution.py:21
  21.1 9.6 %collective-permute-start.7 = (bf16[5,8,2304]{2,1,0:T(8,128)(2,1)S(1)}, bf16[5,8,2304]{2,1,0:T(8,128)(2,1)S(1)}, u32[]{:S(2)}, u32[]{:S(2)}) collective-permute-start(bf16[5,8,2304]{2,1,0:T(8,128)(2,1)S(1)} %get-tuple-element.52), channel_id=1, source_target_pairs={{0,1},{1,0},{2,3},{3,2},{4,5},{5,4},{6,7},{7,6},{8,9},{9,8},{10,11... | collective-permute-start | bytes 552968 | tf_op jit(solution)/shard_map/ppermute | solution.py:21
  22.7 7.3 %collective-permute-start.5 = (bf16[5,4,2304]{2,1,0:T(4,128)(2,1)S(1)}, bf16[5,4,2304]{2,1,0:T(4,128)(2,1)S(1)}, u32[]{:S(2)}, u32[]{:S(2)}) collective-permute-start(bf16[5,4,2304]{2,1,0:T(4,128)(2,1)S(1)} %get-tuple-element.49), channel_id=1, source_target_pairs={{0,8},{8,16},{16,24},{24,0},{1,9},{9,17},{17,25},{25,1},{2,10},{10... | collective-permute-start | bytes 276488 | tf_op jit(solution)/shard_map/ppermute | solution.py:21
  24.3 6.4 %collective-permute-start.6 = (bf16[5,4,2304]{2,1,0:T(4,128)(2,1)S(1)}, bf16[5,4,2304]{2,1,0:T(4,128)(2,1)S(1)}, u32[]{:S(2)}, u32[]{:S(2)}) collective-permute-start(bf16[5,4,2304]{2,1,0:T(4,128)(2,1)S(1)} %get-tuple-element.50), channel_id=1, source_target_pairs={{0,24},{8,0},{16,8},{24,16},{1,25},{9,1},{17,9},{25,17},{2,26},{10... | collective-permute-start | bytes 276488 | tf_op jit(solution)/shard_map/ppermute | solution.py:21
  33.8 5.6 %collective-permute-start.8 = (bf16[5,4,512]{2,1,0:T(4,128)(2,1)S(1)}, bf16[5,4,512]{2,1,0:T(4,128)(2,1)S(1)}, u32[]{:S(2)}, u32[]{:S(2)}) collective-permute-start(bf16[5,4,512]{2,1,0:T(4,128)(2,1)S(1)} %get-tuple-element.54), channel_id=1, source_target_pairs={{0,8},{8,16},{16,24},{24,0},{1,9},{9,17},{17,25},{25,1},{2,10},{10... | collective-permute-start | bytes 61448 | tf_op jit(solution)/shard_map/ppermute | solution.py:21
  34.8 4.5 %collective-permute-start.9 = (bf16[5,4,512]{2,1,0:T(4,128)(2,1)S(1)}, bf16[5,4,512]{2,1,0:T(4,128)(2,1)S(1)}, u32[]{:S(2)}, u32[]{:S(2)}) collective-permute-start(bf16[5,4,512]{2,1,0:T(4,128)(2,1)S(1)} %get-tuple-element.55), channel_id=1, source_target_pairs={{0,24},{8,0},{16,8},{24,16},{1,25},{9,1},{17,9},{25,17},{2,26},{10... | collective-permute-start | bytes 61448 | tf_op jit(solution)/shard_map/ppermute | solution.py:21
  37.6 3.2 %collective-permute-start.10 = (bf16[5,4,512]{2,1,0:T(4,128)(2,1)S(1)}, bf16[5,4,512]{2,1,0:T(4,128)(2,1)S(1)}, u32[]{:S(2)}, u32[]{:S(2)}) collective-permute-start(bf16[5,4,512]{2,1,0:T(4,128)(2,1)S(1)} %get-tuple-element.56), channel_id=1, source_target_pairs={{0,2},{2,4},{4,6},{6,0},{1,3},{3,5},{5,7},{7,1},{8,10},{10,12},{12... | collective-permute-start | bytes 61448 | tf_op jit(solution)/shard_map/ppermute | solution.py:21
  37.6 3.2 %collective-permute-start.11 = (bf16[5,4,512]{2,1,0:T(4,128)(2,1)S(1)}, bf16[5,4,512]{2,1,0:T(4,128)(2,1)S(1)}, u32[]{:S(2)}, u32[]{:S(2)}) collective-permute-start(bf16[5,4,512]{2,1,0:T(4,128)(2,1)S(1)} %get-tuple-element.57), channel_id=1, source_target_pairs={{0,6},{2,0},{4,2},{6,4},{1,7},{3,1},{5,3},{7,5},{8,14},{10,8},{12,... | collective-permute-start | bytes 61448 | tf_op jit(solution)/shard_map/ppermute | solution.py:21
  44.6 7.3 %collective-permute-start.14 = (bf16[5,8,2304]{2,1,0:T(8,128)(2,1)S(1)}, bf16[5,8,2304]{2,1,0:T(8,128)(2,1)S(1)}, u32[]{:S(2)}, u32[]{:S(2)}) collective-permute-start(bf16[5,8,2304]{2,1,0:T(8,128)(2,1)S(1)} %get-tuple-element.63), channel_id=1, source_target_pairs={{0,1},{1,0},{2,3},{3,2},{4,5},{5,4},{6,7},{7,6},{8,9},{9,8},{10,11... | collective-permute-start | bytes 552968 | tf_op jit(solution)/shard_map/ppermute | solution.py:21
  45.1 4.0 %collective-permute-start.12 = (bf16[5,4,2304]{2,1,0:T(4,128)(2,1)S(1)}, bf16[5,4,2304]{2,1,0:T(4,128)(2,1)S(1)}, u32[]{:S(2)}, u32[]{:S(2)}) collective-permute-start(bf16[5,4,2304]{2,1,0:T(4,128)(2,1)S(1)} %get-tuple-element.61), channel_id=1, source_target_pairs={{0,2},{2,4},{4,6},{6,0},{1,3},{3,5},{5,7},{7,1},{8,10},{10,12},{12... | collective-permute-start | bytes 276488 | tf_op jit(solution)/shard_map/ppermute | solution.py:21
  46.0 3.1 %collective-permute-start.13 = (bf16[5,4,2304]{2,1,0:T(4,128)(2,1)S(1)}, bf16[5,4,2304]{2,1,0:T(4,128)(2,1)S(1)}, u32[]{:S(2)}, u32[]{:S(2)}) collective-permute-start(bf16[5,4,2304]{2,1,0:T(4,128)(2,1)S(1)} %get-tuple-element.62), channel_id=1, source_target_pairs={{0,6},{2,0},{4,2},{6,4},{1,7},{3,1},{5,3},{7,5},{8,14},{10,8},{12,... | collective-permute-start | bytes 276488 | tf_op jit(solution)/shard_map/ppermute | solution.py:21
  52.1 7.8 %collective-permute-start.17 = (bf16[5,8,2304]{2,1,0:T(8,128)(2,1)S(1)}, bf16[5,8,2304]{2,1,0:T(8,128)(2,1)S(1)}, u32[]{:S(2)}, u32[]{:S(2)}) collective-permute-start(bf16[5,8,2304]{2,1,0:T(8,128)(2,1)S(1)} %get-tuple-element.68), channel_id=1, source_target_pairs={{0,1},{1,0},{2,3},{3,2},{4,5},{5,4},{6,7},{7,6},{8,9},{9,8},{10,11... | collective-permute-start | bytes 552968 | tf_op jit(solution)/shard_map/ppermute | solution.py:21
  52.6 7.2 %collective-permute-start.15 = (bf16[5,4,2304]{2,1,0:T(4,128)(2,1)S(1)}, bf16[5,4,2304]{2,1,0:T(4,128)(2,1)S(1)}, u32[]{:S(2)}, u32[]{:S(2)}) collective-permute-start(bf16[5,4,2304]{2,1,0:T(4,128)(2,1)S(1)} %get-tuple-element.65), channel_id=1, source_target_pairs={{0,8},{8,16},{16,24},{24,0},{1,9},{9,17},{17,25},{25,1},{2,10},{10... | collective-permute-start | bytes 276488 | tf_op jit(solution)/shard_map/ppermute | solution.py:21
  52.6 7.2 %collective-permute-start.16 = (bf16[5,4,2304]{2,1,0:T(4,128)(2,1)S(1)}, bf16[5,4,2304]{2,1,0:T(4,128)(2,1)S(1)}, u32[]{:S(2)}, u32[]{:S(2)}) collective-permute-start(bf16[5,4,2304]{2,1,0:T(4,128)(2,1)S(1)} %get-tuple-element.66), channel_id=1, source_target_pairs={{0,24},{8,0},{16,8},{24,16},{1,25},{9,1},{17,9},{25,17},{2,26},{10... | collective-permute-start | bytes 276488 | tf_op jit(solution)/shard_map/ppermute | solution.py:21
  63.9 5.6 %collective-permute-start.18 = (bf16[5,4,512]{2,1,0:T(4,128)(2,1)S(1)}, bf16[5,4,512]{2,1,0:T(4,128)(2,1)S(1)}, u32[]{:S(2)}, u32[]{:S(2)}) collective-permute-start(bf16[5,4,512]{2,1,0:T(4,128)(2,1)S(1)} %get-tuple-element.71), channel_id=1, source_target_pairs={{0,8},{8,16},{16,24},{24,0},{1,9},{9,17},{17,25},{25,1},{2,10},{10... | collective-permute-start | bytes 61448 | tf_op jit(solution)/shard_map/ppermute | solution.py:21
  63.9 5.6 %collective-permute-start.19 = (bf16[5,4,512]{2,1,0:T(4,128)(2,1)S(1)}, bf16[5,4,512]{2,1,0:T(4,128)(2,1)S(1)}, u32[]{:S(2)}, u32[]{:S(2)}) collective-permute-start(bf16[5,4,512]{2,1,0:T(4,128)(2,1)S(1)} %get-tuple-element.72), channel_id=1, source_target_pairs={{0,24},{8,0},{16,8},{24,16},{1,25},{9,1},{17,9},{25,17},{2,26},{10... | collective-permute-start | bytes 61448 | tf_op jit(solution)/shard_map/ppermute | solution.py:21
  67.7 3.2 %collective-permute-start.20 = (bf16[5,4,512]{2,1,0:T(4,128)(2,1)S(1)}, bf16[5,4,512]{2,1,0:T(4,128)(2,1)S(1)}, u32[]{:S(2)}, u32[]{:S(2)}) collective-permute-start(bf16[5,4,512]{2,1,0:T(4,128)(2,1)S(1)} %get-tuple-element.73), channel_id=1, source_target_pairs={{0,2},{2,4},{4,6},{6,0},{1,3},{3,5},{5,7},{7,1},{8,10},{10,12},{12... | collective-permute-start | bytes 61448 | tf_op jit(solution)/shard_map/ppermute | solution.py:21
  67.7 3.2 %collective-permute-start.21 = (bf16[5,4,512]{2,1,0:T(4,128)(2,1)S(1)}, bf16[5,4,512]{2,1,0:T(4,128)(2,1)S(1)}, u32[]{:S(2)}, u32[]{:S(2)}) collective-permute-start(bf16[5,4,512]{2,1,0:T(4,128)(2,1)S(1)} %get-tuple-element.74), channel_id=1, source_target_pairs={{0,6},{2,0},{4,2},{6,4},{1,7},{3,1},{5,3},{7,5},{8,14},{10,8},{12,... | collective-permute-start | bytes 61448 | tf_op jit(solution)/shard_map/ppermute | solution.py:21

commit v2 on v1

v2 whole, which is shorter than its diff:
```python
import functools

import jax
import jax.numpy as jnp
from jax import lax
from jax.experimental import pallas as pl
from jax.experimental.pallas import tpu as pltpu
from jax.sharding import PartitionSpec as P


ROUNDS = 2
step_size = 0.2
epsilon = 1e-06

BF16 = jnp.bfloat16
F32 = jnp.float32
MIB = 1024 * 1024


def passed_along(value, axis, by):
    devices = lax.axis_size(axis)
    return lax.ppermute(value, axis, [(i, (i + by) % devices) for i in range(devices)])


def from_partners(value, axis):
    return [passed_along(value, axis, by) for by in range(1, lax.axis_size(axis))]


def rows_by_features(left, right):
    return lax.dot_general(left, right, (((1,), (1,)), ((), ())), preferred_element_type=F32)


def in_two_parts(value):
    high = value.astype(BF16)
    low = (value - high.astype(F32)).astype(BF16)
    return jnp.concatenate([high, low], axis=0)


def small_times(small, wide):
    rows = small.shape[0]
    both = jnp.dot(in_two_parts(small), wide, preferred_element_type=F32)
    return both[:rows] + both[rows:]


def call(kernel, outs, args, arg_spaces, scratch=(), limit=16, flops=1_000_000):
    return pl.pallas_call(
        kernel,
        out_shape=[jax.ShapeDtypeStruct(shape, dtype) for shape, dtype, _ in outs],
        in_specs=[pl.BlockSpec(memory_space=space) for space in arg_spaces],
        out_specs=[pl.BlockSpec(memory_space=space) for _, _, space in outs],
        scratch_shapes=list(scratch),
        compiler_params=pltpu.CompilerParams(vmem_limit_bytes=limit * MIB),
        cost_estimate=pl.CostEstimate(flops=flops, bytes_accessed=0, transcendentals=0),
    )(*args)


def store_products(l, row, col, row_keep, row_send, col_keep, left_send, right_send):
    row_keep[l] = row
    row_send[l] = row.astype(BF16)
    col_keep[l] = col
    left_send[l] = col[:4].astype(BF16)
    right_send[l] = col[4:].astype(BF16)


def layer_of(w_refs, l):
    early = w_refs[0].shape[0]
    return (w_refs[0], l) if l < early else (w_refs[1], l - early)


def load_kernel(w_hbm, down_hbm, right_hbm, w_ref, down_ref, right_ref, sems):
    copies = [
        pltpu.make_async_copy(down_hbm, down_ref, sems.at[0]),
        pltpu.make_async_copy(right_hbm, right_ref, sems.at[1]),
    ]
    for l in range(w_ref.shape[0]):
        copies.append(pltpu.make_async_copy(w_hbm.at[l], w_ref.at[l], sems.at[2 + l]))
    for copy in copies:
        copy.start()
    for copy in copies:
        copy.wait()


def first_products_kernel(w_hbm, w_early, up_ref, down_ref, left_ref, right_ref, *refs):
    w_late, *outs, sems = refs
    early, late = w_early.shape[0], w_late.shape[0]
    copies = [
        pltpu.make_async_copy(w_hbm.at[early + l], w_late.at[l], sems.at[l]) for l in range(late)
    ]
    for copy in copies:
        copy.start()
    for l in range(early + late):
        if l >= early:
            copies[l - early].wait()
        ref, at = layer_of((w_early, w_late), l)
        factors = jnp.concatenate([up_ref[l], down_ref[l], left_ref[l], right_ref[l]], axis=0)
        products = rows_by_features(factors, ref[at])
        store_products(l, products[:8], products[8:], *outs)


def middle_col_kernel(col_keep, from_left, from_right, col_diff, col_send):
    for l in range(col_keep.shape[0]):
        col = col_keep[l] - jnp.concatenate([from_left[l], from_right[l]], axis=0).astype(F32)
        col_diff[l] = col
        col_send[l] = col.astype(BF16)


def middle_row_kernel(partners, row_keep, *refs):
    received, (row_total, up_send, down_send) = refs[:partners], refs[partners:]
    for l in range(row_keep.shape[0]):
        row = row_keep[l]
        for other in received:
            row = row + other[l].astype(F32)
        row_total[l] = row
        up_send[l] = row[:4].astype(BF16)
        down_send[l] = row[4:].astype(BF16)


def orthonormal(vectors):
    rank = vectors.shape[0] // 2
    row = lax.broadcasted_iota(jnp.int32, (vectors.shape[0], 1), 0)
    first = row < rank
    place = jnp.where(first, row, row - rank)
    rest, basis = vectors, None
    for k in range(rank):
        current = jnp.where(first, rest[k : k + 1], rest[rank + k : rank + k + 1])
        square = jnp.sum(current * current, axis=1, keepdims=True)
        unit = current * (1.0 / jnp.sqrt(square + epsilon))
        basis = unit if basis is None else jnp.where(place == k, unit, basis)
        if k + 1 < rank:
            along = jnp.sum(vectors * unit, axis=1, keepdims=True)
            rest = rest - along * unit
    return basis


def back_product(l, vectors, earlier, w_refs, pairs, basis_ref, back_ref, sends):
    basis = orthonormal(vectors).astype(BF16)
    basis_ref[l] = basis
    ref, at = layer_of(w_refs, l)
    back = jnp.dot(basis, ref[at], preferred_element_type=F32)
    for e in range(earlier):
        row_basis, col_basis, old_factors = (ref[l] for ref in pairs[3 * e : 3 * e + 3])
        mixing = rows_by_features(basis, jnp.concatenate([row_basis, col_basis], axis=0))
        back = back + small_times(-step_size * mixing, old_factors)
    back_ref[l] = back
    for i, send in enumerate(sends):
        send[l] = back[4 * i : 4 * i + 4].astype(BF16)


def back_col_kernel(partners, earlier, w_early, w_late, col_diff, *refs):
    received, refs = refs[:partners], refs[partners:]
    pairs, (basis_ref, back_ref, *sends) = refs[: 3 * earlier], refs[3 * earlier :]
    for l in range(col_diff.shape[0]):
        col = col_diff[l]
        for other in received:
            col = col + other[l].astype(F32)
        back_product(l, col, earlier, (w_early, w_late), pairs, basis_ref, back_ref, sends)


def back_row_kernel(earlier, w_early, w_late, row_total, from_above, from_below, *refs):
    pairs, (basis_ref, back_ref, *sends) = refs[: 3 * earlier], refs[3 * earlier :]
    for l in range(row_total.shape[0]):
        row = row_total[l] - jnp.concatenate([from_above[l], from_below[l]], axis=0).astype(F32)
        back_product(l, row, earlier, (w_early, w_late), pairs, basis_ref, back_ref, sends)


def combined_of(l, row_back, col_back, above, below, left, right):
    own = jnp.concatenate([row_back[l], col_back[l]], axis=0)
    theirs = jnp.concatenate([above[l], below[l], left[l], right[l]], axis=0)
    return own + theirs.astype(F32)


def next_products_kernel(earlier, w_early, w_late, *refs):
    moved, refs = refs[:6], refs[6:]
    pairs, refs = refs[: 3 * earlier], refs[3 * earlier :]
    row_basis, col_basis, factors_ref, *outs = refs
    for l in range(factors_ref.shape[0]):
        factors = combined_of(l, *moved).astype(BF16)
        factors_ref[l] = factors
        ref, at = layer_of((w_early, w_late), l)
        products = rows_by_features(factors, ref[at])
        known = [tuple(ref[l] for ref in pairs[3 * e : 3 * e + 3]) for e in range(earlier)]
        for row, col, old in known + [(row_basis[l], col_basis[l], factors)]:
            mixing = rows_by_features(factors, old)
            products = products + small_times(
                -step_size * mixing, jnp.concatenate([row, col], axis=0)
            )
        store_products(l, products[:8], products[8:], *outs)


def finish_kernel(earlier, chunk, w_early, w_late, *refs):
    moved, refs = refs[:6], refs[6:]
    pairs, refs = refs[: 3 * earlier], refs[3 * earlier :]
    row_basis, col_basis, w_out, down_out, right_out, staged, sems = refs
    bases = [pairs[3 * e + i] for e in range(earlier) for i in (0, 1)] + [row_basis, col_basis]
    count, depth, _ = staged.shape
    copies = []
    for l in range(count):
        combined = combined_of(l, *moved)
        down_out[l] = combined[4:8]
        right_out[l] = combined[12:]
        old_factors = [pairs[3 * e + 2][l] for e in range(earlier)]
        factors = jnp.concatenate(old_factors + [combined.astype(BF16)], axis=0)
        ref, at = layer_of((w_early, w_late), l)
        for c in range(depth // chunk):
            part = pl.ds(c * chunk, chunk)
            basis = jnp.concatenate([b[l, :, part] for b in bases], axis=0)
            correction = lax.dot_general(
                basis, factors, (((0,), (0,)), ((), ())), preferred_element_type=F32
            )
            staged[l, part] = (ref[at, part].astype(F32) - step_size * correction).astype(BF16)
            copy = pltpu.make_async_copy(
                staged.at[l, part], w_out.at[l, part], sems.at[l, c]
            )
            copy.start()
            copies.append(copy)
    for copy in copies:
        copy.wait()


def body(weights, warm_down, warm_right):
    vmem, hbm = pltpu.VMEM, pltpu.HBM
    w, down, right = weights[0, 0], warm_down[0, 0], warm_right[0, 0]
    count, depth, width = w.shape
    rank = down.shape[1]
    partners = lax.axis_size("mp") - 1
    pair, every = 2 * rank, 4 * rank

    def local(kernel, outs, args, **more):
        return call(kernel, outs, args, [vmem] * len(args), **more)

    kept = ((count, pair, depth), F32, vmem)
    both_edges = ((count, pair, depth), BF16, vmem)
    one_edge = ((count, rank, depth), BF16, vmem)
    product_outs = [kept, both_edges, kept, one_edge, one_edge]
    back_outs = [both_edges, ((count, pair, width), F32, vmem)]
    back_outs += [((count, rank, width), BF16, vmem)] * 2

    above = passed_along(down, "row", 1)
    beside = passed_along(right, "col", 1)
    w_hbm, down_hbm, right_hbm = (
        pltpu.with_memory_space_constraint(x, pltpu.HBM) for x in (w, down, right)
    )
    early = max(1, 2 * count // 5)
    own_factors = ((count, rank, width), BF16, vmem)
    w_early, own_down, own_right = call(
        load_kernel,
        [((early, depth, width), BF16, vmem), own_factors, own_factors],
        (w_hbm, down_hbm, right_hbm),
        [hbm] * 3,
        [pltpu.SemaphoreType.DMA((early + 2,))],
        flops=100_000_000,
    )
    w_late, *products = call(
        first_products_kernel,
        [((count - early, depth, width), BF16, vmem)] + product_outs,
        (w_hbm, w_early, above, own_down, beside, own_right),
        [hbm] + [vmem] * 5,
        [pltpu.SemaphoreType.DMA((count - early,))],
    )
    w = (w_early, w_late)
    pairs = ()
    for repeat in range(ROUNDS):
        row_keep, row_send, col_keep, left_send, right_send = products
        row_received = from_partners(row_send, "mp")
        from_left = passed_along(right_send, "col", 1)
        from_right = passed_along(left_send, "col", -1)
        col_diff, col_send = local(
            middle_col_kernel, [kept, both_edges], (col_keep, from_left, from_right),
        )
        col_received = from_partners(col_send, "mp")
        row_total, up_send, down_send = local(
            functools.partial(middle_row_kernel, partners),
            [kept, one_edge, one_edge], (row_keep, *row_received),
        )
        from_above = passed_along(down_send, "row", 1)
        from_below = passed_along(up_send, "row", -1)
        col_basis, col_back, left_send, right_send = local(
            functools.partial(back_col_kernel, partners, repeat),
            back_outs, (*w, col_diff, *col_received, *pairs),
        )
        from_left = passed_along(right_send, "col", 1)
        from_right = passed_along(left_send, "col", -1)
        row_basis, row_back, up_send, down_send = local(
            functools.partial(back_row_kernel, repeat),
            back_outs, (*w, row_total, from_above, from_below, *pairs),
        )
        from_above = passed_along(down_send, "row", 1)
        from_below = passed_along(up_send, "row", -1)
        moved = (row_back, col_back, from_above, from_below, from_left, from_right)
        args = (*w, *moved, *pairs, row_basis, col_basis)
        if repeat + 1 < ROUNDS:
            factors, *products = local(
                functools.partial(next_products_kernel, repeat),
                [((count, every, width), BF16, vmem)] + product_outs, args,
            )
            pairs = (*pairs, row_basis, col_basis, factors)
    chunk = depth // 3 if depth % 384 == 0 else depth
    new_w, next_down, next_right = local(
        functools.partial(finish_kernel, ROUNDS - 1, chunk),
        [
            ((count, depth, width), BF16, hbm),
            ((count, rank, width), F32, vmem),
            ((count, rank, width), F32, vmem),
        ],
        args,
        scratch=[
            pltpu.VMEM((count, depth, width), BF16),
            pltpu.SemaphoreType.DMA((count, depth // chunk)),
        ],
        limit=28,
    )
    return new_w[None, None], next_down[None, None], next_right[None, None]


def solution(mesh):
    placed = (P("row", "col", None, None, "mp"),) * 3
    return jax.shard_map(body, mesh=mesh, in_specs=placed, out_specs=placed, check_vma=False)
```

time: 77.6 us -> 72.8 us (0.938); the launches traced: 76.6 us -> 72.6 us
  waiting for transfers between devices: 19.2 us -> 11 us
  Pallas kernels: 25.4 us -> 28.7 us
  starting transfers between devices: 29.6 us -> 32.1 us
  local copies, waits for them, and re-layouts: 1.48 us -> 0 us
    ppermute x22, waiting for transfers between devices: 19.2 us -> 11 us  [passed_along(): lax.ppermute(value, axis, [(i, (i + by) % devices) for i in range(devices)])]
    pallas_call x8 -> x12, Pallas kernels: 25.4 us -> 28.7 us  [call(): pl.pallas_call(kernel, out_shape=[jax.ShapeDtypeStruct(shape, dtype) for...]
    ppermute x22, starting transfers between devices: 29.6 us -> 32.1 us  [passed_along(): lax.ppermute(value, axis, [(i, (i + by) % devices) for i in range(devices)])]
    unnamed x4 -> x0, local copies, waits for them, and re-layouts: 1.48 us -> none
  transfers between devices with their start and end apart: 22 -> 22, of which waited for: 9 -> 8; matrix products, arithmetic and copies ran while one was open for 0% -> 0% of each run, Pallas kernels for 7% -> 20%
where the time goes in v2:
time: 72.8 us; the launch traced here: 72.6 us
  starting transfers between devices  32.1 us (44%)
  Pallas kernels  28.7 us (39%)
  waiting for transfers between devices  11 us (15%)
  between operations  0.85 us (1%)
    ppermute x22, starting transfers between devices, passed_along(): lax.ppermute(value, axis, [(i, (i + by) % devices) for i in range(devices)])  32.1 us
    pallas_call x12, Pallas kernels, call(): pl.pallas_call(kernel, out_shape=[jax.ShapeDtypeStruct(shape, dtype) for...  28.7 us
    ppermute x22, waiting for transfers between devices, passed_along(): lax.ppermute(value, axis, [(i, (i + by) % devices) for i in range(devices)])  11 us
  transfers between devices with their start and end apart: 22, of which 8 were waited for; matrix products, arithmetic and copies ran while one was open for 0% of the time, Pallas kernels for 20%

profile of v2, /device:TPU:0, one launch (start us, length us, event | category | flops | bytes accessed | tf_op | source)
XLA Modules:
  0.0 72.6 jit_solution(17926649942066931850)
XLA Ops:
  0.6 3.1 %collective-permute-start = (bf16[5,4,512]{2,1,0:T(4,128)(2,1)}, bf16[5,4,512]{2,1,0:T(4,128)(2,1)S(1)}, u32[]{:S(2)}, u32[]{:S(2)}) collective-permute-start(bf16[5,4,512]{2,1,0:T(4,128)(2,1)} %bitcast.8), channel_id=1, source_target_pairs={{0,8},{8,16},{16,24},{24,0},{1,9},{9,17},{17,25},{25,1},{2,10},{10... | collective-permute-start | bytes 61448 | tf_op jit(solution)/shard_map/ppermute | solution.py:22
  3.7 0.0 collective-permute-start.1
  3.7 2.4 %shard_map.58 = (bf16[2,2304,512]{2,1,0:T(8,128)(2,1)S(1)}, bf16[5,4,512]{2,1,0:T(4,128)(2,1)S(1)}, bf16[5,4,512]{2,1,0:T(4,128)(2,1)S(1)}) custom-call(bf16[5,2304,512]{2,1,0:T(8,128)(2,1)} %bitcast.6, bf16[5,4,512]{2,1,0:T(4,128)(2,1)} %bitcast.9, bf16[5,4,512]{2,1,0:T(4,128)(2,1)} %bitcast.11), custom_call_target="tpu_custom_call" | custom-call | flops 100000000 | tf_op jit(solution)/shard_map/pallas_call | solution.py:46
  6.2 1.5 %collective-permute-done.up_ref = bf16[5,4,512]{2,1,0:T(4,128)(2,1)S(1)} collective-permute-done((bf16[5,4,512]{2,1,0:T(4,128)(2,1)}, bf16[5,4,512]{2,1,0:T(4,128)(2,1)S(1)}, u32[]{:S(2)}, u32[]{:S(2)}) %collective-permute-start) | collective-permute-done | bytes 20512 | tf_op jit(solution)/shard_map/ppermute | solution.py:22
  7.7 0.0 collective-permute-done.1.left_ref
  7.7 4.6 %shard_map.59 = (bf16[3,2304,512]{2,1,0:T(8,128)(2,1)S(1)}, f32[5,8,2304]{2,1,0:T(8,128)S(1)}, bf16[5,8,2304]{2,1,0:T(8,128)(2,1)S(1)}, f32[5,8,2304]{2,1,0:T(8,...) custom-call(bf16[5,2304,512]{2,1,0:T(8,128)(2,1)} %bitcast.7, ...), custom_call_target="tpu_custom_call" | custom-call | flops 1000000 | tf_op jit(solution)/shard_map/pallas_call | solution.py:46
  12.4 0.1 collective-permute-start.5
  12.5 1.7 %collective-permute-start.6 = (bf16[5,4,2304]{2,1,0:T(4,128)(2,1)S(1)}, bf16[5,4,2304]{2,1,0:T(4,128)(2,1)S(1)}, u32[]{:S(2)}, u32[]{:S(2)}) collective-permute-start(bf16[5,4,2304]{2,1,0:T(4,128)(2,1)S(1)} %get-tuple-element.59), channel_id=1, source_target_pairs={{0,6},{2,0},{4,2},{6,4},{1,7},{3,1},{5,3},{7,5},{8,14},{10,8},{12,... | collective-permute-start | bytes 276488 | tf_op jit(solution)/shard_map/ppermute | solution.py:22
  14.2 1.7 %collective-permute-start.2 = (bf16[5,8,2304]{2,1,0:T(8,128)(2,1)S(1)}, bf16[5,8,2304]{2,1,0:T(8,128)(2,1)S(1)}, u32[]{:S(2)}, u32[]{:S(2)}) collective-permute-start(bf16[5,8,2304]{2,1,0:T(8,128)(2,1)S(1)} %get-tuple-element.52), channel_id=1, source_target_pairs={{0,1},{1,0},{2,3},{3,2},{4,5},{5,4},{6,7},{7,6},{8,9},{9,8},{10,11... | collective-permute-start | bytes 552968 | tf_op jit(solution)/shard_map/ppermute | solution.py:22
  15.9 0.5 collective-permute-done.5.from_left
  16.4 0.2 collective-permute-done.6.from_right
  16.6 0.1 shard_map.62
  16.7 1.6 %collective-permute-start.7 = (bf16[5,8,2304]{2,1,0:T(8,128)(2,1)S(1)}, bf16[5,8,2304]{2,1,0:T(8,128)(2,1)S(1)}, u32[]{:S(2)}, u32[]{:S(2)}) collective-permute-start(bf16[5,8,2304]{2,1,0:T(8,128)(2,1)S(1)} %get-tuple-element.61), channel_id=1, source_target_pairs={{0,1},{1,0},{2,3},{3,2},{4,5},{5,4},{6,7},{7,6},{8,9},{9,8},{10,11... | collective-permute-start | bytes 552968 | tf_op jit(solution)/shard_map/ppermute | solution.py:22
  18.3 2.5 %collective-permute-done.2.refs_0_ = bf16[5,8,2304]{2,1,0:T(8,128)(2,1)S(1)} collective-permute-done((bf16[5,8,2304]{2,1,0:T(8,128)(2,1)S(1)}, bf16[5,8,2304]{2,1,0:T(8,128)(2,1)S(1)}, u32[]{:S(2)}, u32[]{:S(2)}) %collective-permute-start.2) | collective-permute-done | bytes 184352 | tf_op jit(solution)/shard_map/ppermute | solution.py:22
  20.8 0.1 shard_map.60
  20.9 0.8 %collective-permute-start.3 = (bf16[5,4,2304]{2,1,0:T(4,128)(2,1)S(1)}, bf16[5,4,2304]{2,1,0:T(4,128)(2,1)S(1)}, u32[]{:S(2)}, u32[]{:S(2)}) collective-permute-start(bf16[5,4,2304]{2,1,0:T(4,128)(2,1)S(1)} %get-tuple-element.54), channel_id=1, source_target_pairs={{0,8},{8,16},{16,24},{24,0},{1,9},{9,17},{17,25},{25,1},{2,10},{10... | collective-permute-start | bytes 276488 | tf_op jit(solution)/shard_map/ppermute | solution.py:22
  21.7 3.0 %collective-permute-start.4 = (bf16[5,4,2304]{2,1,0:T(4,128)(2,1)S(1)}, bf16[5,4,2304]{2,1,0:T(4,128)(2,1)S(1)}, u32[]{:S(2)}, u32[]{:S(2)}) collective-permute-start(bf16[5,4,2304]{2,1,0:T(4,128)(2,1)S(1)} %get-tuple-element.55), channel_id=1, source_target_pairs={{0,24},{8,0},{16,8},{24,16},{1,25},{9,1},{17,9},{25,17},{2,26},{10... | collective-permute-start | bytes 276488 | tf_op jit(solution)/shard_map/ppermute | solution.py:22
  24.7 0.0 collective-permute-done.7.refs_0_
  24.7 2.5 %shard_map.63 = (bf16[5,8,2304]{2,1,0:T(8,128)(2,1)S(1)}, f32[5,8,512]{2,1,0:T(8,128)S(1)}, bf16[5,4,512]{2,1,0:T(4,128)(2,1)S(1)}, bf16[5,4,512]{2,1,0:T(4,128)(2,1)S(1)}) custom-call(bf16[2,2304,512]{2,1,0:T(8,128)(2,1)S(1)} %get-tuple-element.47.w_early, bf16[3,2304,512]{2,1,0:T(8,128)(2,1)S(1)} %get-tuple-element.50.w_late, ...), custom_call_target="tpu_custom_call" | custom-call | flops 1000000 | tf_op jit(solution)/shard_map/pallas_call | solution.py:46
  27.3 1.8 %collective-permute-start.11 = (bf16[5,4,512]{2,1,0:T(4,128)(2,1)S(1)}, bf16[5,4,512]{2,1,0:T(4,128)(2,1)S(1)}, u32[]{:S(2)}, u32[]{:S(2)}) collective-permute-start(bf16[5,4,512]{2,1,0:T(4,128)(2,1)S(1)} %get-tuple-element.66), channel_id=1, source_target_pairs={{0,6},{2,0},{4,2},{6,4},{1,7},{3,1},{5,3},{7,5},{8,14},{10,8},{12,... | collective-permute-start | bytes 61448 | tf_op jit(solution)/shard_map/ppermute | solution.py:22
  29.0 0.0 collective-permute-done.3.from_above
  29.0 0.0 collective-permute-done.4.from_below
  29.0 2.6 %shard_map.61 = (bf16[5,8,2304]{2,1,0:T(8,128)(2,1)S(1)}, f32[5,8,512]{2,1,0:T(8,128)S(1)}, bf16[5,4,512]{2,1,0:T(4,128)(2,1)S(1)}, bf16[5,4,512]{2,1,0:T(4,128)(2,1)S(1)}) custom-call(bf16[2,2304,512]{2,1,0:T(8,128)(2,1)S(1)} %get-tuple-element.47.w_early, bf16[3,2304,512]{2,1,0:T(8,128)(2,1)S(1)} %get-tuple-element.50.w_late, ...), custom_call_target="tpu_custom_call" | custom-call | flops 1000000 | tf_op jit(solution)/shard_map/pallas_call | solution.py:46
  31.6 0.3 collective-permute-start.8
  31.9 3.5 %collective-permute-start.9 = (bf16[5,4,512]{2,1,0:T(4,128)(2,1)S(1)}, bf16[5,4,512]{2,1,0:T(4,128)(2,1)S(1)}, u32[]{:S(2)}, u32[]{:S(2)}) collective-permute-start(bf16[5,4,512]{2,1,0:T(4,128)(2,1)S(1)} %get-tuple-element.64), channel_id=1, source_target_pairs={{0,24},{8,0},{16,8},{24,16},{1,25},{9,1},{17,9},{25,17},{2,26},{10... | collective-permute-start | bytes 61448 | tf_op jit(solution)/shard_map/ppermute | solution.py:22
  35.4 0.0 collective-permute-done.10.refs_4_
  35.4 0.0 collective-permute-done.11.refs_5_
  35.4 1.7 %collective-permute-done.8.refs_2_ = bf16[5,4,512]{2,1,0:T(4,128)(2,1)S(1)} collective-permute-done((bf16[5,4,512]{2,1,0:T(4,128)(2,1)S(1)}, bf16[5,4,512]{2,1,0:T(4,128)(2,1)S(1)}, u32[]{:S(2)}, u32[]{:S(2)}) %collective-permute-start.8) | collective-permute-done | bytes 20512 | tf_op jit(solution)/shard_map/ppermute | solution.py:22
  37.2 3.8 %shard_map.64 = (bf16[5,16,512]{2,1,0:T(8,128)(2,1)S(1)}, f32[5,8,2304]{2,1,0:T(8,128)S(1)}, bf16[5,8,2304]{2,1,0:T(8,128)(2,1)S(1)}, f32[5,8,2304]{2,1,0:T(8,12...) custom-call(bf16[2,2304,512]{2,1,0:T(8,128)(2,1)S(1)} %get-tuple-element.47.w_early, ...), custom_call_target="tpu_custom_call" | custom-call | flops 1000000 | tf_op jit(solution)/shard_map/pallas_call | solution.py:46
  41.0 0.0 collective-permute-start.15
  41.0 1.7 %collective-permute-start.16 = (bf16[5,4,2304]{2,1,0:T(4,128)(2,1)S(1)}, bf16[5,4,2304]{2,1,0:T(4,128)(2,1)S(1)}, u32[]{:S(2)}, u32[]{:S(2)}) collective-permute-start(bf16[5,4,2304]{2,1,0:T(4,128)(2,1)S(1)} %get-tuple-element.78), channel_id=1, source_target_pairs={{0,6},{2,0},{4,2},{6,4},{1,7},{3,1},{5,3},{7,5},{8,14},{10,8},{12,... | collective-permute-start | bytes 276488 | tf_op jit(solution)/shard_map/ppermute | solution.py:22
  42.7 1.5 %collective-permute-start.12 = (bf16[5,8,2304]{2,1,0:T(8,128)(2,1)S(1)}, bf16[5,8,2304]{2,1,0:T(8,128)(2,1)S(1)}, u32[]{:S(2)}, u32[]{:S(2)}) collective-permute-start(bf16[5,8,2304]{2,1,0:T(8,128)(2,1)S(1)} %get-tuple-element.70), channel_id=1, source_target_pairs={{0,1},{1,0},{2,3},{3,2},{4,5},{5,4},{6,7},{7,6},{8,9},{9,8},{10,11... | collective-permute-start | bytes 552968 | tf_op jit(solution)/shard_map/ppermute | solution.py:22
  44.3 0.7 collective-permute-done.15.from_left
  45.0 0.0 collective-permute-done.16.from_right
  45.0 0.1 shard_map.67
  45.1 1.6 %collective-permute-start.17 = (bf16[5,8,2304]{2,1,0:T(8,128)(2,1)S(1)}, bf16[5,8,2304]{2,1,0:T(8,128)(2,1)S(1)}, u32[]{:S(2)}, u32[]{:S(2)}) collective-permute-start(bf16[5,8,2304]{2,1,0:T(8,128)(2,1)S(1)} %get-tuple-element.80), channel_id=1, source_target_pairs={{0,1},{1,0},{2,3},{3,2},{4,5},{5,4},{6,7},{7,6},{8,9},{9,8},{10,11... | collective-permute-start | bytes 552968 | tf_op jit(solution)/shard_map/ppermute | solution.py:22
  46.6 2.0 %collective-permute-done.12.refs_0_ = bf16[5,8,2304]{2,1,0:T(8,128)(2,1)S(1)} collective-permute-done((bf16[5,8,2304]{2,1,0:T(8,128)(2,1)S(1)}, bf16[5,8,2304]{2,1,0:T(8,128)(2,1)S(1)}, u32[]{:S(2)}, u32[]{:S(2)}) %collective-permute-start.12) | collective-permute-done | bytes 184352 | tf_op jit(solution)/shard_map/ppermute | solution.py:22
  48.6 0.1 shard_map.65
  48.7 0.7 collective-permute-start.13
  49.4 3.2 %collective-permute-start.14 = (bf16[5,4,2304]{2,1,0:T(4,128)(2,1)S(1)}, bf16[5,4,2304]{2,1,0:T(4,128)(2,1)S(1)}, u32[]{:S(2)}, u32[]{:S(2)}) collective-permute-start(bf16[5,4,2304]{2,1,0:T(4,128)(2,1)S(1)} %get-tuple-element.73), channel_id=1, source_target_pairs={{0,24},{8,0},{16,8},{24,16},{1,25},{9,1},{17,9},{25,17},{2,26},{10... | collective-permute-start | bytes 276488 | tf_op jit(solution)/shard_map/ppermute | solution.py:22
  52.6 3.5 %shard_map.68 = (bf16[5,8,2304]{2,1,0:T(8,128)(2,1)S(1)}, f32[5,8,512]{2,1,0:T(8,128)S(1)}, bf16[5,4,512]{2,1,0:T(4,128)(2,1)S(1)}, bf16[5,4,512]{2,1,0:T(4,128)(2,1)S(1)}) custom-call(bf16[2,2304,512]{2,1,0:T(8,128)(2,1)S(1)} %get-tuple-element.47.w_early, bf16[3,2304,512]{2,1,0:T(8,128)(2,1)S(1)} %get-tuple-element.50.w_late, ...), custom_call_target="tpu_custom_call" | custom-call | flops 1000000 | tf_op jit(solution)/shard_map/pallas_call | solution.py:46
  56.1 0.1 collective-permute-start.20
  56.1 1.7 %collective-permute-start.21 = (bf16[5,4,512]{2,1,0:T(4,128)(2,1)S(1)}, bf16[5,4,512]{2,1,0:T(4,128)(2,1)S(1)}, u32[]{:S(2)}, u32[]{:S(2)}) collective-permute-start(bf16[5,4,512]{2,1,0:T(4,128)(2,1)S(1)} %get-tuple-element.85), channel_id=1, source_target_pairs={{0,6},{2,0},{4,2},{6,4},{1,7},{3,1},{5,3},{7,5},{8,14},{10,8},{12,... | collective-permute-start | bytes 61448 | tf_op jit(solution)/shard_map/ppermute | solution.py:22
  57.8 3.5 %shard_map.66 = (bf16[5,8,2304]{2,1,0:T(8,128)(2,1)S(1)}, f32[5,8,512]{2,1,0:T(8,128)S(1)}, bf16[5,4,512]{2,1,0:T(4,128)(2,1)S(1)}, bf16[5,4,512]{2,1,0:T(4,128)(2,1)S(1)}) custom-call(bf16[2,2304,512]{2,1,0:T(8,128)(2,1)S(1)} %get-tuple-element.47.w_early, bf16[3,2304,512]{2,1,0:T(8,128)(2,1)S(1)} %get-tuple-element.50.w_late, ...), custom_call_target="tpu_custom_call" | custom-call | flops 1000000 | tf_op jit(solution)/shard_map/pallas_call | solution.py:46
  61.3 0.2 collective-permute-start.18
  61.5 3.7 %collective-permute-start.19 = (bf16[5,4,512]{2,1,0:T(4,128)(2,1)S(1)}, bf16[5,4,512]{2,1,0:T(4,128)(2,1)S(1)}, u32[]{:S(2)}, u32[]{:S(2)}) collective-permute-start(bf16[5,4,512]{2,1,0:T(4,128)(2,1)S(1)} %get-tuple-element.83), channel_id=1, source_target_pairs={{0,24},{8,0},{16,8},{24,16},{1,25},{9,1},{17,9},{25,17},{2,26},{10... | collective-permute-start | bytes 61448 | tf_op jit(solution)/shard_map/ppermute | solution.py:22
  65.2 1.7 %collective-permute-done.18.refs_2_ = bf16[5,4,512]{2,1,0:T(4,128)(2,1)S(1)} collective-permute-done((bf16[5,4,512]{2,1,0:T(4,128)(2,1)S(1)}, bf16[5,4,512]{2,1,0:T(4,128)(2,1)S(1)}, u32[]{:S(2)}, u32[]{:S(2)}) %collective-permute-start.18) | collective-permute-done | bytes 20512 | tf_op jit(solution)/shard_map/ppermute | solution.py:22
  67.0 5.5 %shard_map.69 = (bf16[5,2304,512]{2,1,0:T(8,128)(2,1)}, f32[5,4,512]{2,1,0:T(4,128)}, f32[5,4,512]{2,1,0:T(4,128)}) custom-call(bf16[2,2304,512]{2,1,0:T(8,128)(2,1)S(1)} %get-tuple-element.47.w_early, bf16[3,2304,512]{2,1,0:T(8,128)(2,1)S(1)} %get-tuple-element.50.w_late, f32[5,8,512]{2,1,0:T(8,128)S(1)} %get-tuple-element.75.refs_0_, ...), custom_call_target="tpu_custom_call" | custom-call | flops 1000000 | tf_op jit(solution)/shard_map/pallas_call | solution.py:46
  (8 shorter events, 0.0 us)
Async XLA Ops:
  0.6 7.1 %collective-permute-start = (bf16[5,4,512]{2,1,0:T(4,128)(2,1)}, bf16[5,4,512]{2,1,0:T(4,128)(2,1)S(1)}, u32[]{:S(2)}, u32[]{:S(2)}) collective-permute-start(bf16[5,4,512]{2,1,0:T(4,128)(2,1)} %bitcast.8), channel_id=1, source_target_pairs={{0,8},{8,16},{16,24},{24,0},{1,9},{9,17},{17,25},{25,1},{2,10},{10... | collective-permute-start | bytes 61448 | tf_op jit(solution)/shard_map/ppermute | solution.py:22
  3.7 4.0 %collective-permute-start.1 = (bf16[5,4,512]{2,1,0:T(4,128)(2,1)}, bf16[5,4,512]{2,1,0:T(4,128)(2,1)S(1)}, u32[]{:S(2)}, u32[]{:S(2)}) collective-permute-start(bf16[5,4,512]{2,1,0:T(4,128)(2,1)} %bitcast.10), channel_id=1, source_target_pairs={{0,2},{2,4},{4,6},{6,0},{1,3},{3,5},{5,7},{7,1},{8,10},{10,12},{12... | collective-permute-start | bytes 61448 | tf_op jit(solution)/shard_map/ppermute | solution.py:22
  12.4 4.0 %collective-permute-start.5 = (bf16[5,4,2304]{2,1,0:T(4,128)(2,1)S(1)}, bf16[5,4,2304]{2,1,0:T(4,128)(2,1)S(1)}, u32[]{:S(2)}, u32[]{:S(2)}) collective-permute-start(bf16[5,4,2304]{2,1,0:T(4,128)(2,1)S(1)} %get-tuple-element.58), channel_id=1, source_target_pairs={{0,2},{2,4},{4,6},{6,0},{1,3},{3,5},{5,7},{7,1},{8,10},{10,12},{12... | collective-permute-start | bytes 276488 | tf_op jit(solution)/shard_map/ppermute | solution.py:22
  12.5 4.1 %collective-permute-start.6 = (bf16[5,4,2304]{2,1,0:T(4,128)(2,1)S(1)}, bf16[5,4,2304]{2,1,0:T(4,128)(2,1)S(1)}, u32[]{:S(2)}, u32[]{:S(2)}) collective-permute-start(bf16[5,4,2304]{2,1,0:T(4,128)(2,1)S(1)} %get-tuple-element.59), channel_id=1, source_target_pairs={{0,6},{2,0},{4,2},{6,4},{1,7},{3,1},{5,3},{7,5},{8,14},{10,8},{12,... | collective-permute-start | bytes 276488 | tf_op jit(solution)/shard_map/ppermute | solution.py:22
  14.2 6.6 %collective-permute-start.2 = (bf16[5,8,2304]{2,1,0:T(8,128)(2,1)S(1)}, bf16[5,8,2304]{2,1,0:T(8,128)(2,1)S(1)}, u32[]{:S(2)}, u32[]{:S(2)}) collective-permute-start(bf16[5,8,2304]{2,1,0:T(8,128)(2,1)S(1)} %get-tuple-element.52), channel_id=1, source_target_pairs={{0,1},{1,0},{2,3},{3,2},{4,5},{5,4},{6,7},{7,6},{8,9},{9,8},{10,11... | collective-permute-start | bytes 552968 | tf_op jit(solution)/shard_map/ppermute | solution.py:22
  16.7 8.0 %collective-permute-start.7 = (bf16[5,8,2304]{2,1,0:T(8,128)(2,1)S(1)}, bf16[5,8,2304]{2,1,0:T(8,128)(2,1)S(1)}, u32[]{:S(2)}, u32[]{:S(2)}) collective-permute-start(bf16[5,8,2304]{2,1,0:T(8,128)(2,1)S(1)} %get-tuple-element.61), channel_id=1, source_target_pairs={{0,1},{1,0},{2,3},{3,2},{4,5},{5,4},{6,7},{7,6},{8,9},{9,8},{10,11... | collective-permute-start | bytes 552968 | tf_op jit(solution)/shard_map/ppermute | solution.py:22
  20.9 8.2 %collective-permute-start.3 = (bf16[5,4,2304]{2,1,0:T(4,128)(2,1)S(1)}, bf16[5,4,2304]{2,1,0:T(4,128)(2,1)S(1)}, u32[]{:S(2)}, u32[]{:S(2)}) collective-permute-start(bf16[5,4,2304]{2,1,0:T(4,128)(2,1)S(1)} %get-tuple-element.54), channel_id=1, source_target_pairs={{0,8},{8,16},{16,24},{24,0},{1,9},{9,17},{17,25},{25,1},{2,10},{10... | collective-permute-start | bytes 276488 | tf_op jit(solution)/shard_map/ppermute | solution.py:22
  21.7 7.4 %collective-permute-start.4 = (bf16[5,4,2304]{2,1,0:T(4,128)(2,1)S(1)}, bf16[5,4,2304]{2,1,0:T(4,128)(2,1)S(1)}, u32[]{:S(2)}, u32[]{:S(2)}) collective-permute-start(bf16[5,4,2304]{2,1,0:T(4,128)(2,1)S(1)} %get-tuple-element.55), channel_id=1, source_target_pairs={{0,24},{8,0},{16,8},{24,16},{1,25},{9,1},{17,9},{25,17},{2,26},{10... | collective-permute-start | bytes 276488 | tf_op jit(solution)/shard_map/ppermute | solution.py:22
  27.3 8.1 %collective-permute-start.10 = (bf16[5,4,512]{2,1,0:T(4,128)(2,1)S(1)}, bf16[5,4,512]{2,1,0:T(4,128)(2,1)S(1)}, u32[]{:S(2)}, u32[]{:S(2)}) collective-permute-start(bf16[5,4,512]{2,1,0:T(4,128)(2,1)S(1)} %get-tuple-element.65), channel_id=1, source_target_pairs={{0,2},{2,4},{4,6},{6,0},{1,3},{3,5},{5,7},{7,1},{8,10},{10,12},{12... | collective-permute-start | bytes 61448 | tf_op jit(solution)/shard_map/ppermute | solution.py:22
  27.3 8.1 %collective-permute-start.11 = (bf16[5,4,512]{2,1,0:T(4,128)(2,1)S(1)}, bf16[5,4,512]{2,1,0:T(4,128)(2,1)S(1)}, u32[]{:S(2)}, u32[]{:S(2)}) collective-permute-start(bf16[5,4,512]{2,1,0:T(4,128)(2,1)S(1)} %get-tuple-element.66), channel_id=1, source_target_pairs={{0,6},{2,0},{4,2},{6,4},{1,7},{3,1},{5,3},{7,5},{8,14},{10,8},{12,... | collective-permute-start | bytes 61448 | tf_op jit(solution)/shard_map/ppermute | solution.py:22
  31.6 5.6 %collective-permute-start.8 = (bf16[5,4,512]{2,1,0:T(4,128)(2,1)S(1)}, bf16[5,4,512]{2,1,0:T(4,128)(2,1)S(1)}, u32[]{:S(2)}, u32[]{:S(2)}) collective-permute-start(bf16[5,4,512]{2,1,0:T(4,128)(2,1)S(1)} %get-tuple-element.63), channel_id=1, source_target_pairs={{0,8},{8,16},{16,24},{24,0},{1,9},{9,17},{17,25},{25,1},{2,10},{10... | collective-permute-start | bytes 61448 | tf_op jit(solution)/shard_map/ppermute | solution.py:22
  31.9 5.3 %collective-permute-start.9 = (bf16[5,4,512]{2,1,0:T(4,128)(2,1)S(1)}, bf16[5,4,512]{2,1,0:T(4,128)(2,1)S(1)}, u32[]{:S(2)}, u32[]{:S(2)}) collective-permute-start(bf16[5,4,512]{2,1,0:T(4,128)(2,1)S(1)} %get-tuple-element.64), channel_id=1, source_target_pairs={{0,24},{8,0},{16,8},{24,16},{1,25},{9,1},{17,9},{25,17},{2,26},{10... | collective-permute-start | bytes 61448 | tf_op jit(solution)/shard_map/ppermute | solution.py:22
  41.0 4.0 %collective-permute-start.15 = (bf16[5,4,2304]{2,1,0:T(4,128)(2,1)S(1)}, bf16[5,4,2304]{2,1,0:T(4,128)(2,1)S(1)}, u32[]{:S(2)}, u32[]{:S(2)}) collective-permute-start(bf16[5,4,2304]{2,1,0:T(4,128)(2,1)S(1)} %get-tuple-element.77), channel_id=1, source_target_pairs={{0,2},{2,4},{4,6},{6,0},{1,3},{3,5},{5,7},{7,1},{8,10},{10,12},{12... | collective-permute-start | bytes 276488 | tf_op jit(solution)/shard_map/ppermute | solution.py:22
  41.0 4.0 %collective-permute-start.16 = (bf16[5,4,2304]{2,1,0:T(4,128)(2,1)S(1)}, bf16[5,4,2304]{2,1,0:T(4,128)(2,1)S(1)}, u32[]{:S(2)}, u32[]{:S(2)}) collective-permute-start(bf16[5,4,2304]{2,1,0:T(4,128)(2,1)S(1)} %get-tuple-element.78), channel_id=1, source_target_pairs={{0,6},{2,0},{4,2},{6,4},{1,7},{3,1},{5,3},{7,5},{8,14},{10,8},{12,... | collective-permute-start | bytes 276488 | tf_op jit(solution)/shard_map/ppermute | solution.py:22
  42.7 5.9 %collective-permute-start.12 = (bf16[5,8,2304]{2,1,0:T(8,128)(2,1)S(1)}, bf16[5,8,2304]{2,1,0:T(8,128)(2,1)S(1)}, u32[]{:S(2)}, u32[]{:S(2)}) collective-permute-start(bf16[5,8,2304]{2,1,0:T(8,128)(2,1)S(1)} %get-tuple-element.70), channel_id=1, source_target_pairs={{0,1},{1,0},{2,3},{3,2},{4,5},{5,4},{6,7},{7,6},{8,9},{9,8},{10,11... | collective-permute-start | bytes 552968 | tf_op jit(solution)/shard_map/ppermute | solution.py:22
  45.1 7.5 %collective-permute-start.17 = (bf16[5,8,2304]{2,1,0:T(8,128)(2,1)S(1)}, bf16[5,8,2304]{2,1,0:T(8,128)(2,1)S(1)}, u32[]{:S(2)}, u32[]{:S(2)}) collective-permute-start(bf16[5,8,2304]{2,1,0:T(8,128)(2,1)S(1)} %get-tuple-element.80), channel_id=1, source_target_pairs={{0,1},{1,0},{2,3},{3,2},{4,5},{5,4},{6,7},{7,6},{8,9},{9,8},{10,11... | collective-permute-start | bytes 552968 | tf_op jit(solution)/shard_map/ppermute | solution.py:22
  48.7 9.1 %collective-permute-start.13 = (bf16[5,4,2304]{2,1,0:T(4,128)(2,1)S(1)}, bf16[5,4,2304]{2,1,0:T(4,128)(2,1)S(1)}, u32[]{:S(2)}, u32[]{:S(2)}) collective-permute-start(bf16[5,4,2304]{2,1,0:T(4,128)(2,1)S(1)} %get-tuple-element.72), channel_id=1, source_target_pairs={{0,8},{8,16},{16,24},{24,0},{1,9},{9,17},{17,25},{25,1},{2,10},{10... | collective-permute-start | bytes 276488 | tf_op jit(solution)/shard_map/ppermute | solution.py:22
  49.4 8.4 %collective-permute-start.14 = (bf16[5,4,2304]{2,1,0:T(4,128)(2,1)S(1)}, bf16[5,4,2304]{2,1,0:T(4,128)(2,1)S(1)}, u32[]{:S(2)}, u32[]{:S(2)}) collective-permute-start(bf16[5,4,2304]{2,1,0:T(4,128)(2,1)S(1)} %get-tuple-element.73), channel_id=1, source_target_pairs={{0,24},{8,0},{16,8},{24,16},{1,25},{9,1},{17,9},{25,17},{2,26},{10... | collective-permute-start | bytes 276488 | tf_op jit(solution)/shard_map/ppermute | solution.py:22
  56.1 9.1 %collective-permute-start.20 = (bf16[5,4,512]{2,1,0:T(4,128)(2,1)S(1)}, bf16[5,4,512]{2,1,0:T(4,128)(2,1)S(1)}, u32[]{:S(2)}, u32[]{:S(2)}) collective-permute-start(bf16[5,4,512]{2,1,0:T(4,128)(2,1)S(1)} %get-tuple-element.84), channel_id=1, source_target_pairs={{0,2},{2,4},{4,6},{6,0},{1,3},{3,5},{5,7},{7,1},{8,10},{10,12},{12... | collective-permute-start | bytes 61448 | tf_op jit(solution)/shard_map/ppermute | solution.py:22
  56.1 9.1 %collective-permute-start.21 = (bf16[5,4,512]{2,1,0:T(4,128)(2,1)S(1)}, bf16[5,4,512]{2,1,0:T(4,128)(2,1)S(1)}, u32[]{:S(2)}, u32[]{:S(2)}) collective-permute-start(bf16[5,4,512]{2,1,0:T(4,128)(2,1)S(1)} %get-tuple-element.85), channel_id=1, source_target_pairs={{0,6},{2,0},{4,2},{6,4},{1,7},{3,1},{5,3},{7,5},{8,14},{10,8},{12,... | collective-permute-start | bytes 61448 | tf_op jit(solution)/shard_map/ppermute | solution.py:22
  61.3 5.6 %collective-permute-start.18 = (bf16[5,4,512]{2,1,0:T(4,128)(2,1)S(1)}, bf16[5,4,512]{2,1,0:T(4,128)(2,1)S(1)}, u32[]{:S(2)}, u32[]{:S(2)}) collective-permute-start(bf16[5,4,512]{2,1,0:T(4,128)(2,1)S(1)} %get-tuple-element.82), channel_id=1, source_target_pairs={{0,8},{8,16},{16,24},{24,0},{1,9},{9,17},{17,25},{25,1},{2,10},{10... | collective-permute-start | bytes 61448 | tf_op jit(solution)/shard_map/ppermute | solution.py:22
  61.5 5.4 %collective-permute-start.19 = (bf16[5,4,512]{2,1,0:T(4,128)(2,1)S(1)}, bf16[5,4,512]{2,1,0:T(4,128)(2,1)S(1)}, u32[]{:S(2)}, u32[]{:S(2)}) collective-permute-start(bf16[5,4,512]{2,1,0:T(4,128)(2,1)S(1)} %get-tuple-element.83), channel_id=1, source_target_pairs={{0,24},{8,0},{16,8},{24,16},{1,25},{9,1},{17,9},{25,17},{2,26},{10... | collective-permute-start | bytes 61448 | tf_op jit(solution)/shard_map/ppermute | solution.py:22

commit v3 on v0

v3 whole, which is shorter than its diff:
```python
import functools

import jax
import jax.numpy as jnp
from jax import lax
from jax.experimental import pallas as pl
from jax.experimental.pallas import tpu as pltpu
from jax.sharding import PartitionSpec as P


ROUNDS = 2
step_size = 0.2
epsilon = 1e-06

BF16 = jnp.bfloat16
F32 = jnp.float32
MIB = 1024 * 1024


def passed_along(value, axis, by):
    devices = lax.axis_size(axis)
    return lax.ppermute(value, axis, [(i, (i + by) % devices) for i in range(devices)])


def from_partners(value, axis):
    return [passed_along(value, axis, by) for by in range(1, lax.axis_size(axis))]


def call(kernel, outs, args, arg_spaces, scratch=(), limit=16, flops=1_000_000):
    return pl.pallas_call(
        kernel,
        out_shape=[jax.ShapeDtypeStruct(shape, dtype) for shape, dtype, _ in outs],
        in_specs=[pl.BlockSpec(memory_space=space) for space in arg_spaces],
        out_specs=[pl.BlockSpec(memory_space=space) for _, _, space in outs],
        scratch_shapes=list(scratch),
        compiler_params=pltpu.CompilerParams(vmem_limit_bytes=limit * MIB),
        cost_estimate=pl.CostEstimate(flops=flops, bytes_accessed=0, transcendentals=0),
    )(*args)


def rows_by_features(left, right):
    return lax.dot_general(left, right, (((1,), (1,)), ((), ())), preferred_element_type=F32)


def layer_of(w_refs, l):
    for ref in w_refs:
        if l < ref.shape[0]:
            return ref, l
        l -= ref.shape[0]


def within_layers(mixing, pair):
    rows, cols = mixing.shape
    row = lax.broadcasted_iota(jnp.int32, (rows, cols), 0)
    col = lax.broadcasted_iota(jnp.int32, (rows, cols), 1)
    stack = cols // 2
    row = jnp.where(row < stack, row, row - stack) // pair
    col = jnp.where(col < stack, col, col - stack) // pair
    return jnp.where(row == col, -step_size * mixing, 0.0)


def small_times(small, wide):
    high = small.astype(BF16)
    low = (small - high.astype(F32)).astype(BF16)
    both = jnp.dot(jnp.concatenate([high, low], axis=0), wide, preferred_element_type=F32)
    return both[: small.shape[0]] + both[small.shape[0] :]


def load_kernel(w_hbm, down_hbm, right_hbm, w_ref, down_ref, right_ref, sems):
    copies = [
        pltpu.make_async_copy(down_hbm, down_ref, sems.at[0]),
        pltpu.make_async_copy(right_hbm, right_ref, sems.at[1]),
    ]
    for l in range(w_ref.shape[0]):
        copies.append(pltpu.make_async_copy(w_hbm.at[l], w_ref.at[l], sems.at[2 + l]))
    for copy in copies:
        copy.start()
    for copy in copies:
        copy.wait()


def load_more_kernel(start, w_hbm, w_ref, sems):
    copies = [
        pltpu.make_async_copy(w_hbm.at[start + l], w_ref.at[l], sems.at[l])
        for l in range(w_ref.shape[0])
    ]
    for copy in copies:
        copy.start()
    for copy in copies:
        copy.wait()


def store_products(l, row, col, row_keep, up_send, down_send, col_keep, col_send):
    rank = row.shape[0] // 2
    row_keep[l] = row
    up_send[l] = row[:rank].astype(BF16)
    down_send[l] = row[rank:].astype(BF16)
    col_keep[l] = col
    col_send[l] = col.astype(BF16)


def first_products_kernel(w_hbm, w_a, w_b, up_ref, down_ref, left_ref, right_ref, *refs):
    w_c, *outs, sems = refs
    early, late = w_a.shape[0] + w_b.shape[0], w_c.shape[0]
    copies = [
        pltpu.make_async_copy(w_hbm.at[early + l], w_c.at[l], sems.at[l]) for l in range(late)
    ]
    for copy in copies:
        copy.start()
    for l in range(early + late):
        if l >= early:
            copies[l - early].wait()
        ref, at = layer_of((w_a, w_b, w_c), l)
        factors = jnp.concatenate([up_ref[l], down_ref[l], left_ref[l], right_ref[l]], axis=0)
        products = rows_by_features(factors, ref[at])
        half = products.shape[0] // 2
        store_products(l, products[:half], products[half:], *outs)


def middle_col_kernel(partners, col_keep, *refs):
    received, (col_total, left_send, right_send) = refs[:partners], refs[partners:]
    rank = left_send.shape[1]
    for l in range(col_keep.shape[0]):
        col = col_keep[l]
        for other in received:
            col = col + other[l].astype(F32)
        col_total[l] = col
        left_send[l] = col[:rank].astype(BF16)
        right_send[l] = col[rank:].astype(BF16)


def middle_row_kernel(row_keep, from_above, from_below, row_diff, row_send):
    for l in range(row_keep.shape[0]):
        row = row_keep[l] - jnp.concatenate([from_above[l], from_below[l]], axis=0).astype(F32)
        row_diff[l] = row
        row_send[l] = row.astype(BF16)


def lane_sum(parts):
    total = parts[0]
    for part in parts[1:]:
        total = total + part
    return jnp.sum(total, axis=1, keepdims=True)


def orthonormal(v_ref, rank):
    tiles, stack, _ = v_ref.shape
    groups = stack // rank

    def vector(k):
        return [v_ref[t, pl.ds(k, groups, stride=rank), :] for t in range(tiles)]

    rest = [vector(k) for k in range(rank)]
    for k in range(rank):
        u = rest[k]
        square = lane_sum([x * x for x in u]) + epsilon
        for j in range(k + 1, rank):
            along = lane_sum([x * y for x, y in zip(vector(j), u)]) / square
            rest[j] = [x - along * y for x, y in zip(rest[j], u)]
        scale = 1.0 / jnp.sqrt(square)
        rest[k] = [x * scale for x in u]
    for k in range(rank):
        for t in range(tiles):
            v_ref[t, pl.ds(k, groups, stride=rank), :] = rest[k][t]


def store_vectors(v_ref, rows, values):
    for t in range(v_ref.shape[0]):
        v_ref[t, rows, :] = values[:, 128 * t : 128 * (t + 1)]


def back_products(v_ref, w_refs, pairs, basis_ref, back_ref, sends, layers):
    tiles, stack, _ = v_ref.shape
    pair = stack // layers
    rank = pair // 2
    orthonormal(v_ref, rank)
    basis = jnp.concatenate([v_ref[t] for t in range(tiles)], axis=1)
    basis_ref[...] = basis.astype(BF16)
    changes = None
    for old_basis, old_factors in pairs:
        mixing = within_layers(rows_by_features(basis.astype(BF16), old_basis[...]), pair)
        change = small_times(mixing, old_factors[...])
        changes = change if changes is None else changes + change
    for l in range(layers):
        here = slice(l * pair, (l + 1) * pair)
        ref, at = layer_of(w_refs, l)
        back = jnp.dot(basis[here].astype(BF16), ref[at], preferred_element_type=F32)
        if changes is not None:
            back = back + changes[here]
        back_ref[here, :] = back
        for i, send in enumerate(sends):
            send[l] = back[rank * i : rank * i + rank].astype(BF16)


def back_col_kernel(earlier, w_a, w_b, w_c, col_total, from_left, from_right, *refs):
    pairs, refs = refs[: 2 * earlier], refs[2 * earlier :]
    basis_ref, back_ref, *sends, v_ref = refs
    layers, pair, _ = col_total.shape
    for l in range(layers):
        theirs = jnp.concatenate([from_left[l], from_right[l]], axis=0).astype(F32)
        store_vectors(v_ref, slice(l * pair, (l + 1) * pair), col_total[l] - theirs)
    pairs = list(zip(pairs[::2], pairs[1::2]))
    back_products(v_ref, (w_a, w_b, w_c), pairs, basis_ref, back_ref, sends, layers)


def back_row_kernel(partners, earlier, w_a, w_b, w_c, row_diff, *refs):
    received, refs = refs[:partners], refs[partners:]
    pairs, refs = refs[: 2 * earlier], refs[2 * earlier :]
    basis_ref, back_ref, *sends, v_ref = refs
    layers, pair, _ = row_diff.shape
    for l in range(layers):
        row = row_diff[l]
        for other in received:
            row = row + other[l].astype(F32)
        store_vectors(v_ref, slice(l * pair, (l + 1) * pair), row)
    pairs = list(zip(pairs[::2], pairs[1::2]))
    back_products(v_ref, (w_a, w_b, w_c), pairs, basis_ref, back_ref, sends, layers)


def combined_of(l, back_ref, first, second):
    pair = 2 * first.shape[1]
    theirs = jnp.concatenate([first[l], second[l]], axis=0)
    return back_ref[l * pair : (l + 1) * pair, :] + theirs.astype(F32)


def next_products_kernel(earlier, w_a, w_b, w_c, *refs):
    (row_back, col_back, above, below, left, right), refs = refs[:6], refs[6:]
    pairs, refs = refs[: 2 * earlier], refs[2 * earlier :]
    row_basis, col_basis, bases_ref, factors_ref, *outs, f_ref = refs
    layers, rank, _ = above.shape
    pair, stack = 2 * rank, row_basis.shape[0]
    bases_ref[:stack, :] = row_basis[...]
    bases_ref[stack:, :] = col_basis[...]
    for l in range(layers):
        f_ref[l * pair : (l + 1) * pair, :] = combined_of(l, row_back, above, below)
        f_ref[stack + l * pair : stack + (l + 1) * pair, :] = combined_of(l, col_back, left, right)
    factors = f_ref[...].astype(BF16)
    factors_ref[...] = factors
    known = list(zip(pairs[::2], pairs[1::2])) + [(bases_ref, factors_ref)]
    changes = None
    for old_basis, old_factors in known:
        mixing = within_layers(rows_by_features(factors, old_factors[...]), pair)
        change = small_times(mixing, old_basis[...])
        changes = change if changes is None else changes + change
    for l in range(layers):
        row_at = slice(l * pair, (l + 1) * pair)
        col_at = slice(stack + l * pair, stack + (l + 1) * pair)
        own = jnp.concatenate([f_ref[row_at, :], f_ref[col_at, :]], axis=0).astype(BF16)
        ref, at = layer_of((w_a, w_b, w_c), l)
        products = rows_by_features(own, ref[at])
        store_products(
            l, products[:pair] + changes[row_at], products[pair:] + changes[col_at], *outs
        )


def finish_kernel(earlier, chunk, w_a, w_b, w_c, *refs):
    (row_back, col_back, above, below, left, right), refs = refs[:6], refs[6:]
    pairs, refs = refs[: 2 * earlier], refs[2 * earlier :]
    row_basis, col_basis, w_out, down_out, right_out, staged, sems = refs
    layers, depth, _ = staged.shape
    rank, stack = above.shape[1], row_basis.shape[0]
    pair = 2 * rank
    copies = []
    for l in range(layers):
        row_at = slice(l * pair, (l + 1) * pair)
        col_at = slice(stack + l * pair, stack + (l + 1) * pair)
        row = combined_of(l, row_back, above, below)
        col = combined_of(l, col_back, left, right)
        down_out[l] = row[rank:]
        right_out[l] = col[rank:]
        old = [f[at, :] for f in pairs[1::2] for at in (row_at, col_at)]
        factors = jnp.concatenate(old + [row.astype(BF16), col.astype(BF16)], axis=0)
        ref, at = layer_of((w_a, w_b, w_c), l)
        for c in range(depth // chunk):
            part = slice(c * chunk, (c + 1) * chunk)
            old = [b[rows, part] for b in pairs[::2] for rows in (row_at, col_at)]
            basis = jnp.concatenate(
                old + [row_basis[row_at, part], col_basis[row_at, part]], axis=0
            )
            correction = lax.dot_general(
                basis, factors, (((0,), (0,)), ((), ())), preferred_element_type=F32
            )
            staged[l, part] = (ref[at, part].astype(F32) - step_size * correction).astype(BF16)
            copy = pltpu.make_async_copy(staged.at[l, part], w_out.at[l, part], sems.at[l, c])
            copy.start()
            copies.append(copy)
    for copy in copies:
        copy.wait()


def body(weights, warm_down, warm_right):
    vmem, hbm = pltpu.VMEM, pltpu.HBM
    w_hbm, down_hbm, right_hbm = (
        pltpu.with_memory_space_constraint(x[0, 0], hbm) for x in (weights, warm_down, warm_right)
    )
    count, depth, width = w_hbm.shape
    rank = down_hbm.shape[1]
    partners = lax.axis_size("mp") - 1
    pair, stack = 2 * rank, 2 * rank * count
    dma = pltpu.SemaphoreType.DMA

    def local(kernel, outs, args, **more):
        return call(kernel, outs, args, [vmem] * len(args), **more)

    kept = ((count, pair, depth), F32, vmem)
    both_edges = ((count, pair, depth), BF16, vmem)
    one_edge = ((count, rank, depth), BF16, vmem)
    product_outs = [kept, one_edge, one_edge, kept, both_edges]
    own_factors = ((count, rank, width), BF16, vmem)
    back_outs = [((stack, depth), BF16, vmem), ((stack, width), F32, vmem), own_factors, own_factors]
    vectors = [pltpu.VMEM((depth // 128, stack, 128), F32)]

    some, more = max(1, count // 5), max(1, 2 * count // 5)
    w_a, own_down, own_right = call(
        load_kernel,
        [((some, depth, width), BF16, vmem), own_factors, own_factors],
        (w_hbm, down_hbm, right_hbm),
        [hbm] * 3,
        scratch=[dma((some + 2,))],
    )
    above = passed_along(own_down, "row", 1)
    beside = passed_along(own_right, "col", 1)
    (w_b,) = call(
        functools.partial(load_more_kernel, some),
        [((more, depth, width), BF16, vmem)],
        (w_hbm,),
        [hbm],
        scratch=[dma((more,))],
        flops=100_000_000,
    )
    rest = count - some - more
    w_c, *products = call(
        first_products_kernel,
        [((rest, depth, width), BF16, vmem)] + product_outs,
        (w_hbm, w_a, w_b, above, own_down, beside, own_right),
        [hbm] + [vmem] * 6,
        scratch=[dma((rest,))],
    )
    w = (w_a, w_b, w_c)
    pairs = ()
    for repeat in range(ROUNDS):
        row_keep, up_send, down_send, col_keep, col_send = products
        col_received = from_partners(col_send, "mp")
        from_above = passed_along(down_send, "row", 1)
        from_below = passed_along(up_send, "row", -1)
        col_total, left_send, right_send = local(
            functools.partial(middle_col_kernel, partners),
            [kept, one_edge, one_edge],
            (col_keep, *col_received),
        )
        from_left = passed_along(right_send, "col", 1)
        from_right = passed_along(left_send, "col", -1)
        row_diff, row_send = local(
            middle_row_kernel, [kept, both_edges], (row_keep, from_above, from_below)
        )
        row_received = from_partners(row_send, "mp")
        col_basis, col_back, left_send, right_send = local(
            functools.partial(back_col_kernel, repeat),
            back_outs,
            (*w, col_total, from_left, from_right, *pairs),
            scratch=vectors,
        )
        from_left = passed_along(right_send, "col", 1)
        from_right = passed_along(left_send, "col", -1)
        row_basis, row_back, up_send, down_send = local(
            functools.partial(back_row_kernel, partners, repeat),
            back_outs,
            (*w, row_diff, *row_received, *pairs),
            scratch=vectors,
        )
        from_above = passed_along(down_send, "row", 1)
        from_below = passed_along(up_send, "row", -1)
        moved = (row_back, col_back, from_above, from_below, from_left, from_right)
        args = (*w, *moved, *pairs, row_basis, col_basis)
        if repeat + 1 < ROUNDS:
            bases, factors, *products = local(
                functools.partial(next_products_kernel, repeat),
                [((2 * stack, depth), BF16, vmem), ((2 * stack, width), BF16, vmem)] + product_outs,
                args,
                scratch=[pltpu.VMEM((2 * stack, width), F32)],
            )
            pairs = (*pairs, bases, factors)
    chunk = depth // 3 if depth % 384 == 0 else depth
    new_w, next_down, next_right = local(
        functools.partial(finish_kernel, ROUNDS - 1, chunk),
        [
            ((count, depth, width), BF16, hbm),
            ((count, rank, width), F32, vmem),
            ((count, rank, width), F32, vmem),
        ],
        args,
        scratch=[pltpu.VMEM((count, depth, width), BF16), dma((count, depth // chunk))],
        limit=28,
    )
    return new_w[None, None], next_down[None, None], next_right[None, None]


def solution(mesh):
    placed = (P("row", "col", None, None, "mp"),) * 3
    return jax.shard_map(body, mesh=mesh, in_specs=placed, out_specs=placed, check_vma=False)
```

time: 181 us -> 75.6 us (0.42)
  waiting for transfers between devices: 84.3 us -> 15.3 us
  matrix products: 42.7 us -> 0 us
  Pallas kernels: 0 us -> 26.3 us
  between operations: 14.2 us -> 0.88 us
  other arithmetic: 11.7 us -> 0 us
  starting transfers between devices: 20.7 us -> 32 us
  local copies, waits for them, and re-layouts: 7.13 us -> 0 us
    psum x2 -> x0, waiting for transfers between devices: 65.5 us -> none  [gossip_round(): totals = lax.psum(partial_rows, 'mp')]
    dot_general x6 -> x0, matrix products: 42.7 us -> none  [the longest x2 17.9 us: gossip_round(): jnp.einsum('lsd,lsk->ldk', flat_basis, flat_factors, preferred_element_ty...]
    pallas_call x0 -> x13, Pallas kernels: none -> 26.3 us  [call(): pl.pallas_call(kernel, out_shape=[jax.ShapeDtypeStruct(shape, dtype) for...]
    ppermute x18 -> x22, starting transfers between devices: 20.6 us -> 32 us  [passed_along(): lax.ppermute(value, axis, [(i, (i + by) % devices) for i in range(devices)])]
    ppermute x18 -> x22, waiting for transfers between devices: 18.8 us -> 15.3 us  [passed_along(): lax.ppermute(value, axis, [(i, (i + by) % devices) for i in range(devices)])]
    reduce_sum x14 -> x0, other arithmetic: 3.45 us -> none  [the longest x8 2.08 us: orthonormal(): jnp.sum(source * earlier, axis=-1, keepdims=True) * earlier]
    div x2 -> x0, other arithmetic: 3.42 us -> none  [orthonormal(): update / jnp.sqrt(jnp.sum(update * update, axis=-1, keepdims=True) + epsi...]
    convert_element_type x6 -> x0, local copies, waits for them, and re-layouts: 2.76 us -> none  [the longest x4 2.59 us: neighbours(): payload[:, 1].astype(jnp.bfloat16)]
  transfers between devices with their start and end apart: 20 -> 22, of which waited for: 15 -> 10; matrix products, arithmetic and copies ran while one was open for 2% -> 0% of each run, Pallas kernels for 0% -> 16%
where the time goes in v3:
time: 75.6 us; the launch traced here: 74.4 us
  starting transfers between devices  32 us (42%)
  Pallas kernels  26.3 us (35%)
  waiting for transfers between devices  15.3 us (20%)
  between operations  0.88 us (1%)
    ppermute x22, starting transfers between devices, passed_along(): lax.ppermute(value, axis, [(i, (i + by) % devices) for i in range(devices)])  32 us
    pallas_call x13, Pallas kernels, call(): pl.pallas_call(kernel, out_shape=[jax.ShapeDtypeStruct(shape, dtype) for...  26.3 us
    ppermute x22, waiting for transfers between devices, passed_along(): lax.ppermute(value, axis, [(i, (i + by) % devices) for i in range(devices)])  15.3 us
  transfers between devices with their start and end apart: 22, of which 10 were waited for; matrix products, arithmetic and copies ran while one was open for 0% of the time, Pallas kernels for 16%

profile of v3, /device:TPU:0, one launch (start us, length us, event | category | flops | bytes accessed | tf_op | source)
XLA Modules:
  0.0 74.4 jit_solution(13870122169614344509)
XLA Ops:
  0.6 1.7 %shard_map.58 = (bf16[1,2304,512]{2,1,0:T(8,128)(2,1)S(1)}, bf16[5,4,512]{2,1,0:T(4,128)(2,1)S(1)}, bf16[5,4,512]{2,1,0:T(4,128)(2,1)S(1)}) custom-call(bf16[5,2304,512]{2,1,0:T(8,128)(2,1)} %bitcast.6, bf16[5,4,512]{2,1,0:T(4,128)(2,1)} %bitcast.9, bf16[5,4,512]{2,1,0:T(4,128)(2,1)} %bitcast.10), custom_call_target="tpu_custom_call" | custom-call | flops 1000000 | tf_op jit(solution)/shard_map/pallas_call | solution.py:30
  2.4 3.1 %collective-permute-start = (bf16[5,4,512]{2,1,0:T(4,128)(2,1)S(1)}, bf16[5,4,512]{2,1,0:T(4,128)(2,1)S(1)}, u32[]{:S(2)}, u32[]{:S(2)}) collective-permute-start(bf16[5,4,512]{2,1,0:T(4,128)(2,1)S(1)} %get-tuple-element.49.down_ref), channel_id=1, source_target_pairs={{0,8},{8,16},{16,24},{24,0},{1,9},{9,17},{17,25},{25,1},{2,10},{10... | collective-permute-start | bytes 61448 | tf_op jit(solution)/shard_map/ppermute | solution.py:22
  5.5 0.0 collective-permute-start.1
  5.5 2.4 %shard_map.59.w_b = bf16[2,2304,512]{2,1,0:T(8,128)(2,1)S(1)} custom-call(bf16[5,2304,512]{2,1,0:T(8,128)(2,1)} %bitcast.7), custom_call_target="tpu_custom_call" | custom-call | flops 100000000 | tf_op jit(solution)/shard_map/pallas_call | solution.py:30
  7.9 1.4 %collective-permute-done.up_ref = bf16[5,4,512]{2,1,0:T(4,128)(2,1)S(1)} collective-permute-done((bf16[5,4,512]{2,1,0:T(4,128)(2,1)S(1)}, bf16[5,4,512]{2,1,0:T(4,128)(2,1)S(1)}, u32[]{:S(2)}, u32[]{:S(2)}) %collective-permute-start) | collective-permute-done | bytes 20512 | tf_op jit(solution)/shard_map/ppermute | solution.py:22
  9.3 0.0 collective-permute-done.1.left_ref
  9.3 3.6 %shard_map.60 = (bf16[2,2304,512]{2,1,0:T(8,128)(2,1)S(1)}, f32[5,8,2304]{2,1,0:T(8,128)S(1)}, bf16[5,4,2304]{2,1,0:T(4,128)(2,1)S(1)}, bf16[5,4,2304]{2,1,0:T(4...) custom-call(bf16[5,2304,512]{2,1,0:T(8,128)(2,1)} %bitcast.8, ...), custom_call_target="tpu_custom_call" | custom-call | flops 1000000 | tf_op jit(solution)/shard_map/pallas_call | solution.py:30
  12.8 1.0 %collective-permute-start.2 = (bf16[5,4,2304]{2,1,0:T(4,128)(2,1)S(1)}, bf16[5,4,2304]{2,1,0:T(4,128)(2,1)S(1)}, u32[]{:S(2)}, u32[]{:S(2)}) collective-permute-start(bf16[5,4,2304]{2,1,0:T(4,128)(2,1)S(1)} %get-tuple-element.53), channel_id=1, source_target_pairs={{0,8},{8,16},{16,24},{24,0},{1,9},{9,17},{17,25},{25,1},{2,10},{10... | collective-permute-start | bytes 276488 | tf_op jit(solution)/shard_map/ppermute | solution.py:22
  13.9 2.8 %collective-permute-start.3 = (bf16[5,4,2304]{2,1,0:T(4,128)(2,1)S(1)}, bf16[5,4,2304]{2,1,0:T(4,128)(2,1)S(1)}, u32[]{:S(2)}, u32[]{:S(2)}) collective-permute-start(bf16[5,4,2304]{2,1,0:T(4,128)(2,1)S(1)} %get-tuple-element.54), channel_id=1, source_target_pairs={{0,24},{8,0},{16,8},{24,16},{1,25},{9,1},{17,9},{25,17},{2,26},{10... | collective-permute-start | bytes 276488 | tf_op jit(solution)/shard_map/ppermute | solution.py:22
  16.7 1.7 %collective-permute-start.5 = (bf16[5,8,2304]{2,1,0:T(8,128)(2,1)S(1)}, bf16[5,8,2304]{2,1,0:T(8,128)(2,1)S(1)}, u32[]{:S(2)}, u32[]{:S(2)}) collective-permute-start(bf16[5,8,2304]{2,1,0:T(8,128)(2,1)S(1)} %get-tuple-element.59), channel_id=1, source_target_pairs={{0,1},{1,0},{2,3},{3,2},{4,5},{5,4},{6,7},{7,6},{8,9},{9,8},{10,11... | collective-permute-start | bytes 552968 | tf_op jit(solution)/shard_map/ppermute | solution.py:22
  18.5 1.8 %collective-permute-done.2.from_above = bf16[5,4,2304]{2,1,0:T(4,128)(2,1)S(1)} collective-permute-done((bf16[5,4,2304]{2,1,0:T(4,128)(2,1)S(1)}, bf16[5,4,2304]{2,1,0:T(4,128)(2,1)S(1)}, u32[]{:S(2)}, u32[]{:S(2)}) %collective-permute-start.2) | collective-permute-done | bytes 92192 | tf_op jit(solution)/shard_map/ppermute | solution.py:22
  20.2 0.7 collective-permute-done.3.from_below
  21.0 0.1 shard_map.61
  21.1 1.6 %collective-permute-start.4 = (bf16[5,8,2304]{2,1,0:T(8,128)(2,1)S(1)}, bf16[5,8,2304]{2,1,0:T(8,128)(2,1)S(1)}, u32[]{:S(2)}, u32[]{:S(2)}) collective-permute-start(bf16[5,8,2304]{2,1,0:T(8,128)(2,1)S(1)} %get-tuple-element.56), channel_id=1, source_target_pairs={{0,1},{1,0},{2,3},{3,2},{4,5},{5,4},{6,7},{7,6},{8,9},{9,8},{10,11... | collective-permute-start | bytes 552968 | tf_op jit(solution)/shard_map/ppermute | solution.py:22
  22.6 0.3 collective-permute-done.5.refs_0_
  22.9 0.1 shard_map.63
  23.0 0.1 collective-permute-start.6
  23.1 1.7 %collective-permute-start.7 = (bf16[5,4,2304]{2,1,0:T(4,128)(2,1)S(1)}, bf16[5,4,2304]{2,1,0:T(4,128)(2,1)S(1)}, u32[]{:S(2)}, u32[]{:S(2)}) collective-permute-start(bf16[5,4,2304]{2,1,0:T(4,128)(2,1)S(1)} %get-tuple-element.62), channel_id=1, source_target_pairs={{0,6},{2,0},{4,2},{6,4},{1,7},{3,1},{5,3},{7,5},{8,14},{10,8},{12,... | collective-permute-start | bytes 276488 | tf_op jit(solution)/shard_map/ppermute | solution.py:22
  24.8 2.6 %collective-permute-done.4.refs_0_ = bf16[5,8,2304]{2,1,0:T(8,128)(2,1)S(1)} collective-permute-done((bf16[5,8,2304]{2,1,0:T(8,128)(2,1)S(1)}, bf16[5,8,2304]{2,1,0:T(8,128)(2,1)S(1)}, u32[]{:S(2)}, u32[]{:S(2)}) %collective-permute-start.4) | collective-permute-done | bytes 184352 | tf_op jit(solution)/shard_map/ppermute | solution.py:22
  27.4 2.1 %shard_map.62 = (bf16[40,2304]{1,0:T(8,128)(2,1)S(1)}, f32[40,512]{1,0:T(8,128)S(1)}, bf16[5,4,512]{2,1,0:T(4,128)(2,1)S(1)}, bf16[5,4,512]{2,1,0:T(4,128)(2,1)S(1)}) custom-call(bf16[1,2304,512]{2,1,0:T(8,128)(2,1)S(1)} %get-tuple-element.48.w_a, bf16[2,2304,512]{2,1,0:T(8,128)(2,1)S(1)} %shard_map.59.w_b, bf16[2,2304,512]{2,1,0:T(8,128)(2,1)S(1)} %get-tuple-element.51.w_c, ...), custom_call_target="tpu_custom_call" | custom-call | flops 1000000 | tf_op jit(solution)/shard_map/pallas_call | solution.py:30
  29.5 1.5 %collective-permute-start.8 = (bf16[5,4,512]{2,1,0:T(4,128)(2,1)S(1)}, bf16[5,4,512]{2,1,0:T(4,128)(2,1)S(1)}, u32[]{:S(2)}, u32[]{:S(2)}) collective-permute-start(bf16[5,4,512]{2,1,0:T(4,128)(2,1)S(1)} %get-tuple-element.64), channel_id=1, source_target_pairs={{0,8},{8,16},{16,24},{24,0},{1,9},{9,17},{17,25},{25,1},{2,10},{10... | collective-permute-start | bytes 61448 | tf_op jit(solution)/shard_map/ppermute | solution.py:22
  30.9 2.4 %collective-permute-start.9 = (bf16[5,4,512]{2,1,0:T(4,128)(2,1)S(1)}, bf16[5,4,512]{2,1,0:T(4,128)(2,1)S(1)}, u32[]{:S(2)}, u32[]{:S(2)}) collective-permute-start(bf16[5,4,512]{2,1,0:T(4,128)(2,1)S(1)} %get-tuple-element.65), channel_id=1, source_target_pairs={{0,24},{8,0},{16,8},{24,16},{1,25},{9,1},{17,9},{25,17},{2,26},{10... | collective-permute-start | bytes 61448 | tf_op jit(solution)/shard_map/ppermute | solution.py:22
  33.3 0.0 collective-permute-done.6.from_left
  33.3 2.1 %shard_map.64 = (bf16[40,2304]{1,0:T(8,128)(2,1)S(1)}, f32[40,512]{1,0:T(8,128)S(1)}, bf16[5,4,512]{2,1,0:T(4,128)(2,1)S(1)}, bf16[5,4,512]{2,1,0:T(4,128)(2,1)S(1)}) custom-call(bf16[1,2304,512]{2,1,0:T(8,128)(2,1)S(1)} %get-tuple-element.48.w_a, bf16[2,2304,512]{2,1,0:T(8,128)(2,1)S(1)} %shard_map.59.w_b, bf16[2,2304,512]{2,1,0:T(8,128)(2,1)S(1)} %get-tuple-element.51.w_c, ...), custom_call_target="tpu_custom_call" | custom-call | flops 1000000 | tf_op jit(solution)/shard_map/pallas_call | solution.py:30
  35.4 0.0 collective-permute-start.10
  35.4 1.8 %collective-permute-start.11 = (bf16[5,4,512]{2,1,0:T(4,128)(2,1)S(1)}, bf16[5,4,512]{2,1,0:T(4,128)(2,1)S(1)}, u32[]{:S(2)}, u32[]{:S(2)}) collective-permute-start(bf16[5,4,512]{2,1,0:T(4,128)(2,1)S(1)} %get-tuple-element.67), channel_id=1, source_target_pairs={{0,6},{2,0},{4,2},{6,4},{1,7},{3,1},{5,3},{7,5},{8,14},{10,8},{12,... | collective-permute-start | bytes 61448 | tf_op jit(solution)/shard_map/ppermute | solution.py:22
  37.2 1.5 %collective-permute-done.10.refs_4_ = bf16[5,4,512]{2,1,0:T(4,128)(2,1)S(1)} collective-permute-done((bf16[5,4,512]{2,1,0:T(4,128)(2,1)S(1)}, bf16[5,4,512]{2,1,0:T(4,128)(2,1)S(1)}, u32[]{:S(2)}, u32[]{:S(2)}) %collective-permute-start.10) | collective-permute-done | bytes 20512 | tf_op jit(solution)/shard_map/ppermute | solution.py:22
  38.7 0.0 collective-permute-done.11.refs_5_
  38.7 3.5 %shard_map.65 = (bf16[80,2304]{1,0:T(8,128)(2,1)S(1)}, bf16[80,512]{1,0:T(8,128)(2,1)S(1)}, f32[5,8,2304]{2,1,0:T(8,128)S(1)}, bf16[5,4,2304]{2,1,0:T(4,128)(2,1...) custom-call(bf16[1,2304,512]{2,1,0:T(8,128)(2,1)S(1)} %get-tuple-element.48.w_a, ...), custom_call_target="tpu_custom_call" | custom-call | flops 1000000 | tf_op jit(solution)/shard_map/pallas_call | solution.py:30
  42.2 0.0 collective-permute-start.12
  42.2 3.8 %collective-permute-start.13 = (bf16[5,4,2304]{2,1,0:T(4,128)(2,1)S(1)}, bf16[5,4,2304]{2,1,0:T(4,128)(2,1)S(1)}, u32[]{:S(2)}, u32[]{:S(2)}) collective-permute-start(bf16[5,4,2304]{2,1,0:T(4,128)(2,1)S(1)} %get-tuple-element.72), channel_id=1, source_target_pairs={{0,24},{8,0},{16,8},{24,16},{1,25},{9,1},{17,9},{25,17},{2,26},{10... | collective-permute-start | bytes 276488 | tf_op jit(solution)/shard_map/ppermute | solution.py:22
  46.1 1.5 %collective-permute-start.15 = (bf16[5,8,2304]{2,1,0:T(8,128)(2,1)S(1)}, bf16[5,8,2304]{2,1,0:T(8,128)(2,1)S(1)}, u32[]{:S(2)}, u32[]{:S(2)}) collective-permute-start(bf16[5,8,2304]{2,1,0:T(8,128)(2,1)S(1)} %get-tuple-element.79), channel_id=1, source_target_pairs={{0,1},{1,0},{2,3},{3,2},{4,5},{5,4},{6,7},{7,6},{8,9},{9,8},{10,11... | collective-permute-start | bytes 552968 | tf_op jit(solution)/shard_map/ppermute | solution.py:22
  47.6 2.0 %collective-permute-done.12.from_above = bf16[5,4,2304]{2,1,0:T(4,128)(2,1)S(1)} collective-permute-done((bf16[5,4,2304]{2,1,0:T(4,128)(2,1)S(1)}, bf16[5,4,2304]{2,1,0:T(4,128)(2,1)S(1)}, u32[]{:S(2)}, u32[]{:S(2)}) %collective-permute-start.12) | collective-permute-done | bytes 92192 | tf_op jit(solution)/shard_map/ppermute | solution.py:22
  49.6 0.0 collective-permute-done.13.from_below
  49.6 0.1 shard_map.66
  49.7 1.6 %collective-permute-start.14 = (bf16[5,8,2304]{2,1,0:T(8,128)(2,1)S(1)}, bf16[5,8,2304]{2,1,0:T(8,128)(2,1)S(1)}, u32[]{:S(2)}, u32[]{:S(2)}) collective-permute-start(bf16[5,8,2304]{2,1,0:T(8,128)(2,1)S(1)} %get-tuple-element.74), channel_id=1, source_target_pairs={{0,1},{1,0},{2,3},{3,2},{4,5},{5,4},{6,7},{7,6},{8,9},{9,8},{10,11... | collective-permute-start | bytes 552968 | tf_op jit(solution)/shard_map/ppermute | solution.py:22
  51.2 2.3 %collective-permute-done.15.refs_0_ = bf16[5,8,2304]{2,1,0:T(8,128)(2,1)S(1)} collective-permute-done((bf16[5,8,2304]{2,1,0:T(8,128)(2,1)S(1)}, bf16[5,8,2304]{2,1,0:T(8,128)(2,1)S(1)}, u32[]{:S(2)}, u32[]{:S(2)}) %collective-permute-start.15) | collective-permute-done | bytes 184352 | tf_op jit(solution)/shard_map/ppermute | solution.py:22
  53.6 0.1 shard_map.68
  53.6 0.1 collective-permute-start.16
  53.7 1.7 %collective-permute-start.17 = (bf16[5,4,2304]{2,1,0:T(4,128)(2,1)S(1)}, bf16[5,4,2304]{2,1,0:T(4,128)(2,1)S(1)}, u32[]{:S(2)}, u32[]{:S(2)}) collective-permute-start(bf16[5,4,2304]{2,1,0:T(4,128)(2,1)S(1)} %get-tuple-element.82), channel_id=1, source_target_pairs={{0,6},{2,0},{4,2},{6,4},{1,7},{3,1},{5,3},{7,5},{8,14},{10,8},{12,... | collective-permute-start | bytes 276488 | tf_op jit(solution)/shard_map/ppermute | solution.py:22
  55.4 1.2 %collective-permute-done.14.refs_0_ = bf16[5,8,2304]{2,1,0:T(8,128)(2,1)S(1)} collective-permute-done((bf16[5,8,2304]{2,1,0:T(8,128)(2,1)S(1)}, bf16[5,8,2304]{2,1,0:T(8,128)(2,1)S(1)}, u32[]{:S(2)}, u32[]{:S(2)}) %collective-permute-start.14) | collective-permute-done | bytes 184352 | tf_op jit(solution)/shard_map/ppermute | solution.py:22
  56.6 2.5 %shard_map.67 = (bf16[40,2304]{1,0:T(8,128)(2,1)S(1)}, f32[40,512]{1,0:T(8,128)S(1)}, bf16[5,4,512]{2,1,0:T(4,128)(2,1)S(1)}, bf16[5,4,512]{2,1,0:T(4,128)(2,1)S(1)}) custom-call(bf16[1,2304,512]{2,1,0:T(8,128)(2,1)S(1)} %get-tuple-element.48.w_a, bf16[2,2304,512]{2,1,0:T(8,128)(2,1)S(1)} %shard_map.59.w_b, bf16[2,2304,512]{2,1,0:T(8,128)(2,1)S(1)} %get-tuple-element.51.w_c, ...), custom_call_target="tpu_custom_call" | custom-call | flops 1000000 | tf_op jit(solution)/shard_map/pallas_call | solution.py:30
  59.2 3.8 %collective-permute-start.19 = (bf16[5,4,512]{2,1,0:T(4,128)(2,1)S(1)}, bf16[5,4,512]{2,1,0:T(4,128)(2,1)S(1)}, u32[]{:S(2)}, u32[]{:S(2)}) collective-permute-start(bf16[5,4,512]{2,1,0:T(4,128)(2,1)S(1)} %get-tuple-element.85), channel_id=1, source_target_pairs={{0,24},{8,0},{16,8},{24,16},{1,25},{9,1},{17,9},{25,17},{2,26},{10... | collective-permute-start | bytes 61448 | tf_op jit(solution)/shard_map/ppermute | solution.py:22
  63.0 2.6 %shard_map.69 = (bf16[40,2304]{1,0:T(8,128)(2,1)S(1)}, f32[40,512]{1,0:T(8,128)S(1)}, bf16[5,4,512]{2,1,0:T(4,128)(2,1)S(1)}, bf16[5,4,512]{2,1,0:T(4,128)(2,1)S(1)}) custom-call(bf16[1,2304,512]{2,1,0:T(8,128)(2,1)S(1)} %get-tuple-element.48.w_a, bf16[2,2304,512]{2,1,0:T(8,128)(2,1)S(1)} %shard_map.59.w_b, bf16[2,2304,512]{2,1,0:T(8,128)(2,1)S(1)} %get-tuple-element.51.w_c, ...), custom_call_target="tpu_custom_call" | custom-call | flops 1000000 | tf_op jit(solution)/shard_map/pallas_call | solution.py:30
  65.6 1.8 %collective-permute-start.21 = (bf16[5,4,512]{2,1,0:T(4,128)(2,1)S(1)}, bf16[5,4,512]{2,1,0:T(4,128)(2,1)S(1)}, u32[]{:S(2)}, u32[]{:S(2)}) collective-permute-start(bf16[5,4,512]{2,1,0:T(4,128)(2,1)S(1)} %get-tuple-element.87), channel_id=1, source_target_pairs={{0,6},{2,0},{4,2},{6,4},{1,7},{3,1},{5,3},{7,5},{8,14},{10,8},{12,... | collective-permute-start | bytes 61448 | tf_op jit(solution)/shard_map/ppermute | solution.py:22
  67.3 1.5 %collective-permute-done.20.refs_4_ = bf16[5,4,512]{2,1,0:T(4,128)(2,1)S(1)} collective-permute-done((bf16[5,4,512]{2,1,0:T(4,128)(2,1)S(1)}, bf16[5,4,512]{2,1,0:T(4,128)(2,1)S(1)}, u32[]{:S(2)}, u32[]{:S(2)}) %collective-permute-start.20) | collective-permute-done | bytes 20512 | tf_op jit(solution)/shard_map/ppermute | solution.py:22
  68.8 0.0 collective-permute-done.21.refs_5_
  68.8 5.5 %shard_map.70 = (bf16[5,2304,512]{2,1,0:T(8,128)(2,1)}, f32[5,4,512]{2,1,0:T(4,128)}, f32[5,4,512]{2,1,0:T(4,128)}) custom-call(bf16[1,2304,512]{2,1,0:T(8,128)(2,1)S(1)} %get-tuple-element.48.w_a, bf16[2,2304,512]{2,1,0:T(8,128)(2,1)S(1)} %shard_map.59.w_b, bf16[2,2304,512]{2,1,0:T(8,128)(2,1)S(1)} %get-tuple-element.51.w_c, ...), custom_call_target="tpu_custom_call" | custom-call | flops 1000000 | tf_op jit(solution)/shard_map/pallas_call | solution.py:30
  (9 shorter events, 0.0 us)
Async XLA Ops:
  2.4 6.9 %collective-permute-start = (bf16[5,4,512]{2,1,0:T(4,128)(2,1)S(1)}, bf16[5,4,512]{2,1,0:T(4,128)(2,1)S(1)}, u32[]{:S(2)}, u32[]{:S(2)}) collective-permute-start(bf16[5,4,512]{2,1,0:T(4,128)(2,1)S(1)} %get-tuple-element.49.down_ref), channel_id=1, source_target_pairs={{0,8},{8,16},{16,24},{24,0},{1,9},{9,17},{17,25},{25,1},{2,10},{10... | collective-permute-start | bytes 61448 | tf_op jit(solution)/shard_map/ppermute | solution.py:22
  5.5 3.8 %collective-permute-start.1 = (bf16[5,4,512]{2,1,0:T(4,128)(2,1)S(1)}, bf16[5,4,512]{2,1,0:T(4,128)(2,1)S(1)}, u32[]{:S(2)}, u32[]{:S(2)}) collective-permute-start(bf16[5,4,512]{2,1,0:T(4,128)(2,1)S(1)} %get-tuple-element.50.right_ref), channel_id=1, source_target_pairs={{0,2},{2,4},{4,6},{6,0},{1,3},{3,5},{5,7},{7,1},{8,10},{10,12},{12... | collective-permute-start | bytes 61448 | tf_op jit(solution)/shard_map/ppermute | solution.py:22
  12.8 7.4 %collective-permute-start.2 = (bf16[5,4,2304]{2,1,0:T(4,128)(2,1)S(1)}, bf16[5,4,2304]{2,1,0:T(4,128)(2,1)S(1)}, u32[]{:S(2)}, u32[]{:S(2)}) collective-permute-start(bf16[5,4,2304]{2,1,0:T(4,128)(2,1)S(1)} %get-tuple-element.53), channel_id=1, source_target_pairs={{0,8},{8,16},{16,24},{24,0},{1,9},{9,17},{17,25},{25,1},{2,10},{10... | collective-permute-start | bytes 276488 | tf_op jit(solution)/shard_map/ppermute | solution.py:22
  13.9 7.1 %collective-permute-start.3 = (bf16[5,4,2304]{2,1,0:T(4,128)(2,1)S(1)}, bf16[5,4,2304]{2,1,0:T(4,128)(2,1)S(1)}, u32[]{:S(2)}, u32[]{:S(2)}) collective-permute-start(bf16[5,4,2304]{2,1,0:T(4,128)(2,1)S(1)} %get-tuple-element.54), channel_id=1, source_target_pairs={{0,24},{8,0},{16,8},{24,16},{1,25},{9,1},{17,9},{25,17},{2,26},{10... | collective-permute-start | bytes 276488 | tf_op jit(solution)/shard_map/ppermute | solution.py:22
  16.7 6.2 %collective-permute-start.5 = (bf16[5,8,2304]{2,1,0:T(8,128)(2,1)S(1)}, bf16[5,8,2304]{2,1,0:T(8,128)(2,1)S(1)}, u32[]{:S(2)}, u32[]{:S(2)}) collective-permute-start(bf16[5,8,2304]{2,1,0:T(8,128)(2,1)S(1)} %get-tuple-element.59), channel_id=1, source_target_pairs={{0,1},{1,0},{2,3},{3,2},{4,5},{5,4},{6,7},{7,6},{8,9},{9,8},{10,11... | collective-permute-start | bytes 552968 | tf_op jit(solution)/shard_map/ppermute | solution.py:22
  21.1 6.3 %collective-permute-start.4 = (bf16[5,8,2304]{2,1,0:T(8,128)(2,1)S(1)}, bf16[5,8,2304]{2,1,0:T(8,128)(2,1)S(1)}, u32[]{:S(2)}, u32[]{:S(2)}) collective-permute-start(bf16[5,8,2304]{2,1,0:T(8,128)(2,1)S(1)} %get-tuple-element.56), channel_id=1, source_target_pairs={{0,1},{1,0},{2,3},{3,2},{4,5},{5,4},{6,7},{7,6},{8,9},{9,8},{10,11... | collective-permute-start | bytes 552968 | tf_op jit(solution)/shard_map/ppermute | solution.py:22
  23.0 10.3 %collective-permute-start.6 = (bf16[5,4,2304]{2,1,0:T(4,128)(2,1)S(1)}, bf16[5,4,2304]{2,1,0:T(4,128)(2,1)S(1)}, u32[]{:S(2)}, u32[]{:S(2)}) collective-permute-start(bf16[5,4,2304]{2,1,0:T(4,128)(2,1)S(1)} %get-tuple-element.61), channel_id=1, source_target_pairs={{0,2},{2,4},{4,6},{6,0},{1,3},{3,5},{5,7},{7,1},{8,10},{10,12},{12... | collective-permute-start | bytes 276488 | tf_op jit(solution)/shard_map/ppermute | solution.py:22
  23.1 10.2 %collective-permute-start.7 = (bf16[5,4,2304]{2,1,0:T(4,128)(2,1)S(1)}, bf16[5,4,2304]{2,1,0:T(4,128)(2,1)S(1)}, u32[]{:S(2)}, u32[]{:S(2)}) collective-permute-start(bf16[5,4,2304]{2,1,0:T(4,128)(2,1)S(1)} %get-tuple-element.62), channel_id=1, source_target_pairs={{0,6},{2,0},{4,2},{6,4},{1,7},{3,1},{5,3},{7,5},{8,14},{10,8},{12,... | collective-permute-start | bytes 276488 | tf_op jit(solution)/shard_map/ppermute | solution.py:22
  29.5 7.7 %collective-permute-start.8 = (bf16[5,4,512]{2,1,0:T(4,128)(2,1)S(1)}, bf16[5,4,512]{2,1,0:T(4,128)(2,1)S(1)}, u32[]{:S(2)}, u32[]{:S(2)}) collective-permute-start(bf16[5,4,512]{2,1,0:T(4,128)(2,1)S(1)} %get-tuple-element.64), channel_id=1, source_target_pairs={{0,8},{8,16},{16,24},{24,0},{1,9},{9,17},{17,25},{25,1},{2,10},{10... | collective-permute-start | bytes 61448 | tf_op jit(solution)/shard_map/ppermute | solution.py:22
  30.9 6.3 %collective-permute-start.9 = (bf16[5,4,512]{2,1,0:T(4,128)(2,1)S(1)}, bf16[5,4,512]{2,1,0:T(4,128)(2,1)S(1)}, u32[]{:S(2)}, u32[]{:S(2)}) collective-permute-start(bf16[5,4,512]{2,1,0:T(4,128)(2,1)S(1)} %get-tuple-element.65), channel_id=1, source_target_pairs={{0,24},{8,0},{16,8},{24,16},{1,25},{9,1},{17,9},{25,17},{2,26},{10... | collective-permute-start | bytes 61448 | tf_op jit(solution)/shard_map/ppermute | solution.py:22
  35.4 3.2 %collective-permute-start.10 = (bf16[5,4,512]{2,1,0:T(4,128)(2,1)S(1)}, bf16[5,4,512]{2,1,0:T(4,128)(2,1)S(1)}, u32[]{:S(2)}, u32[]{:S(2)}) collective-permute-start(bf16[5,4,512]{2,1,0:T(4,128)(2,1)S(1)} %get-tuple-element.66), channel_id=1, source_target_pairs={{0,2},{2,4},{4,6},{6,0},{1,3},{3,5},{5,7},{7,1},{8,10},{10,12},{12... | collective-permute-start | bytes 61448 | tf_op jit(solution)/shard_map/ppermute | solution.py:22
  35.4 3.2 %collective-permute-start.11 = (bf16[5,4,512]{2,1,0:T(4,128)(2,1)S(1)}, bf16[5,4,512]{2,1,0:T(4,128)(2,1)S(1)}, u32[]{:S(2)}, u32[]{:S(2)}) collective-permute-start(bf16[5,4,512]{2,1,0:T(4,128)(2,1)S(1)} %get-tuple-element.67), channel_id=1, source_target_pairs={{0,6},{2,0},{4,2},{6,4},{1,7},{3,1},{5,3},{7,5},{8,14},{10,8},{12,... | collective-permute-start | bytes 61448 | tf_op jit(solution)/shard_map/ppermute | solution.py:22
  42.2 7.4 %collective-permute-start.12 = (bf16[5,4,2304]{2,1,0:T(4,128)(2,1)S(1)}, bf16[5,4,2304]{2,1,0:T(4,128)(2,1)S(1)}, u32[]{:S(2)}, u32[]{:S(2)}) collective-permute-start(bf16[5,4,2304]{2,1,0:T(4,128)(2,1)S(1)} %get-tuple-element.71), channel_id=1, source_target_pairs={{0,8},{8,16},{16,24},{24,0},{1,9},{9,17},{17,25},{25,1},{2,10},{10... | collective-permute-start | bytes 276488 | tf_op jit(solution)/shard_map/ppermute | solution.py:22
  42.2 7.3 %collective-permute-start.13 = (bf16[5,4,2304]{2,1,0:T(4,128)(2,1)S(1)}, bf16[5,4,2304]{2,1,0:T(4,128)(2,1)S(1)}, u32[]{:S(2)}, u32[]{:S(2)}) collective-permute-start(bf16[5,4,2304]{2,1,0:T(4,128)(2,1)S(1)} %get-tuple-element.72), channel_id=1, source_target_pairs={{0,24},{8,0},{16,8},{24,16},{1,25},{9,1},{17,9},{25,17},{2,26},{10... | collective-permute-start | bytes 276488 | tf_op jit(solution)/shard_map/ppermute | solution.py:22
  46.1 7.5 %collective-permute-start.15 = (bf16[5,8,2304]{2,1,0:T(8,128)(2,1)S(1)}, bf16[5,8,2304]{2,1,0:T(8,128)(2,1)S(1)}, u32[]{:S(2)}, u32[]{:S(2)}) collective-permute-start(bf16[5,8,2304]{2,1,0:T(8,128)(2,1)S(1)} %get-tuple-element.79), channel_id=1, source_target_pairs={{0,1},{1,0},{2,3},{3,2},{4,5},{5,4},{6,7},{7,6},{8,9},{9,8},{10,11... | collective-permute-start | bytes 552968 | tf_op jit(solution)/shard_map/ppermute | solution.py:22
  49.7 7.0 %collective-permute-start.14 = (bf16[5,8,2304]{2,1,0:T(8,128)(2,1)S(1)}, bf16[5,8,2304]{2,1,0:T(8,128)(2,1)S(1)}, u32[]{:S(2)}, u32[]{:S(2)}) collective-permute-start(bf16[5,8,2304]{2,1,0:T(8,128)(2,1)S(1)} %get-tuple-element.74), channel_id=1, source_target_pairs={{0,1},{1,0},{2,3},{3,2},{4,5},{5,4},{6,7},{7,6},{8,9},{9,8},{10,11... | collective-permute-start | bytes 552968 | tf_op jit(solution)/shard_map/ppermute | solution.py:22
  53.6 9.4 %collective-permute-start.16 = (bf16[5,4,2304]{2,1,0:T(4,128)(2,1)S(1)}, bf16[5,4,2304]{2,1,0:T(4,128)(2,1)S(1)}, u32[]{:S(2)}, u32[]{:S(2)}) collective-permute-start(bf16[5,4,2304]{2,1,0:T(4,128)(2,1)S(1)} %get-tuple-element.81), channel_id=1, source_target_pairs={{0,2},{2,4},{4,6},{6,0},{1,3},{3,5},{5,7},{7,1},{8,10},{10,12},{12... | collective-permute-start | bytes 276488 | tf_op jit(solution)/shard_map/ppermute | solution.py:22
  53.7 9.3 %collective-permute-start.17 = (bf16[5,4,2304]{2,1,0:T(4,128)(2,1)S(1)}, bf16[5,4,2304]{2,1,0:T(4,128)(2,1)S(1)}, u32[]{:S(2)}, u32[]{:S(2)}) collective-permute-start(bf16[5,4,2304]{2,1,0:T(4,128)(2,1)S(1)} %get-tuple-element.82), channel_id=1, source_target_pairs={{0,6},{2,0},{4,2},{6,4},{1,7},{3,1},{5,3},{7,5},{8,14},{10,8},{12,... | collective-permute-start | bytes 276488 | tf_op jit(solution)/shard_map/ppermute | solution.py:22
  59.2 8.2 %collective-permute-start.18 = (bf16[5,4,512]{2,1,0:T(4,128)(2,1)S(1)}, bf16[5,4,512]{2,1,0:T(4,128)(2,1)S(1)}, u32[]{:S(2)}, u32[]{:S(2)}) collective-permute-start(bf16[5,4,512]{2,1,0:T(4,128)(2,1)S(1)} %get-tuple-element.84), channel_id=1, source_target_pairs={{0,8},{8,16},{16,24},{24,0},{1,9},{9,17},{17,25},{25,1},{2,10},{10... | collective-permute-start | bytes 61448 | tf_op jit(solution)/shard_map/ppermute | solution.py:22
  59.2 8.2 %collective-permute-start.19 = (bf16[5,4,512]{2,1,0:T(4,128)(2,1)S(1)}, bf16[5,4,512]{2,1,0:T(4,128)(2,1)S(1)}, u32[]{:S(2)}, u32[]{:S(2)}) collective-permute-start(bf16[5,4,512]{2,1,0:T(4,128)(2,1)S(1)} %get-tuple-element.85), channel_id=1, source_target_pairs={{0,24},{8,0},{16,8},{24,16},{1,25},{9,1},{17,9},{25,17},{2,26},{10... | collective-permute-start | bytes 61448 | tf_op jit(solution)/shard_map/ppermute | solution.py:22
  65.6 3.2 %collective-permute-start.20 = (bf16[5,4,512]{2,1,0:T(4,128)(2,1)S(1)}, bf16[5,4,512]{2,1,0:T(4,128)(2,1)S(1)}, u32[]{:S(2)}, u32[]{:S(2)}) collective-permute-start(bf16[5,4,512]{2,1,0:T(4,128)(2,1)S(1)} %get-tuple-element.86), channel_id=1, source_target_pairs={{0,2},{2,4},{4,6},{6,0},{1,3},{3,5},{5,7},{7,1},{8,10},{10,12},{12... | collective-permute-start | bytes 61448 | tf_op jit(solution)/shard_map/ppermute | solution.py:22
  65.6 3.2 %collective-permute-start.21 = (bf16[5,4,512]{2,1,0:T(4,128)(2,1)S(1)}, bf16[5,4,512]{2,1,0:T(4,128)(2,1)S(1)}, u32[]{:S(2)}, u32[]{:S(2)}) collective-permute-start(bf16[5,4,512]{2,1,0:T(4,128)(2,1)S(1)} %get-tuple-element.87), channel_id=1, source_target_pairs={{0,6},{2,0},{4,2},{6,4},{1,7},{3,1},{5,3},{7,5},{8,14},{10,8},{12,... | collective-permute-start | bytes 61448 | tf_op jit(solution)/shard_map/ppermute | solution.py:22

commit v4 on v3

--- a/solution.py
+++ b/solution.py
@@ -20,6 +20,18 @@
 def passed_along(value, axis, by):
     devices = lax.axis_size(axis)
     return lax.ppermute(value, axis, [(i, (i + by) % devices) for i in range(devices)])
+
+
+def exchanged(value, axis, place):
+    devices = lax.axis_size(axis)
+    pairs = []
+    for i in range(place, devices, 2):
+        pairs += [(i, (i + 1) % devices), ((i + 1) % devices, i)]
+    return lax.ppermute(value, axis, sorted(pairs))
+
+
+def is_even(axis):
+    return lax.rem(lax.axis_index(axis), 2) == 0
 
 
 def from_partners(value, axis):
@@ -102,6 +114,7 @@
 def first_products_kernel(w_hbm, w_a, w_b, up_ref, down_ref, left_ref, right_ref, *refs):
     w_c, *outs, sems = refs
     early, late = w_a.shape[0] + w_b.shape[0], w_c.shape[0]
+    even = is_even("col")
     copies = [
         pltpu.make_async_copy(w_hbm.at[early + l], w_c.at[l], sems.at[l]) for l in range(late)
     ]
@@ -111,22 +124,24 @@
         if l >= early:
             copies[l - early].wait()
         ref, at = layer_of((w_a, w_b, w_c), l)
-        factors = jnp.concatenate([up_ref[l], down_ref[l], left_ref[l], right_ref[l]], axis=0)
+        left, right = left_ref[l], right_ref[l]
+        cols = [jnp.where(even, right, left), jnp.where(even, left, right)]
+        factors = jnp.concatenate([up_ref[l], down_ref[l]] + cols, axis=0)
         products = rows_by_features(factors, ref[at])
         half = products.shape[0] // 2
         store_products(l, products[:half], products[half:], *outs)
 
 
 def middle_col_kernel(partners, col_keep, *refs):
-    received, (col_total, left_send, right_send) = refs[:partners], refs[partners:]
-    rank = left_send.shape[1]
+    received, (col_total, even_send, odd_send) = refs[:partners], refs[partners:]
+    rank = even_send.shape[1]
     for l in range(col_keep.shape[0]):
         col = col_keep[l]
         for other in received:
             col = col + other[l].astype(F32)
         col_total[l] = col
-        left_send[l] = col[:rank].astype(BF16)
-        right_send[l] = col[rank:].astype(BF16)
+        even_send[l] = col[:rank].astype(BF16)
+        odd_send[l] = col[rank:].astype(BF16)
 
 
 def middle_row_kernel(row_keep, from_above, from_below, row_diff, row_send):
@@ -192,12 +207,12 @@
             send[l] = back[rank * i : rank * i + rank].astype(BF16)
 
 
-def back_col_kernel(earlier, w_a, w_b, w_c, col_total, from_left, from_right, *refs):
+def back_col_kernel(earlier, w_a, w_b, w_c, col_total, from_even, from_odd, *refs):
     pairs, refs = refs[: 2 * earlier], refs[2 * earlier :]
     basis_ref, back_ref, *sends, v_ref = refs
     layers, pair, _ = col_total.shape
     for l in range(layers):
-        theirs = jnp.concatenate([from_left[l], from_right[l]], axis=0).astype(F32)
+        theirs = jnp.concatenate([from_even[l], from_odd[l]], axis=0).astype(F32)
         store_vectors(v_ref, slice(l * pair, (l + 1) * pair), col_total[l] - theirs)
     pairs = list(zip(pairs[::2], pairs[1::2]))
     back_products(v_ref, (w_a, w_b, w_c), pairs, basis_ref, back_ref, sends, layers)
@@ -224,7 +239,7 @@
 
 
 def next_products_kernel(earlier, w_a, w_b, w_c, *refs):
-    (row_back, col_back, above, below, left, right), refs = refs[:6], refs[6:]
+    (row_back, col_back, above, below, at_even, at_odd), refs = refs[:6], refs[6:]
     pairs, refs = refs[: 2 * earlier], refs[2 * earlier :]
     row_basis, col_basis, bases_ref, factors_ref, *outs, f_ref = refs
     layers, rank, _ = above.shape
@@ -233,7 +248,7 @@
     bases_ref[stack:, :] = col_basis[...]
     for l in range(layers):
         f_ref[l * pair : (l + 1) * pair, :] = combined_of(l, row_back, above, below)
-        f_ref[stack + l * pair : stack + (l + 1) * pair, :] = combined_of(l, col_back, left, right)
+        f_ref[stack + l * pair : stack + (l + 1) * pair, :] = combined_of(l, col_back, at_even, at_odd)
     factors = f_ref[...].astype(BF16)
     factors_ref[...] = factors
     known = list(zip(pairs[::2], pairs[1::2])) + [(bases_ref, factors_ref)]
@@ -254,20 +269,21 @@
 
 
 def finish_kernel(earlier, chunk, w_a, w_b, w_c, *refs):
-    (row_back, col_back, above, below, left, right), refs = refs[:6], refs[6:]
+    (row_back, col_back, above, below, at_even, at_odd), refs = refs[:6], refs[6:]
     pairs, refs = refs[: 2 * earlier], refs[2 * earlier :]
     row_basis, col_basis, w_out, down_out, right_out, staged, sems = refs
     layers, depth, _ = staged.shape
     rank, stack = above.shape[1], row_basis.shape[0]
     pair = 2 * rank
+    even = is_even("col")
     copies = []
     for l in range(layers):
         row_at = slice(l * pair, (l + 1) * pair)
         col_at = slice(stack + l * pair, stack + (l + 1) * pair)
         row = combined_of(l, row_back, above, below)
-        col = combined_of(l, col_back, left, right)
+        col = combined_of(l, col_back, at_even, at_odd)
         down_out[l] = row[rank:]
-        right_out[l] = col[rank:]
+        right_out[l] = jnp.where(even, col[:rank], col[rank:])
         old = [f[at, :] for f in pairs[1::2] for at in (row_at, col_at)]
         factors = jnp.concatenate(old + [row.astype(BF16), col.astype(BF16)], axis=0)
         ref, at = layer_of((w_a, w_b, w_c), l)
@@ -343,25 +359,25 @@
         col_received = from_partners(col_send, "mp")
         from_above = passed_along(down_send, "row", 1)
         from_below = passed_along(up_send, "row", -1)
-        col_total, left_send, right_send = local(
+        col_total, even_send, odd_send = local(
             functools.partial(middle_col_kernel, partners),
             [kept, one_edge, one_edge],
             (col_keep, *col_received),
         )
-        from_left = passed_along(right_send, "col", 1)
-        from_right = passed_along(left_send, "col", -1)
+        from_odd = exchanged(odd_send, "col", 1)
+        from_even = exchanged(even_send, "col", 0)
         row_diff, row_send = local(
             middle_row_kernel, [kept, both_edges], (row_keep, from_above, from_below)
         )
         row_received = from_partners(row_send, "mp")
-        col_basis, col_back, left_send, right_send = local(
+        col_basis, col_back, even_send, odd_send = local(
             functools.partial(back_col_kernel, repeat),
             back_outs,
-            (*w, col_total, from_left, from_right, *pairs),
+            (*w, col_total, from_even, from_odd, *pairs),
             scratch=vectors,
         )
-        from_left = passed_along(right_send, "col", 1)
-        from_right = passed_along(left_send, "col", -1)
+        from_odd = exchanged(odd_send, "col", 1)
+        from_even = exchanged(even_send, "col", 0)
         row_basis, row_back, up_send, down_send = local(
             functools.partial(back_row_kernel, partners, repeat),
             back_outs,
@@ -370,7 +386,7 @@
         )
         from_above = passed_along(down_send, "row", 1)
         from_below = passed_along(up_send, "row", -1)
-        moved = (row_back, col_back, from_above, from_below, from_left, from_right)
+        moved = (row_back, col_back, from_above, from_below, from_even, from_odd)
         args = (*w, *moved, *pairs, row_basis, col_basis)
         if repeat + 1 < ROUNDS:
             bases, factors, *products = local(

time: 75.6 us -> 74.4 us (0.984); the launches traced: 74.4 us -> 74.3 us
  starting transfers between devices: 32 us -> 29.4 us
  waiting for transfers between devices: 15.3 us -> 17.7 us
    ppermute x22 -> x14, starting transfers between devices: 32 us -> 24.9 us  [passed_along(): lax.ppermute(value, axis, [(i, (i + by) % devices) for i in range(devices)])]
    ppermute x0 -> x8, waiting for transfers between devices: none -> 5.12 us  [exchanged(): return lax.ppermute(value, axis, sorted(pairs))]
    ppermute x0 -> x8, starting transfers between devices: none -> 4.49 us  [exchanged(): return lax.ppermute(value, axis, sorted(pairs))]
    ppermute x22 -> x14, waiting for transfers between devices: 15.3 us -> 12.6 us  [passed_along(): lax.ppermute(value, axis, [(i, (i + by) % devices) for i in range(devices)])]
  transfers between devices with their start and end apart: 22 -> 22, of which waited for: 10 -> 12; matrix products, arithmetic and copies ran while one was open for 0% -> 0% of each run, Pallas kernels for 16% -> 16%
where the time goes in v4:
time: 74.4 us; the launch traced here: 74.3 us
  starting transfers between devices  29.4 us (40%)
  Pallas kernels  26.3 us (35%)
  waiting for transfers between devices  17.7 us (24%)
  between operations  0.88 us (1%)
    pallas_call x13, Pallas kernels, call(): pl.pallas_call(kernel, out_shape=[jax.ShapeDtypeStruct(shape, dtype) for...  26.3 us
    ppermute x14, starting transfers between devices, passed_along(): lax.ppermute(value, axis, [(i, (i + by) % devices) for i in range(devices)])  24.9 us
    ppermute x14, waiting for transfers between devices, passed_along(): lax.ppermute(value, axis, [(i, (i + by) % devices) for i in range(devices)])  12.6 us
    ppermute x8, waiting for transfers between devices, exchanged(): return lax.ppermute(value, axis, sorted(pairs))  5.12 us
    ppermute x8, starting transfers between devices, exchanged(): return lax.ppermute(value, axis, sorted(pairs))  4.49 us
  transfers between devices with their start and end apart: 22, of which 12 were waited for; matrix products, arithmetic and copies ran while one was open for 0% of the time, Pallas kernels for 16%

profile of v4, /device:TPU:0, one launch (start us, length us, event | category | flops | bytes accessed | tf_op | source)
XLA Modules:
  0.0 74.3 jit_solution(12719452489153613370)
XLA Ops:
  0.6 1.7 %shard_map.58 = (bf16[1,2304,512]{2,1,0:T(8,128)(2,1)S(1)}, bf16[5,4,512]{2,1,0:T(4,128)(2,1)S(1)}, bf16[5,4,512]{2,1,0:T(4,128)(2,1)S(1)}) custom-call(bf16[5,2304,512]{2,1,0:T(8,128)(2,1)} %bitcast.6, bf16[5,4,512]{2,1,0:T(4,128)(2,1)} %bitcast.9, bf16[5,4,512]{2,1,0:T(4,128)(2,1)} %bitcast.10), custom_call_target="tpu_custom_call" | custom-call | flops 1000000 | tf_op jit(solution)/shard_map/pallas_call | solution.py:42
  2.4 3.1 %collective-permute-start = (bf16[5,4,512]{2,1,0:T(4,128)(2,1)S(1)}, bf16[5,4,512]{2,1,0:T(4,128)(2,1)S(1)}, u32[]{:S(2)}, u32[]{:S(2)}) collective-permute-start(bf16[5,4,512]{2,1,0:T(4,128)(2,1)S(1)} %get-tuple-element.49.down_ref), channel_id=1, source_target_pairs={{0,8},{8,16},{16,24},{24,0},{1,9},{9,17},{17,25},{25,1},{2,10},{10... | collective-permute-start | bytes 61448 | tf_op jit(solution)/shard_map/ppermute | solution.py:22
  5.5 0.0 collective-permute-start.1
  5.5 2.4 %shard_map.59.w_b = bf16[2,2304,512]{2,1,0:T(8,128)(2,1)S(1)} custom-call(bf16[5,2304,512]{2,1,0:T(8,128)(2,1)} %bitcast.7), custom_call_target="tpu_custom_call" | custom-call | flops 100000000 | tf_op jit(solution)/shard_map/pallas_call | solution.py:42
  7.9 1.4 %collective-permute-done.up_ref = bf16[5,4,512]{2,1,0:T(4,128)(2,1)S(1)} collective-permute-done((bf16[5,4,512]{2,1,0:T(4,128)(2,1)S(1)}, bf16[5,4,512]{2,1,0:T(4,128)(2,1)S(1)}, u32[]{:S(2)}, u32[]{:S(2)}) %collective-permute-start) | collective-permute-done | bytes 20512 | tf_op jit(solution)/shard_map/ppermute | solution.py:22
  9.3 0.0 collective-permute-done.1.left_ref
  9.3 3.6 %shard_map.60 = (bf16[2,2304,512]{2,1,0:T(8,128)(2,1)S(1)}, f32[5,8,2304]{2,1,0:T(8,128)S(1)}, bf16[5,4,2304]{2,1,0:T(4,128)(2,1)S(1)}, bf16[5,4,2304]{2,1,0:T(4...) custom-call(bf16[5,2304,512]{2,1,0:T(8,128)(2,1)} %bitcast.8, ...), custom_call_target="tpu_custom_call" | custom-call | flops 1000000 | tf_op jit(solution)/shard_map/pallas_call | solution.py:42
  12.8 1.0 %collective-permute-start.2 = (bf16[5,4,2304]{2,1,0:T(4,128)(2,1)S(1)}, bf16[5,4,2304]{2,1,0:T(4,128)(2,1)S(1)}, u32[]{:S(2)}, u32[]{:S(2)}) collective-permute-start(bf16[5,4,2304]{2,1,0:T(4,128)(2,1)S(1)} %get-tuple-element.53), channel_id=1, source_target_pairs={{0,8},{8,16},{16,24},{24,0},{1,9},{9,17},{17,25},{25,1},{2,10},{10... | collective-permute-start | bytes 276488 | tf_op jit(solution)/shard_map/ppermute | solution.py:22
  13.9 2.8 %collective-permute-start.3 = (bf16[5,4,2304]{2,1,0:T(4,128)(2,1)S(1)}, bf16[5,4,2304]{2,1,0:T(4,128)(2,1)S(1)}, u32[]{:S(2)}, u32[]{:S(2)}) collective-permute-start(bf16[5,4,2304]{2,1,0:T(4,128)(2,1)S(1)} %get-tuple-element.54), channel_id=1, source_target_pairs={{0,24},{8,0},{16,8},{24,16},{1,25},{9,1},{17,9},{25,17},{2,26},{10... | collective-permute-start | bytes 276488 | tf_op jit(solution)/shard_map/ppermute | solution.py:22
  16.7 1.7 %collective-permute-start.5 = (bf16[5,8,2304]{2,1,0:T(8,128)(2,1)S(1)}, bf16[5,8,2304]{2,1,0:T(8,128)(2,1)S(1)}, u32[]{:S(2)}, u32[]{:S(2)}) collective-permute-start(bf16[5,8,2304]{2,1,0:T(8,128)(2,1)S(1)} %get-tuple-element.59), channel_id=1, source_target_pairs={{0,1},{1,0},{2,3},{3,2},{4,5},{5,4},{6,7},{7,6},{8,9},{9,8},{10,11... | collective-permute-start | bytes 552968 | tf_op jit(solution)/shard_map/ppermute | solution.py:22
  18.5 1.8 %collective-permute-done.2.from_above = bf16[5,4,2304]{2,1,0:T(4,128)(2,1)S(1)} collective-permute-done((bf16[5,4,2304]{2,1,0:T(4,128)(2,1)S(1)}, bf16[5,4,2304]{2,1,0:T(4,128)(2,1)S(1)}, u32[]{:S(2)}, u32[]{:S(2)}) %collective-permute-start.2) | collective-permute-done | bytes 92192 | tf_op jit(solution)/shard_map/ppermute | solution.py:22
  20.2 0.7 collective-permute-done.3.from_below
  21.0 0.1 shard_map.61
  21.1 1.6 %collective-permute-start.4 = (bf16[5,8,2304]{2,1,0:T(8,128)(2,1)S(1)}, bf16[5,8,2304]{2,1,0:T(8,128)(2,1)S(1)}, u32[]{:S(2)}, u32[]{:S(2)}) collective-permute-start(bf16[5,8,2304]{2,1,0:T(8,128)(2,1)S(1)} %get-tuple-element.56), channel_id=1, source_target_pairs={{0,1},{1,0},{2,3},{3,2},{4,5},{5,4},{6,7},{7,6},{8,9},{9,8},{10,11... | collective-permute-start | bytes 552968 | tf_op jit(solution)/shard_map/ppermute | solution.py:22
  22.6 0.3 collective-permute-done.5.refs_0_
  22.9 0.1 shard_map.63
  23.0 0.1 collective-permute-start.6
  23.1 2.3 %collective-permute-start.7 = (bf16[5,4,2304]{2,1,0:T(4,128)(2,1)S(1)}, bf16[5,4,2304]{2,1,0:T(4,128)(2,1)S(1)}, u32[]{:S(2)}, u32[]{:S(2)}) collective-permute-start(bf16[5,4,2304]{2,1,0:T(4,128)(2,1)S(1)} %get-tuple-element.62), channel_id=1, source_target_pairs={{0,6},{2,4},{4,2},{6,0},{1,7},{3,5},{5,3},{7,1},{8,14},{10,12},{12... | collective-permute-start | bytes 276488 | tf_op jit(solution)/shard_map/ppermute | solution.py:30
  25.4 2.0 %collective-permute-done.4.refs_0_ = bf16[5,8,2304]{2,1,0:T(8,128)(2,1)S(1)} collective-permute-done((bf16[5,8,2304]{2,1,0:T(8,128)(2,1)S(1)}, bf16[5,8,2304]{2,1,0:T(8,128)(2,1)S(1)}, u32[]{:S(2)}, u32[]{:S(2)}) %collective-permute-start.4) | collective-permute-done | bytes 184352 | tf_op jit(solution)/shard_map/ppermute | solution.py:22
  27.4 2.1 %shard_map.62 = (bf16[40,2304]{1,0:T(8,128)(2,1)S(1)}, f32[40,512]{1,0:T(8,128)S(1)}, bf16[5,4,512]{2,1,0:T(4,128)(2,1)S(1)}, bf16[5,4,512]{2,1,0:T(4,128)(2,1)S(1)}) custom-call(bf16[1,2304,512]{2,1,0:T(8,128)(2,1)S(1)} %get-tuple-element.48.w_a, bf16[2,2304,512]{2,1,0:T(8,128)(2,1)S(1)} %shard_map.59.w_b, bf16[2,2304,512]{2,1,0:T(8,128)(2,1)S(1)} %get-tuple-element.51.w_c, ...), custom_call_target="tpu_custom_call" | custom-call | flops 1000000 | tf_op jit(solution)/shard_map/pallas_call | solution.py:42
  29.5 1.5 %collective-permute-start.8 = (bf16[5,4,512]{2,1,0:T(4,128)(2,1)S(1)}, bf16[5,4,512]{2,1,0:T(4,128)(2,1)S(1)}, u32[]{:S(2)}, u32[]{:S(2)}) collective-permute-start(bf16[5,4,512]{2,1,0:T(4,128)(2,1)S(1)} %get-tuple-element.64), channel_id=1, source_target_pairs={{0,8},{8,16},{16,24},{24,0},{1,9},{9,17},{17,25},{25,1},{2,10},{10... | collective-permute-start | bytes 61448 | tf_op jit(solution)/shard_map/ppermute | solution.py:22
  30.9 2.4 %collective-permute-start.9 = (bf16[5,4,512]{2,1,0:T(4,128)(2,1)S(1)}, bf16[5,4,512]{2,1,0:T(4,128)(2,1)S(1)}, u32[]{:S(2)}, u32[]{:S(2)}) collective-permute-start(bf16[5,4,512]{2,1,0:T(4,128)(2,1)S(1)} %get-tuple-element.65), channel_id=1, source_target_pairs={{0,24},{8,0},{16,8},{24,16},{1,25},{9,1},{17,9},{25,17},{2,26},{10... | collective-permute-start | bytes 61448 | tf_op jit(solution)/shard_map/ppermute | solution.py:22
  33.3 0.0 collective-permute-done.6.from_even
  33.3 2.1 %shard_map.64 = (bf16[40,2304]{1,0:T(8,128)(2,1)S(1)}, f32[40,512]{1,0:T(8,128)S(1)}, bf16[5,4,512]{2,1,0:T(4,128)(2,1)S(1)}, bf16[5,4,512]{2,1,0:T(4,128)(2,1)S(1)}) custom-call(bf16[1,2304,512]{2,1,0:T(8,128)(2,1)S(1)} %get-tuple-element.48.w_a, bf16[2,2304,512]{2,1,0:T(8,128)(2,1)S(1)} %shard_map.59.w_b, bf16[2,2304,512]{2,1,0:T(8,128)(2,1)S(1)} %get-tuple-element.51.w_c, ...), custom_call_target="tpu_custom_call" | custom-call | flops 1000000 | tf_op jit(solution)/shard_map/pallas_call | solution.py:42
  35.4 0.0 collective-permute-start.10
  35.4 0.7 collective-permute-start.11
  36.1 0.5 collective-permute-done.10.refs_4_
  36.6 2.0 %collective-permute-done.11.refs_5_ = bf16[5,4,512]{2,1,0:T(4,128)(2,1)S(1)} collective-permute-done((bf16[5,4,512]{2,1,0:T(4,128)(2,1)S(1)}, bf16[5,4,512]{2,1,0:T(4,128)(2,1)S(1)}, u32[]{:S(2)}, u32[]{:S(2)}) %collective-permute-start.11) | collective-permute-done | bytes 20512 | tf_op jit(solution)/shard_map/ppermute | solution.py:30
  38.7 3.5 %shard_map.65 = (bf16[80,2304]{1,0:T(8,128)(2,1)S(1)}, bf16[80,512]{1,0:T(8,128)(2,1)S(1)}, f32[5,8,2304]{2,1,0:T(8,128)S(1)}, bf16[5,4,2304]{2,1,0:T(4,128)(2,1...) custom-call(bf16[1,2304,512]{2,1,0:T(8,128)(2,1)S(1)} %get-tuple-element.48.w_a, ...), custom_call_target="tpu_custom_call" | custom-call | flops 1000000 | tf_op jit(solution)/shard_map/pallas_call | solution.py:42
  42.2 0.0 collective-permute-start.12
  42.3 3.8 %collective-permute-start.13 = (bf16[5,4,2304]{2,1,0:T(4,128)(2,1)S(1)}, bf16[5,4,2304]{2,1,0:T(4,128)(2,1)S(1)}, u32[]{:S(2)}, u32[]{:S(2)}) collective-permute-start(bf16[5,4,2304]{2,1,0:T(4,128)(2,1)S(1)} %get-tuple-element.72), channel_id=1, source_target_pairs={{0,24},{8,0},{16,8},{24,16},{1,25},{9,1},{17,9},{25,17},{2,26},{10... | collective-permute-start | bytes 276488 | tf_op jit(solution)/shard_map/ppermute | solution.py:22
  46.1 1.5 %collective-permute-start.15 = (bf16[5,8,2304]{2,1,0:T(8,128)(2,1)S(1)}, bf16[5,8,2304]{2,1,0:T(8,128)(2,1)S(1)}, u32[]{:S(2)}, u32[]{:S(2)}) collective-permute-start(bf16[5,8,2304]{2,1,0:T(8,128)(2,1)S(1)} %get-tuple-element.79), channel_id=1, source_target_pairs={{0,1},{1,0},{2,3},{3,2},{4,5},{5,4},{6,7},{7,6},{8,9},{9,8},{10,11... | collective-permute-start | bytes 552968 | tf_op jit(solution)/shard_map/ppermute | solution.py:22
  47.6 2.0 %collective-permute-done.12.from_above = bf16[5,4,2304]{2,1,0:T(4,128)(2,1)S(1)} collective-permute-done((bf16[5,4,2304]{2,1,0:T(4,128)(2,1)S(1)}, bf16[5,4,2304]{2,1,0:T(4,128)(2,1)S(1)}, u32[]{:S(2)}, u32[]{:S(2)}) %collective-permute-start.12) | collective-permute-done | bytes 92192 | tf_op jit(solution)/shard_map/ppermute | solution.py:22
  49.6 0.0 collective-permute-done.13.from_below
  49.6 0.1 shard_map.66
  49.7 1.6 %collective-permute-start.14 = (bf16[5,8,2304]{2,1,0:T(8,128)(2,1)S(1)}, bf16[5,8,2304]{2,1,0:T(8,128)(2,1)S(1)}, u32[]{:S(2)}, u32[]{:S(2)}) collective-permute-start(bf16[5,8,2304]{2,1,0:T(8,128)(2,1)S(1)} %get-tuple-element.74), channel_id=1, source_target_pairs={{0,1},{1,0},{2,3},{3,2},{4,5},{5,4},{6,7},{7,6},{8,9},{9,8},{10,11... | collective-permute-start | bytes 552968 | tf_op jit(solution)/shard_map/ppermute | solution.py:22
  51.2 2.3 %collective-permute-done.15.refs_0_ = bf16[5,8,2304]{2,1,0:T(8,128)(2,1)S(1)} collective-permute-done((bf16[5,8,2304]{2,1,0:T(8,128)(2,1)S(1)}, bf16[5,8,2304]{2,1,0:T(8,128)(2,1)S(1)}, u32[]{:S(2)}, u32[]{:S(2)}) %collective-permute-start.15) | collective-permute-done | bytes 184352 | tf_op jit(solution)/shard_map/ppermute | solution.py:22
  53.6 0.1 shard_map.68
  53.6 0.1 collective-permute-start.16
  53.7 0.7 collective-permute-start.17
  54.4 2.1 %collective-permute-done.14.refs_0_ = bf16[5,8,2304]{2,1,0:T(8,128)(2,1)S(1)} collective-permute-done((bf16[5,8,2304]{2,1,0:T(8,128)(2,1)S(1)}, bf16[5,8,2304]{2,1,0:T(8,128)(2,1)S(1)}, u32[]{:S(2)}, u32[]{:S(2)}) %collective-permute-start.14) | collective-permute-done | bytes 184352 | tf_op jit(solution)/shard_map/ppermute | solution.py:22
  56.5 2.5 %shard_map.67 = (bf16[40,2304]{1,0:T(8,128)(2,1)S(1)}, f32[40,512]{1,0:T(8,128)S(1)}, bf16[5,4,512]{2,1,0:T(4,128)(2,1)S(1)}, bf16[5,4,512]{2,1,0:T(4,128)(2,1)S(1)}) custom-call(bf16[1,2304,512]{2,1,0:T(8,128)(2,1)S(1)} %get-tuple-element.48.w_a, bf16[2,2304,512]{2,1,0:T(8,128)(2,1)S(1)} %shard_map.59.w_b, bf16[2,2304,512]{2,1,0:T(8,128)(2,1)S(1)} %get-tuple-element.51.w_c, ...), custom_call_target="tpu_custom_call" | custom-call | flops 1000000 | tf_op jit(solution)/shard_map/pallas_call | solution.py:42
  59.0 3.8 %collective-permute-start.19 = (bf16[5,4,512]{2,1,0:T(4,128)(2,1)S(1)}, bf16[5,4,512]{2,1,0:T(4,128)(2,1)S(1)}, u32[]{:S(2)}, u32[]{:S(2)}) collective-permute-start(bf16[5,4,512]{2,1,0:T(4,128)(2,1)S(1)} %get-tuple-element.85), channel_id=1, source_target_pairs={{0,24},{8,0},{16,8},{24,16},{1,25},{9,1},{17,9},{25,17},{2,26},{10... | collective-permute-start | bytes 61448 | tf_op jit(solution)/shard_map/ppermute | solution.py:22
  62.8 2.6 %shard_map.69 = (bf16[40,2304]{1,0:T(8,128)(2,1)S(1)}, f32[40,512]{1,0:T(8,128)S(1)}, bf16[5,4,512]{2,1,0:T(4,128)(2,1)S(1)}, bf16[5,4,512]{2,1,0:T(4,128)(2,1)S(1)}) custom-call(bf16[1,2304,512]{2,1,0:T(8,128)(2,1)S(1)} %get-tuple-element.48.w_a, bf16[2,2304,512]{2,1,0:T(8,128)(2,1)S(1)} %shard_map.59.w_b, bf16[2,2304,512]{2,1,0:T(8,128)(2,1)S(1)} %get-tuple-element.51.w_c, ...), custom_call_target="tpu_custom_call" | custom-call | flops 1000000 | tf_op jit(solution)/shard_map/pallas_call | solution.py:42
  65.4 0.7 collective-permute-start.21
  66.1 0.5 collective-permute-done.20.refs_4_
  66.6 2.0 %collective-permute-done.21.refs_5_ = bf16[5,4,512]{2,1,0:T(4,128)(2,1)S(1)} collective-permute-done((bf16[5,4,512]{2,1,0:T(4,128)(2,1)S(1)}, bf16[5,4,512]{2,1,0:T(4,128)(2,1)S(1)}, u32[]{:S(2)}, u32[]{:S(2)}) %collective-permute-start.21) | collective-permute-done | bytes 20512 | tf_op jit(solution)/shard_map/ppermute | solution.py:30
  68.6 5.5 %shard_map.70 = (bf16[5,2304,512]{2,1,0:T(8,128)(2,1)}, f32[5,4,512]{2,1,0:T(4,128)}, f32[5,4,512]{2,1,0:T(4,128)}) custom-call(bf16[1,2304,512]{2,1,0:T(8,128)(2,1)S(1)} %get-tuple-element.48.w_a, bf16[2,2304,512]{2,1,0:T(8,128)(2,1)S(1)} %shard_map.59.w_b, bf16[2,2304,512]{2,1,0:T(8,128)(2,1)S(1)} %get-tuple-element.51.w_c, ...), custom_call_target="tpu_custom_call" | custom-call | flops 1000000 | tf_op jit(solution)/shard_map/pallas_call | solution.py:42
  (9 shorter events, 0.0 us)
Async XLA Ops:
  2.4 6.9 %collective-permute-start = (bf16[5,4,512]{2,1,0:T(4,128)(2,1)S(1)}, bf16[5,4,512]{2,1,0:T(4,128)(2,1)S(1)}, u32[]{:S(2)}, u32[]{:S(2)}) collective-permute-start(bf16[5,4,512]{2,1,0:T(4,128)(2,1)S(1)} %get-tuple-element.49.down_ref), channel_id=1, source_target_pairs={{0,8},{8,16},{16,24},{24,0},{1,9},{9,17},{17,25},{25,1},{2,10},{10... | collective-permute-start | bytes 61448 | tf_op jit(solution)/shard_map/ppermute | solution.py:22
  5.5 3.8 %collective-permute-start.1 = (bf16[5,4,512]{2,1,0:T(4,128)(2,1)S(1)}, bf16[5,4,512]{2,1,0:T(4,128)(2,1)S(1)}, u32[]{:S(2)}, u32[]{:S(2)}) collective-permute-start(bf16[5,4,512]{2,1,0:T(4,128)(2,1)S(1)} %get-tuple-element.50.right_ref), channel_id=1, source_target_pairs={{0,2},{2,4},{4,6},{6,0},{1,3},{3,5},{5,7},{7,1},{8,10},{10,12},{12... | collective-permute-start | bytes 61448 | tf_op jit(solution)/shard_map/ppermute | solution.py:22
  12.8 7.4 %collective-permute-start.2 = (bf16[5,4,2304]{2,1,0:T(4,128)(2,1)S(1)}, bf16[5,4,2304]{2,1,0:T(4,128)(2,1)S(1)}, u32[]{:S(2)}, u32[]{:S(2)}) collective-permute-start(bf16[5,4,2304]{2,1,0:T(4,128)(2,1)S(1)} %get-tuple-element.53), channel_id=1, source_target_pairs={{0,8},{8,16},{16,24},{24,0},{1,9},{9,17},{17,25},{25,1},{2,10},{10... | collective-permute-start | bytes 276488 | tf_op jit(solution)/shard_map/ppermute | solution.py:22
  13.9 7.1 %collective-permute-start.3 = (bf16[5,4,2304]{2,1,0:T(4,128)(2,1)S(1)}, bf16[5,4,2304]{2,1,0:T(4,128)(2,1)S(1)}, u32[]{:S(2)}, u32[]{:S(2)}) collective-permute-start(bf16[5,4,2304]{2,1,0:T(4,128)(2,1)S(1)} %get-tuple-element.54), channel_id=1, source_target_pairs={{0,24},{8,0},{16,8},{24,16},{1,25},{9,1},{17,9},{25,17},{2,26},{10... | collective-permute-start | bytes 276488 | tf_op jit(solution)/shard_map/ppermute | solution.py:22
  16.7 6.2 %collective-permute-start.5 = (bf16[5,8,2304]{2,1,0:T(8,128)(2,1)S(1)}, bf16[5,8,2304]{2,1,0:T(8,128)(2,1)S(1)}, u32[]{:S(2)}, u32[]{:S(2)}) collective-permute-start(bf16[5,8,2304]{2,1,0:T(8,128)(2,1)S(1)} %get-tuple-element.59), channel_id=1, source_target_pairs={{0,1},{1,0},{2,3},{3,2},{4,5},{5,4},{6,7},{7,6},{8,9},{9,8},{10,11... | collective-permute-start | bytes 552968 | tf_op jit(solution)/shard_map/ppermute | solution.py:22
  21.1 6.3 %collective-permute-start.4 = (bf16[5,8,2304]{2,1,0:T(8,128)(2,1)S(1)}, bf16[5,8,2304]{2,1,0:T(8,128)(2,1)S(1)}, u32[]{:S(2)}, u32[]{:S(2)}) collective-permute-start(bf16[5,8,2304]{2,1,0:T(8,128)(2,1)S(1)} %get-tuple-element.56), channel_id=1, source_target_pairs={{0,1},{1,0},{2,3},{3,2},{4,5},{5,4},{6,7},{7,6},{8,9},{9,8},{10,11... | collective-permute-start | bytes 552968 | tf_op jit(solution)/shard_map/ppermute | solution.py:22
  23.0 10.3 %collective-permute-start.6 = (bf16[5,4,2304]{2,1,0:T(4,128)(2,1)S(1)}, bf16[5,4,2304]{2,1,0:T(4,128)(2,1)S(1)}, u32[]{:S(2)}, u32[]{:S(2)}) collective-permute-start(bf16[5,4,2304]{2,1,0:T(4,128)(2,1)S(1)} %get-tuple-element.61), channel_id=1, source_target_pairs={{0,2},{2,0},{4,6},{6,4},{1,3},{3,1},{5,7},{7,5},{8,10},{10,8},{12,... | collective-permute-start | bytes 276488 | tf_op jit(solution)/shard_map/ppermute | solution.py:30
  23.1 10.2 %collective-permute-start.7 = (bf16[5,4,2304]{2,1,0:T(4,128)(2,1)S(1)}, bf16[5,4,2304]{2,1,0:T(4,128)(2,1)S(1)}, u32[]{:S(2)}, u32[]{:S(2)}) collective-permute-start(bf16[5,4,2304]{2,1,0:T(4,128)(2,1)S(1)} %get-tuple-element.62), channel_id=1, source_target_pairs={{0,6},{2,4},{4,2},{6,0},{1,7},{3,5},{5,3},{7,1},{8,14},{10,12},{12... | collective-permute-start | bytes 276488 | tf_op jit(solution)/shard_map/ppermute | solution.py:30
  29.5 6.7 %collective-permute-start.8 = (bf16[5,4,512]{2,1,0:T(4,128)(2,1)S(1)}, bf16[5,4,512]{2,1,0:T(4,128)(2,1)S(1)}, u32[]{:S(2)}, u32[]{:S(2)}) collective-permute-start(bf16[5,4,512]{2,1,0:T(4,128)(2,1)S(1)} %get-tuple-element.64), channel_id=1, source_target_pairs={{0,8},{8,16},{16,24},{24,0},{1,9},{9,17},{17,25},{25,1},{2,10},{10... | collective-permute-start | bytes 61448 | tf_op jit(solution)/shard_map/ppermute | solution.py:22
  30.9 5.2 %collective-permute-start.9 = (bf16[5,4,512]{2,1,0:T(4,128)(2,1)S(1)}, bf16[5,4,512]{2,1,0:T(4,128)(2,1)S(1)}, u32[]{:S(2)}, u32[]{:S(2)}) collective-permute-start(bf16[5,4,512]{2,1,0:T(4,128)(2,1)S(1)} %get-tuple-element.65), channel_id=1, source_target_pairs={{0,24},{8,0},{16,8},{24,16},{1,25},{9,1},{17,9},{25,17},{2,26},{10... | collective-permute-start | bytes 61448 | tf_op jit(solution)/shard_map/ppermute | solution.py:22
  35.4 1.2 %collective-permute-start.10 = (bf16[5,4,512]{2,1,0:T(4,128)(2,1)S(1)}, bf16[5,4,512]{2,1,0:T(4,128)(2,1)S(1)}, u32[]{:S(2)}, u32[]{:S(2)}) collective-permute-start(bf16[5,4,512]{2,1,0:T(4,128)(2,1)S(1)} %get-tuple-element.66), channel_id=1, source_target_pairs={{0,2},{2,0},{4,6},{6,4},{1,3},{3,1},{5,7},{7,5},{8,10},{10,8},{12,... | collective-permute-start | bytes 61448 | tf_op jit(solution)/shard_map/ppermute | solution.py:30
  35.4 3.2 %collective-permute-start.11 = (bf16[5,4,512]{2,1,0:T(4,128)(2,1)S(1)}, bf16[5,4,512]{2,1,0:T(4,128)(2,1)S(1)}, u32[]{:S(2)}, u32[]{:S(2)}) collective-permute-start(bf16[5,4,512]{2,1,0:T(4,128)(2,1)S(1)} %get-tuple-element.67), channel_id=1, source_target_pairs={{0,6},{2,4},{4,2},{6,0},{1,7},{3,5},{5,3},{7,1},{8,14},{10,12},{12... | collective-permute-start | bytes 61448 | tf_op jit(solution)/shard_map/ppermute | solution.py:30
  42.2 7.4 %collective-permute-start.12 = (bf16[5,4,2304]{2,1,0:T(4,128)(2,1)S(1)}, bf16[5,4,2304]{2,1,0:T(4,128)(2,1)S(1)}, u32[]{:S(2)}, u32[]{:S(2)}) collective-permute-start(bf16[5,4,2304]{2,1,0:T(4,128)(2,1)S(1)} %get-tuple-element.71), channel_id=1, source_target_pairs={{0,8},{8,16},{16,24},{24,0},{1,9},{9,17},{17,25},{25,1},{2,10},{10... | collective-permute-start | bytes 276488 | tf_op jit(solution)/shard_map/ppermute | solution.py:22
  42.3 7.3 %collective-permute-start.13 = (bf16[5,4,2304]{2,1,0:T(4,128)(2,1)S(1)}, bf16[5,4,2304]{2,1,0:T(4,128)(2,1)S(1)}, u32[]{:S(2)}, u32[]{:S(2)}) collective-permute-start(bf16[5,4,2304]{2,1,0:T(4,128)(2,1)S(1)} %get-tuple-element.72), channel_id=1, source_target_pairs={{0,24},{8,0},{16,8},{24,16},{1,25},{9,1},{17,9},{25,17},{2,26},{10... | collective-permute-start | bytes 276488 | tf_op jit(solution)/shard_map/ppermute | solution.py:22
  46.1 7.5 %collective-permute-start.15 = (bf16[5,8,2304]{2,1,0:T(8,128)(2,1)S(1)}, bf16[5,8,2304]{2,1,0:T(8,128)(2,1)S(1)}, u32[]{:S(2)}, u32[]{:S(2)}) collective-permute-start(bf16[5,8,2304]{2,1,0:T(8,128)(2,1)S(1)} %get-tuple-element.79), channel_id=1, source_target_pairs={{0,1},{1,0},{2,3},{3,2},{4,5},{5,4},{6,7},{7,6},{8,9},{9,8},{10,11... | collective-permute-start | bytes 552968 | tf_op jit(solution)/shard_map/ppermute | solution.py:22
  49.7 6.8 %collective-permute-start.14 = (bf16[5,8,2304]{2,1,0:T(8,128)(2,1)S(1)}, bf16[5,8,2304]{2,1,0:T(8,128)(2,1)S(1)}, u32[]{:S(2)}, u32[]{:S(2)}) collective-permute-start(bf16[5,8,2304]{2,1,0:T(8,128)(2,1)S(1)} %get-tuple-element.74), channel_id=1, source_target_pairs={{0,1},{1,0},{2,3},{3,2},{4,5},{5,4},{6,7},{7,6},{8,9},{9,8},{10,11... | collective-permute-start | bytes 552968 | tf_op jit(solution)/shard_map/ppermute | solution.py:22
  53.6 9.2 %collective-permute-start.16 = (bf16[5,4,2304]{2,1,0:T(4,128)(2,1)S(1)}, bf16[5,4,2304]{2,1,0:T(4,128)(2,1)S(1)}, u32[]{:S(2)}, u32[]{:S(2)}) collective-permute-start(bf16[5,4,2304]{2,1,0:T(4,128)(2,1)S(1)} %get-tuple-element.81), channel_id=1, source_target_pairs={{0,2},{2,0},{4,6},{6,4},{1,3},{3,1},{5,7},{7,5},{8,10},{10,8},{12,... | collective-permute-start | bytes 276488 | tf_op jit(solution)/shard_map/ppermute | solution.py:30
  53.7 9.1 %collective-permute-start.17 = (bf16[5,4,2304]{2,1,0:T(4,128)(2,1)S(1)}, bf16[5,4,2304]{2,1,0:T(4,128)(2,1)S(1)}, u32[]{:S(2)}, u32[]{:S(2)}) collective-permute-start(bf16[5,4,2304]{2,1,0:T(4,128)(2,1)S(1)} %get-tuple-element.82), channel_id=1, source_target_pairs={{0,6},{2,4},{4,2},{6,0},{1,7},{3,5},{5,3},{7,1},{8,14},{10,12},{12... | collective-permute-start | bytes 276488 | tf_op jit(solution)/shard_map/ppermute | solution.py:30
  59.0 7.1 %collective-permute-start.18 = (bf16[5,4,512]{2,1,0:T(4,128)(2,1)S(1)}, bf16[5,4,512]{2,1,0:T(4,128)(2,1)S(1)}, u32[]{:S(2)}, u32[]{:S(2)}) collective-permute-start(bf16[5,4,512]{2,1,0:T(4,128)(2,1)S(1)} %get-tuple-element.84), channel_id=1, source_target_pairs={{0,8},{8,16},{16,24},{24,0},{1,9},{9,17},{17,25},{25,1},{2,10},{10... | collective-permute-start | bytes 61448 | tf_op jit(solution)/shard_map/ppermute | solution.py:22
  59.0 7.1 %collective-permute-start.19 = (bf16[5,4,512]{2,1,0:T(4,128)(2,1)S(1)}, bf16[5,4,512]{2,1,0:T(4,128)(2,1)S(1)}, u32[]{:S(2)}, u32[]{:S(2)}) collective-permute-start(bf16[5,4,512]{2,1,0:T(4,128)(2,1)S(1)} %get-tuple-element.85), channel_id=1, source_target_pairs={{0,24},{8,0},{16,8},{24,16},{1,25},{9,1},{17,9},{25,17},{2,26},{10... | collective-permute-start | bytes 61448 | tf_op jit(solution)/shard_map/ppermute | solution.py:22
  65.4 1.2 %collective-permute-start.20 = (bf16[5,4,512]{2,1,0:T(4,128)(2,1)S(1)}, bf16[5,4,512]{2,1,0:T(4,128)(2,1)S(1)}, u32[]{:S(2)}, u32[]{:S(2)}) collective-permute-start(bf16[5,4,512]{2,1,0:T(4,128)(2,1)S(1)} %get-tuple-element.86), channel_id=1, source_target_pairs={{0,2},{2,0},{4,6},{6,4},{1,3},{3,1},{5,7},{7,5},{8,10},{10,8},{12,... | collective-permute-start | bytes 61448 | tf_op jit(solution)/shard_map/ppermute | solution.py:30
  65.4 3.2 %collective-permute-start.21 = (bf16[5,4,512]{2,1,0:T(4,128)(2,1)S(1)}, bf16[5,4,512]{2,1,0:T(4,128)(2,1)S(1)}, u32[]{:S(2)}, u32[]{:S(2)}) collective-permute-start(bf16[5,4,512]{2,1,0:T(4,128)(2,1)S(1)} %get-tuple-element.87), channel_id=1, source_target_pairs={{0,6},{2,4},{4,2},{6,0},{1,7},{3,5},{5,3},{7,1},{8,14},{10,12},{12... | collective-permute-start | bytes 61448 | tf_op jit(solution)/shard_map/ppermute | solution.py:30

commit v5 on v4

--- a/solution.py
+++ b/solution.py
@@ -91,17 +91,6 @@
         copy.wait()
 
 
-def load_more_kernel(start, w_hbm, w_ref, sems):
-    copies = [
-        pltpu.make_async_copy(w_hbm.at[start + l], w_ref.at[l], sems.at[l])
-        for l in range(w_ref.shape[0])
-    ]
-    for copy in copies:
-        copy.start()
-    for copy in copies:
-        copy.wait()
-
-
 def store_products(l, row, col, row_keep, up_send, down_send, col_keep, col_send):
     rank = row.shape[0] // 2
     row_keep[l] = row
@@ -111,9 +100,9 @@
     col_send[l] = col.astype(BF16)
 
 
-def first_products_kernel(w_hbm, w_a, w_b, up_ref, down_ref, left_ref, right_ref, *refs):
+def first_products_kernel(w_hbm, w_a, up_ref, down_ref, left_ref, right_ref, *refs):
     w_c, *outs, sems = refs
-    early, late = w_a.shape[0] + w_b.shape[0], w_c.shape[0]
+    early, late = w_a.shape[0], w_c.shape[0]
     even = is_even("col")
     copies = [
         pltpu.make_async_copy(w_hbm.at[early + l], w_c.at[l], sems.at[l]) for l in range(late)
@@ -123,7 +112,7 @@
     for l in range(early + late):
         if l >= early:
             copies[l - early].wait()
-        ref, at = layer_of((w_a, w_b, w_c), l)
+        ref, at = layer_of((w_a, w_c), l)
         left, right = left_ref[l], right_ref[l]
         cols = [jnp.where(even, right, left), jnp.where(even, left, right)]
         factors = jnp.concatenate([up_ref[l], down_ref[l]] + cols, axis=0)
@@ -207,7 +196,7 @@
             send[l] = back[rank * i : rank * i + rank].astype(BF16)
 
 
-def back_col_kernel(earlier, w_a, w_b, w_c, col_total, from_even, from_odd, *refs):
+def back_col_kernel(earlier, w_a, w_c, col_total, from_even, from_odd, *refs):
     pairs, refs = refs[: 2 * earlier], refs[2 * earlier :]
     basis_ref, back_ref, *sends, v_ref = refs
     layers, pair, _ = col_total.shape
@@ -215,10 +204,10 @@
         theirs = jnp.concatenate([from_even[l], from_odd[l]], axis=0).astype(F32)
         store_vectors(v_ref, slice(l * pair, (l + 1) * pair), col_total[l] - theirs)
     pairs = list(zip(pairs[::2], pairs[1::2]))
-    back_products(v_ref, (w_a, w_b, w_c), pairs, basis_ref, back_ref, sends, layers)
-
-
-def back_row_kernel(partners, earlier, w_a, w_b, w_c, row_diff, *refs):
+    back_products(v_ref, (w_a, w_c), pairs, basis_ref, back_ref, sends, layers)
+
+
+def back_row_kernel(partners, earlier, w_a, w_c, row_diff, *refs):
     received, refs = refs[:partners], refs[partners:]
     pairs, refs = refs[: 2 * earlier], refs[2 * earlier :]
     basis_ref, back_ref, *sends, v_ref = refs
@@ -229,7 +218,7 @@
             row = row + other[l].astype(F32)
         store_vectors(v_ref, slice(l * pair, (l + 1) * pair), row)
     pairs = list(zip(pairs[::2], pairs[1::2]))
-    back_products(v_ref, (w_a, w_b, w_c), pairs, basis_ref, back_ref, sends, layers)
+    back_products(v_ref, (w_a, w_c), pairs, basis_ref, back_ref, sends, layers)
 
 
 def combined_of(l, back_ref, first, second):
@@ -238,7 +227,7 @@
     return back_ref[l * pair : (l + 1) * pair, :] + theirs.astype(F32)
 
 
-def next_products_kernel(earlier, w_a, w_b, w_c, *refs):
+def next_products_kernel(earlier, w_a, w_c, *refs):
     (row_back, col_back, above, below, at_even, at_odd), refs = refs[:6], refs[6:]
     pairs, refs = refs[: 2 * earlier], refs[2 * earlier :]
     row_basis, col_basis, bases_ref, factors_ref, *outs, f_ref = refs
@@ -261,14 +250,14 @@
         row_at = slice(l * pair, (l + 1) * pair)
         col_at = slice(stack + l * pair, stack + (l + 1) * pair)
         own = jnp.concatenate([f_ref[row_at, :], f_ref[col_at, :]], axis=0).astype(BF16)
-        ref, at = layer_of((w_a, w_b, w_c), l)
+        ref, at = layer_of((w_a, w_c), l)
         products = rows_by_features(own, ref[at])
         store_products(
             l, products[:pair] + changes[row_at], products[pair:] + changes[col_at], *outs
         )
 
 
-def finish_kernel(earlier, chunk, w_a, w_b, w_c, *refs):
+def finish_kernel(earlier, chunk, w_a, w_c, *refs):
     (row_back, col_back, above, below, at_even, at_odd), refs = refs[:6], refs[6:]
     pairs, refs = refs[: 2 * earlier], refs[2 * earlier :]
     row_basis, col_basis, w_out, down_out, right_out, staged, sems = refs
@@ -286,7 +275,7 @@
         right_out[l] = jnp.where(even, col[:rank], col[rank:])
         old = [f[at, :] for f in pairs[1::2] for at in (row_at, col_at)]
         factors = jnp.concatenate(old + [row.astype(BF16), col.astype(BF16)], axis=0)
-        ref, at = layer_of((w_a, w_b, w_c), l)
+        ref, at = layer_of((w_a, w_c), l)
         for c in range(depth // chunk):
             part = slice(c * chunk, (c + 1) * chunk)
             old = [b[rows, part] for b in pairs[::2] for rows in (row_at, col_at)]
@@ -326,33 +315,26 @@
     back_outs = [((stack, depth), BF16, vmem), ((stack, width), F32, vmem), own_factors, own_factors]
     vectors = [pltpu.VMEM((depth // 128, stack, 128), F32)]
 
-    some, more = max(1, count // 5), max(1, 2 * count // 5)
+    some = max(1, 3 * count // 5)
+    above = passed_along(warm_down[0, 0], "row", 1)
+    beside = passed_along(warm_right[0, 0], "col", 1)
     w_a, own_down, own_right = call(
         load_kernel,
         [((some, depth, width), BF16, vmem), own_factors, own_factors],
         (w_hbm, down_hbm, right_hbm),
         [hbm] * 3,
         scratch=[dma((some + 2,))],
-    )
-    above = passed_along(own_down, "row", 1)
-    beside = passed_along(own_right, "col", 1)
-    (w_b,) = call(
-        functools.partial(load_more_kernel, some),
-        [((more, depth, width), BF16, vmem)],
-        (w_hbm,),
-        [hbm],
-        scratch=[dma((more,))],
         flops=100_000_000,
     )
-    rest = count - some - more
+    rest = count - some
     w_c, *products = call(
         first_products_kernel,
         [((rest, depth, width), BF16, vmem)] + product_outs,
-        (w_hbm, w_a, w_b, above, own_down, beside, own_right),
-        [hbm] + [vmem] * 6,
+        (w_hbm, w_a, above, own_down, beside, own_right),
+        [hbm] + [vmem] * 5,
         scratch=[dma((rest,))],
     )
-    w = (w_a, w_b, w_c)
+    w = (w_a, w_c)
     pairs = ()
     for repeat in range(ROUNDS):
         row_keep, up_send, down_send, col_keep, col_send = products
@@ -396,7 +378,7 @@
                 scratch=[pltpu.VMEM((2 * stack, width), F32)],
             )
             pairs = (*pairs, bases, factors)
-    chunk = depth // 3 if depth % 384 == 0 else depth
+    chunk = depth // 6 if depth % 768 == 0 else depth
     new_w, next_down, next_right = local(
         functools.partial(finish_kernel, ROUNDS - 1, chunk),
         [

time: 74.4 us -> 73.8 us (level)
  waiting for transfers between devices: 17.7 us -> 20.8 us
  starting transfers between devices: 29.4 us -> 26.6 us
  Pallas kernels: 26.3 us -> 25.4 us
    ppermute x8, starting transfers between devices: 4.49 us -> 1.63 us  [exchanged(): return lax.ppermute(value, axis, sorted(pairs))]
    ppermute x14, waiting for transfers between devices: 12.6 us -> 14.6 us  [passed_along(): lax.ppermute(value, axis, [(i, (i + by) % devices) for i in range(devices)])]
    ppermute x8, waiting for transfers between devices: 5.12 us -> 6.29 us  [exchanged(): return lax.ppermute(value, axis, sorted(pairs))]
    pallas_call x13 -> x12, Pallas kernels: 26.3 us -> 25.4 us  [call(): pl.pallas_call(kernel, out_shape=[jax.ShapeDtypeStruct(shape, dtype) for...]
  transfers between devices with their start and end apart: 22 -> 22, of which waited for: 12 -> 12; matrix products, arithmetic and copies ran while one was open for 0% -> 0% of each run, Pallas kernels for 16% -> 17%
where the time goes in v5:
time: 73.8 us; the launch traced here: 73.7 us
  starting transfers between devices  26.6 us (36%)
  Pallas kernels  25.4 us (34%)
  waiting for transfers between devices  20.8 us (28%)
  between operations  0.89 us (1%)
    pallas_call x12, Pallas kernels, call(): pl.pallas_call(kernel, out_shape=[jax.ShapeDtypeStruct(shape, dtype) for...  25.4 us
    ppermute x14, starting transfers between devices, passed_along(): lax.ppermute(value, axis, [(i, (i + by) % devices) for i in range(devices)])  24.9 us
    ppermute x14, waiting for transfers between devices, passed_along(): lax.ppermute(value, axis, [(i, (i + by) % devices) for i in range(devices)])  14.6 us
    ppermute x8, waiting for transfers between devices, exchanged(): return lax.ppermute(value, axis, sorted(pairs))  6.29 us
    ppermute x8, starting transfers between devices, exchanged(): return lax.ppermute(value, axis, sorted(pairs))  1.63 us
  transfers between devices with their start and end apart: 22, of which 12 were waited for; matrix products, arithmetic and copies ran while one was open for 0% of the time, Pallas kernels for 17%

profile of v5, /device:TPU:0, one launch (start us, length us, event | category | flops | bytes accessed | tf_op | source)
XLA Modules:
  0.0 73.7 jit_solution(11527012915034660888)
XLA Ops:
  0.6 3.1 %collective-permute-start = (bf16[5,4,512]{2,1,0:T(4,128)(2,1)}, bf16[5,4,512]{2,1,0:T(4,128)(2,1)S(1)}, u32[]{:S(2)}, u32[]{:S(2)}) collective-permute-start(bf16[5,4,512]{2,1,0:T(4,128)(2,1)} %bitcast.8), channel_id=1, source_target_pairs={{0,8},{8,16},{16,24},{24,0},{1,9},{9,17},{17,25},{25,1},{2,10},{10... | collective-permute-start | bytes 61448 | tf_op jit(solution)/shard_map/ppermute | solution.py:22
  3.7 0.0 collective-permute-start.1
  3.7 3.2 %shard_map.58 = (bf16[3,2304,512]{2,1,0:T(8,128)(2,1)S(1)}, bf16[5,4,512]{2,1,0:T(4,128)(2,1)S(1)}, bf16[5,4,512]{2,1,0:T(4,128)(2,1)S(1)}) custom-call(bf16[5,2304,512]{2,1,0:T(8,128)(2,1)} %bitcast.6, bf16[5,4,512]{2,1,0:T(4,128)(2,1)} %bitcast.9, bf16[5,4,512]{2,1,0:T(4,128)(2,1)} %bitcast.11), custom_call_target="tpu_custom_call" | custom-call | flops 100000000 | tf_op jit(solution)/shard_map/pallas_call | solution.py:42
  6.9 0.8 %collective-permute-done.up_ref = bf16[5,4,512]{2,1,0:T(4,128)(2,1)S(1)} collective-permute-done((bf16[5,4,512]{2,1,0:T(4,128)(2,1)}, bf16[5,4,512]{2,1,0:T(4,128)(2,1)S(1)}, u32[]{:S(2)}, u32[]{:S(2)}) %collective-permute-start) | collective-permute-done | bytes 20512 | tf_op jit(solution)/shard_map/ppermute | solution.py:22
  7.7 0.0 collective-permute-done.1.left_ref
  7.7 3.6 %shard_map.59 = (bf16[2,2304,512]{2,1,0:T(8,128)(2,1)S(1)}, f32[5,8,2304]{2,1,0:T(8,128)S(1)}, bf16[5,4,2304]{2,1,0:T(4,128)(2,1)S(1)}, bf16[5,4,2304]{2,1,0:T(4...) custom-call(bf16[5,2304,512]{2,1,0:T(8,128)(2,1)} %bitcast.7, ...), custom_call_target="tpu_custom_call" | custom-call | flops 1000000 | tf_op jit(solution)/shard_map/pallas_call | solution.py:42
  11.3 1.0 %collective-permute-start.2 = (bf16[5,4,2304]{2,1,0:T(4,128)(2,1)S(1)}, bf16[5,4,2304]{2,1,0:T(4,128)(2,1)S(1)}, u32[]{:S(2)}, u32[]{:S(2)}) collective-permute-start(bf16[5,4,2304]{2,1,0:T(4,128)(2,1)S(1)} %get-tuple-element.53), channel_id=1, source_target_pairs={{0,8},{8,16},{16,24},{24,0},{1,9},{9,17},{17,25},{25,1},{2,10},{10... | collective-permute-start | bytes 276488 | tf_op jit(solution)/shard_map/ppermute | solution.py:22
  12.4 2.8 %collective-permute-start.3 = (bf16[5,4,2304]{2,1,0:T(4,128)(2,1)S(1)}, bf16[5,4,2304]{2,1,0:T(4,128)(2,1)S(1)}, u32[]{:S(2)}, u32[]{:S(2)}) collective-permute-start(bf16[5,4,2304]{2,1,0:T(4,128)(2,1)S(1)} %get-tuple-element.54), channel_id=1, source_target_pairs={{0,24},{8,0},{16,8},{24,16},{1,25},{9,1},{17,9},{25,17},{2,26},{10... | collective-permute-start | bytes 276488 | tf_op jit(solution)/shard_map/ppermute | solution.py:22
  15.2 1.7 %collective-permute-start.5 = (bf16[5,8,2304]{2,1,0:T(8,128)(2,1)S(1)}, bf16[5,8,2304]{2,1,0:T(8,128)(2,1)S(1)}, u32[]{:S(2)}, u32[]{:S(2)}) collective-permute-start(bf16[5,8,2304]{2,1,0:T(8,128)(2,1)S(1)} %get-tuple-element.59), channel_id=1, source_target_pairs={{0,1},{1,0},{2,3},{3,2},{4,5},{5,4},{6,7},{7,6},{8,9},{9,8},{10,11... | collective-permute-start | bytes 552968 | tf_op jit(solution)/shard_map/ppermute | solution.py:22
  16.9 1.8 %collective-permute-done.2.from_above = bf16[5,4,2304]{2,1,0:T(4,128)(2,1)S(1)} collective-permute-done((bf16[5,4,2304]{2,1,0:T(4,128)(2,1)S(1)}, bf16[5,4,2304]{2,1,0:T(4,128)(2,1)S(1)}, u32[]{:S(2)}, u32[]{:S(2)}) %collective-permute-start.2) | collective-permute-done | bytes 92192 | tf_op jit(solution)/shard_map/ppermute | solution.py:22
  18.7 1.0 %collective-permute-done.3.from_below = bf16[5,4,2304]{2,1,0:T(4,128)(2,1)S(1)} collective-permute-done((bf16[5,4,2304]{2,1,0:T(4,128)(2,1)S(1)}, bf16[5,4,2304]{2,1,0:T(4,128)(2,1)S(1)}, u32[]{:S(2)}, u32[]{:S(2)}) %collective-permute-start.3) | collective-permute-done | bytes 92192 | tf_op jit(solution)/shard_map/ppermute | solution.py:22
  19.7 0.1 shard_map.60
  19.8 1.6 %collective-permute-start.4 = (bf16[5,8,2304]{2,1,0:T(8,128)(2,1)S(1)}, bf16[5,8,2304]{2,1,0:T(8,128)(2,1)S(1)}, u32[]{:S(2)}, u32[]{:S(2)}) collective-permute-start(bf16[5,8,2304]{2,1,0:T(8,128)(2,1)S(1)} %get-tuple-element.56), channel_id=1, source_target_pairs={{0,1},{1,0},{2,3},{3,2},{4,5},{5,4},{6,7},{7,6},{8,9},{9,8},{10,11... | collective-permute-start | bytes 552968 | tf_op jit(solution)/shard_map/ppermute | solution.py:22
  21.4 0.6 collective-permute-done.5.refs_0_
  22.0 0.1 shard_map.62
  22.0 0.1 collective-permute-start.6
  22.1 0.8 %collective-permute-start.7 = (bf16[5,4,2304]{2,1,0:T(4,128)(2,1)S(1)}, bf16[5,4,2304]{2,1,0:T(4,128)(2,1)S(1)}, u32[]{:S(2)}, u32[]{:S(2)}) collective-permute-start(bf16[5,4,2304]{2,1,0:T(4,128)(2,1)S(1)} %get-tuple-element.62), channel_id=1, source_target_pairs={{0,6},{2,4},{4,2},{6,0},{1,7},{3,5},{5,3},{7,1},{8,14},{10,12},{12... | collective-permute-start | bytes 276488 | tf_op jit(solution)/shard_map/ppermute | solution.py:30
  22.9 3.7 %collective-permute-done.4.refs_0_ = bf16[5,8,2304]{2,1,0:T(8,128)(2,1)S(1)} collective-permute-done((bf16[5,8,2304]{2,1,0:T(8,128)(2,1)S(1)}, bf16[5,8,2304]{2,1,0:T(8,128)(2,1)S(1)}, u32[]{:S(2)}, u32[]{:S(2)}) %collective-permute-start.4) | collective-permute-done | bytes 184352 | tf_op jit(solution)/shard_map/ppermute | solution.py:22
  26.7 2.1 %shard_map.61 = (bf16[40,2304]{1,0:T(8,128)(2,1)S(1)}, f32[40,512]{1,0:T(8,128)S(1)}, bf16[5,4,512]{2,1,0:T(4,128)(2,1)S(1)}, bf16[5,4,512]{2,1,0:T(4,128)(2,1)S(1)}) custom-call(bf16[3,2304,512]{2,1,0:T(8,128)(2,1)S(1)} %get-tuple-element.48.w_a, bf16[2,2304,512]{2,1,0:T(8,128)(2,1)S(1)} %get-tuple-element.51.w_c, ...), custom_call_target="tpu_custom_call" | custom-call | flops 1000000 | tf_op jit(solution)/shard_map/pallas_call | solution.py:42
  28.8 1.2 %collective-permute-start.8 = (bf16[5,4,512]{2,1,0:T(4,128)(2,1)S(1)}, bf16[5,4,512]{2,1,0:T(4,128)(2,1)S(1)}, u32[]{:S(2)}, u32[]{:S(2)}) collective-permute-start(bf16[5,4,512]{2,1,0:T(4,128)(2,1)S(1)} %get-tuple-element.64), channel_id=1, source_target_pairs={{0,8},{8,16},{16,24},{24,0},{1,9},{9,17},{17,25},{25,1},{2,10},{10... | collective-permute-start | bytes 61448 | tf_op jit(solution)/shard_map/ppermute | solution.py:22
  30.0 2.6 %collective-permute-start.9 = (bf16[5,4,512]{2,1,0:T(4,128)(2,1)S(1)}, bf16[5,4,512]{2,1,0:T(4,128)(2,1)S(1)}, u32[]{:S(2)}, u32[]{:S(2)}) collective-permute-start(bf16[5,4,512]{2,1,0:T(4,128)(2,1)S(1)} %get-tuple-element.65), channel_id=1, source_target_pairs={{0,24},{8,0},{16,8},{24,16},{1,25},{9,1},{17,9},{25,17},{2,26},{10... | collective-permute-start | bytes 61448 | tf_op jit(solution)/shard_map/ppermute | solution.py:22
  32.6 2.2 %shard_map.63 = (bf16[40,2304]{1,0:T(8,128)(2,1)S(1)}, f32[40,512]{1,0:T(8,128)S(1)}, bf16[5,4,512]{2,1,0:T(4,128)(2,1)S(1)}, bf16[5,4,512]{2,1,0:T(4,128)(2,1)S(1)}) custom-call(bf16[3,2304,512]{2,1,0:T(8,128)(2,1)S(1)} %get-tuple-element.48.w_a, bf16[2,2304,512]{2,1,0:T(8,128)(2,1)S(1)} %get-tuple-element.51.w_c, ...), custom_call_target="tpu_custom_call" | custom-call | flops 1000000 | tf_op jit(solution)/shard_map/pallas_call | solution.py:42
  34.8 0.0 collective-permute-start.11
  34.9 0.0 collective-permute-done.9.refs_3_
  34.9 1.1 %collective-permute-done.10.refs_4_ = bf16[5,4,512]{2,1,0:T(4,128)(2,1)S(1)} collective-permute-done((bf16[5,4,512]{2,1,0:T(4,128)(2,1)S(1)}, bf16[5,4,512]{2,1,0:T(4,128)(2,1)S(1)}, u32[]{:S(2)}, u32[]{:S(2)}) %collective-permute-start.10) | collective-permute-done | bytes 20512 | tf_op jit(solution)/shard_map/ppermute | solution.py:30
  36.0 2.0 %collective-permute-done.11.refs_5_ = bf16[5,4,512]{2,1,0:T(4,128)(2,1)S(1)} collective-permute-done((bf16[5,4,512]{2,1,0:T(4,128)(2,1)S(1)}, bf16[5,4,512]{2,1,0:T(4,128)(2,1)S(1)}, u32[]{:S(2)}, u32[]{:S(2)}) %collective-permute-start.11) | collective-permute-done | bytes 20512 | tf_op jit(solution)/shard_map/ppermute | solution.py:30
  38.1 3.5 %shard_map.64 = (bf16[80,2304]{1,0:T(8,128)(2,1)S(1)}, bf16[80,512]{1,0:T(8,128)(2,1)S(1)}, f32[5,8,2304]{2,1,0:T(8,128)S(1)}, bf16[5,4,2304]{2,1,0:T(4,128)(2,1...) custom-call(bf16[3,2304,512]{2,1,0:T(8,128)(2,1)S(1)} %get-tuple-element.48.w_a, ...), custom_call_target="tpu_custom_call" | custom-call | flops 1000000 | tf_op jit(solution)/shard_map/pallas_call | solution.py:42
  41.6 0.0 collective-permute-start.12
  41.6 3.8 %collective-permute-start.13 = (bf16[5,4,2304]{2,1,0:T(4,128)(2,1)S(1)}, bf16[5,4,2304]{2,1,0:T(4,128)(2,1)S(1)}, u32[]{:S(2)}, u32[]{:S(2)}) collective-permute-start(bf16[5,4,2304]{2,1,0:T(4,128)(2,1)S(1)} %get-tuple-element.72), channel_id=1, source_target_pairs={{0,24},{8,0},{16,8},{24,16},{1,25},{9,1},{17,9},{25,17},{2,26},{10... | collective-permute-start | bytes 276488 | tf_op jit(solution)/shard_map/ppermute | solution.py:22
  45.4 1.5 %collective-permute-start.15 = (bf16[5,8,2304]{2,1,0:T(8,128)(2,1)S(1)}, bf16[5,8,2304]{2,1,0:T(8,128)(2,1)S(1)}, u32[]{:S(2)}, u32[]{:S(2)}) collective-permute-start(bf16[5,8,2304]{2,1,0:T(8,128)(2,1)S(1)} %get-tuple-element.79), channel_id=1, source_target_pairs={{0,1},{1,0},{2,3},{3,2},{4,5},{5,4},{6,7},{7,6},{8,9},{9,8},{10,11... | collective-permute-start | bytes 552968 | tf_op jit(solution)/shard_map/ppermute | solution.py:22
  47.0 2.0 %collective-permute-done.12.from_above = bf16[5,4,2304]{2,1,0:T(4,128)(2,1)S(1)} collective-permute-done((bf16[5,4,2304]{2,1,0:T(4,128)(2,1)S(1)}, bf16[5,4,2304]{2,1,0:T(4,128)(2,1)S(1)}, u32[]{:S(2)}, u32[]{:S(2)}) %collective-permute-start.12) | collective-permute-done | bytes 92192 | tf_op jit(solution)/shard_map/ppermute | solution.py:22
  48.9 0.0 collective-permute-done.13.from_below
  48.9 0.1 shard_map.65
  49.0 1.6 %collective-permute-start.14 = (bf16[5,8,2304]{2,1,0:T(8,128)(2,1)S(1)}, bf16[5,8,2304]{2,1,0:T(8,128)(2,1)S(1)}, u32[]{:S(2)}, u32[]{:S(2)}) collective-permute-start(bf16[5,8,2304]{2,1,0:T(8,128)(2,1)S(1)} %get-tuple-element.74), channel_id=1, source_target_pairs={{0,1},{1,0},{2,3},{3,2},{4,5},{5,4},{6,7},{7,6},{8,9},{9,8},{10,11... | collective-permute-start | bytes 552968 | tf_op jit(solution)/shard_map/ppermute | solution.py:22
  50.6 2.3 %collective-permute-done.15.refs_0_ = bf16[5,8,2304]{2,1,0:T(8,128)(2,1)S(1)} collective-permute-done((bf16[5,8,2304]{2,1,0:T(8,128)(2,1)S(1)}, bf16[5,8,2304]{2,1,0:T(8,128)(2,1)S(1)}, u32[]{:S(2)}, u32[]{:S(2)}) %collective-permute-start.15) | collective-permute-done | bytes 184352 | tf_op jit(solution)/shard_map/ppermute | solution.py:22
  52.9 0.1 shard_map.67
  53.0 0.1 collective-permute-start.16
  53.1 0.5 collective-permute-start.17
  53.6 2.3 %collective-permute-done.14.refs_0_ = bf16[5,8,2304]{2,1,0:T(8,128)(2,1)S(1)} collective-permute-done((bf16[5,8,2304]{2,1,0:T(8,128)(2,1)S(1)}, bf16[5,8,2304]{2,1,0:T(8,128)(2,1)S(1)}, u32[]{:S(2)}, u32[]{:S(2)}) %collective-permute-start.14) | collective-permute-done | bytes 184352 | tf_op jit(solution)/shard_map/ppermute | solution.py:22
  55.8 2.5 %shard_map.66 = (bf16[40,2304]{1,0:T(8,128)(2,1)S(1)}, f32[40,512]{1,0:T(8,128)S(1)}, bf16[5,4,512]{2,1,0:T(4,128)(2,1)S(1)}, bf16[5,4,512]{2,1,0:T(4,128)(2,1)S(1)}) custom-call(bf16[3,2304,512]{2,1,0:T(8,128)(2,1)S(1)} %get-tuple-element.48.w_a, bf16[2,2304,512]{2,1,0:T(8,128)(2,1)S(1)} %get-tuple-element.51.w_c, ...), custom_call_target="tpu_custom_call" | custom-call | flops 1000000 | tf_op jit(solution)/shard_map/pallas_call | solution.py:42
  58.4 0.0 collective-permute-start.18
  58.4 3.8 %collective-permute-start.19 = (bf16[5,4,512]{2,1,0:T(4,128)(2,1)S(1)}, bf16[5,4,512]{2,1,0:T(4,128)(2,1)S(1)}, u32[]{:S(2)}, u32[]{:S(2)}) collective-permute-start(bf16[5,4,512]{2,1,0:T(4,128)(2,1)S(1)} %get-tuple-element.85), channel_id=1, source_target_pairs={{0,24},{8,0},{16,8},{24,16},{1,25},{9,1},{17,9},{25,17},{2,26},{10... | collective-permute-start | bytes 61448 | tf_op jit(solution)/shard_map/ppermute | solution.py:22
  62.2 2.6 %shard_map.68 = (bf16[40,2304]{1,0:T(8,128)(2,1)S(1)}, f32[40,512]{1,0:T(8,128)S(1)}, bf16[5,4,512]{2,1,0:T(4,128)(2,1)S(1)}, bf16[5,4,512]{2,1,0:T(4,128)(2,1)S(1)}) custom-call(bf16[3,2304,512]{2,1,0:T(8,128)(2,1)S(1)} %get-tuple-element.48.w_a, bf16[2,2304,512]{2,1,0:T(8,128)(2,1)S(1)} %get-tuple-element.51.w_c, ...), custom_call_target="tpu_custom_call" | custom-call | flops 1000000 | tf_op jit(solution)/shard_map/pallas_call | solution.py:42
  64.8 0.0 collective-permute-start.20
  64.8 0.1 collective-permute-start.21
  64.9 1.1 %collective-permute-done.20.refs_4_ = bf16[5,4,512]{2,1,0:T(4,128)(2,1)S(1)} collective-permute-done((bf16[5,4,512]{2,1,0:T(4,128)(2,1)S(1)}, bf16[5,4,512]{2,1,0:T(4,128)(2,1)S(1)}, u32[]{:S(2)}, u32[]{:S(2)}) %collective-permute-start.20) | collective-permute-done | bytes 20512 | tf_op jit(solution)/shard_map/ppermute | solution.py:30
  66.0 2.0 %collective-permute-done.21.refs_5_ = bf16[5,4,512]{2,1,0:T(4,128)(2,1)S(1)} collective-permute-done((bf16[5,4,512]{2,1,0:T(4,128)(2,1)S(1)}, bf16[5,4,512]{2,1,0:T(4,128)(2,1)S(1)}, u32[]{:S(2)}, u32[]{:S(2)}) %collective-permute-start.21) | collective-permute-done | bytes 20512 | tf_op jit(solution)/shard_map/ppermute | solution.py:30
  68.0 5.5 %shard_map.69 = (bf16[5,2304,512]{2,1,0:T(8,128)(2,1)}, f32[5,4,512]{2,1,0:T(4,128)}, f32[5,4,512]{2,1,0:T(4,128)}) custom-call(bf16[3,2304,512]{2,1,0:T(8,128)(2,1)S(1)} %get-tuple-element.48.w_a, bf16[2,2304,512]{2,1,0:T(8,128)(2,1)S(1)} %get-tuple-element.51.w_c, f32[40,512]{1,0:T(8,128)S(1)} %get-tuple-element.77.refs_0_, ...), custom_call_target="tpu_custom_call" | custom-call | flops 1000000 | tf_op jit(solution)/shard_map/pallas_call | solution.py:42
  (8 shorter events, 0.0 us)
Async XLA Ops:
  0.6 7.1 %collective-permute-start = (bf16[5,4,512]{2,1,0:T(4,128)(2,1)}, bf16[5,4,512]{2,1,0:T(4,128)(2,1)S(1)}, u32[]{:S(2)}, u32[]{:S(2)}) collective-permute-start(bf16[5,4,512]{2,1,0:T(4,128)(2,1)} %bitcast.8), channel_id=1, source_target_pairs={{0,8},{8,16},{16,24},{24,0},{1,9},{9,17},{17,25},{25,1},{2,10},{10... | collective-permute-start | bytes 61448 | tf_op jit(solution)/shard_map/ppermute | solution.py:22
  3.7 4.0 %collective-permute-start.1 = (bf16[5,4,512]{2,1,0:T(4,128)(2,1)}, bf16[5,4,512]{2,1,0:T(4,128)(2,1)S(1)}, u32[]{:S(2)}, u32[]{:S(2)}) collective-permute-start(bf16[5,4,512]{2,1,0:T(4,128)(2,1)} %bitcast.10), channel_id=1, source_target_pairs={{0,2},{2,4},{4,6},{6,0},{1,3},{3,5},{5,7},{7,1},{8,10},{10,12},{12... | collective-permute-start | bytes 61448 | tf_op jit(solution)/shard_map/ppermute | solution.py:22
  11.3 7.4 %collective-permute-start.2 = (bf16[5,4,2304]{2,1,0:T(4,128)(2,1)S(1)}, bf16[5,4,2304]{2,1,0:T(4,128)(2,1)S(1)}, u32[]{:S(2)}, u32[]{:S(2)}) collective-permute-start(bf16[5,4,2304]{2,1,0:T(4,128)(2,1)S(1)} %get-tuple-element.53), channel_id=1, source_target_pairs={{0,8},{8,16},{16,24},{24,0},{1,9},{9,17},{17,25},{25,1},{2,10},{10... | collective-permute-start | bytes 276488 | tf_op jit(solution)/shard_map/ppermute | solution.py:22
  12.4 7.4 %collective-permute-start.3 = (bf16[5,4,2304]{2,1,0:T(4,128)(2,1)S(1)}, bf16[5,4,2304]{2,1,0:T(4,128)(2,1)S(1)}, u32[]{:S(2)}, u32[]{:S(2)}) collective-permute-start(bf16[5,4,2304]{2,1,0:T(4,128)(2,1)S(1)} %get-tuple-element.54), channel_id=1, source_target_pairs={{0,24},{8,0},{16,8},{24,16},{1,25},{9,1},{17,9},{25,17},{2,26},{10... | collective-permute-start | bytes 276488 | tf_op jit(solution)/shard_map/ppermute | solution.py:22
  15.2 6.8 %collective-permute-start.5 = (bf16[5,8,2304]{2,1,0:T(8,128)(2,1)S(1)}, bf16[5,8,2304]{2,1,0:T(8,128)(2,1)S(1)}, u32[]{:S(2)}, u32[]{:S(2)}) collective-permute-start(bf16[5,8,2304]{2,1,0:T(8,128)(2,1)S(1)} %get-tuple-element.59), channel_id=1, source_target_pairs={{0,1},{1,0},{2,3},{3,2},{4,5},{5,4},{6,7},{7,6},{8,9},{9,8},{10,11... | collective-permute-start | bytes 552968 | tf_op jit(solution)/shard_map/ppermute | solution.py:22
  19.8 6.9 %collective-permute-start.4 = (bf16[5,8,2304]{2,1,0:T(8,128)(2,1)S(1)}, bf16[5,8,2304]{2,1,0:T(8,128)(2,1)S(1)}, u32[]{:S(2)}, u32[]{:S(2)}) collective-permute-start(bf16[5,8,2304]{2,1,0:T(8,128)(2,1)S(1)} %get-tuple-element.56), channel_id=1, source_target_pairs={{0,1},{1,0},{2,3},{3,2},{4,5},{5,4},{6,7},{7,6},{8,9},{9,8},{10,11... | collective-permute-start | bytes 552968 | tf_op jit(solution)/shard_map/ppermute | solution.py:22
  22.0 10.6 %collective-permute-start.6 = (bf16[5,4,2304]{2,1,0:T(4,128)(2,1)S(1)}, bf16[5,4,2304]{2,1,0:T(4,128)(2,1)S(1)}, u32[]{:S(2)}, u32[]{:S(2)}) collective-permute-start(bf16[5,4,2304]{2,1,0:T(4,128)(2,1)S(1)} %get-tuple-element.61), channel_id=1, source_target_pairs={{0,2},{2,0},{4,6},{6,4},{1,3},{3,1},{5,7},{7,5},{8,10},{10,8},{12,... | collective-permute-start | bytes 276488 | tf_op jit(solution)/shard_map/ppermute | solution.py:30
  22.1 10.5 %collective-permute-start.7 = (bf16[5,4,2304]{2,1,0:T(4,128)(2,1)S(1)}, bf16[5,4,2304]{2,1,0:T(4,128)(2,1)S(1)}, u32[]{:S(2)}, u32[]{:S(2)}) collective-permute-start(bf16[5,4,2304]{2,1,0:T(4,128)(2,1)S(1)} %get-tuple-element.62), channel_id=1, source_target_pairs={{0,6},{2,4},{4,2},{6,0},{1,7},{3,5},{5,3},{7,1},{8,14},{10,12},{12... | collective-permute-start | bytes 276488 | tf_op jit(solution)/shard_map/ppermute | solution.py:30
  28.8 6.0 %collective-permute-start.8 = (bf16[5,4,512]{2,1,0:T(4,128)(2,1)S(1)}, bf16[5,4,512]{2,1,0:T(4,128)(2,1)S(1)}, u32[]{:S(2)}, u32[]{:S(2)}) collective-permute-start(bf16[5,4,512]{2,1,0:T(4,128)(2,1)S(1)} %get-tuple-element.64), channel_id=1, source_target_pairs={{0,8},{8,16},{16,24},{24,0},{1,9},{9,17},{17,25},{25,1},{2,10},{10... | collective-permute-start | bytes 61448 | tf_op jit(solution)/shard_map/ppermute | solution.py:22
  30.0 4.9 %collective-permute-start.9 = (bf16[5,4,512]{2,1,0:T(4,128)(2,1)S(1)}, bf16[5,4,512]{2,1,0:T(4,128)(2,1)S(1)}, u32[]{:S(2)}, u32[]{:S(2)}) collective-permute-start(bf16[5,4,512]{2,1,0:T(4,128)(2,1)S(1)} %get-tuple-element.65), channel_id=1, source_target_pairs={{0,24},{8,0},{16,8},{24,16},{1,25},{9,1},{17,9},{25,17},{2,26},{10... | collective-permute-start | bytes 61448 | tf_op jit(solution)/shard_map/ppermute | solution.py:22
  34.8 1.2 %collective-permute-start.10 = (bf16[5,4,512]{2,1,0:T(4,128)(2,1)S(1)}, bf16[5,4,512]{2,1,0:T(4,128)(2,1)S(1)}, u32[]{:S(2)}, u32[]{:S(2)}) collective-permute-start(bf16[5,4,512]{2,1,0:T(4,128)(2,1)S(1)} %get-tuple-element.66), channel_id=1, source_target_pairs={{0,2},{2,0},{4,6},{6,4},{1,3},{3,1},{5,7},{7,5},{8,10},{10,8},{12,... | collective-permute-start | bytes 61448 | tf_op jit(solution)/shard_map/ppermute | solution.py:30
  34.8 3.2 %collective-permute-start.11 = (bf16[5,4,512]{2,1,0:T(4,128)(2,1)S(1)}, bf16[5,4,512]{2,1,0:T(4,128)(2,1)S(1)}, u32[]{:S(2)}, u32[]{:S(2)}) collective-permute-start(bf16[5,4,512]{2,1,0:T(4,128)(2,1)S(1)} %get-tuple-element.67), channel_id=1, source_target_pairs={{0,6},{2,4},{4,2},{6,0},{1,7},{3,5},{5,3},{7,1},{8,14},{10,12},{12... | collective-permute-start | bytes 61448 | tf_op jit(solution)/shard_map/ppermute | solution.py:30
  41.6 7.4 %collective-permute-start.12 = (bf16[5,4,2304]{2,1,0:T(4,128)(2,1)S(1)}, bf16[5,4,2304]{2,1,0:T(4,128)(2,1)S(1)}, u32[]{:S(2)}, u32[]{:S(2)}) collective-permute-start(bf16[5,4,2304]{2,1,0:T(4,128)(2,1)S(1)} %get-tuple-element.71), channel_id=1, source_target_pairs={{0,8},{8,16},{16,24},{24,0},{1,9},{9,17},{17,25},{25,1},{2,10},{10... | collective-permute-start | bytes 276488 | tf_op jit(solution)/shard_map/ppermute | solution.py:22
  41.6 7.3 %collective-permute-start.13 = (bf16[5,4,2304]{2,1,0:T(4,128)(2,1)S(1)}, bf16[5,4,2304]{2,1,0:T(4,128)(2,1)S(1)}, u32[]{:S(2)}, u32[]{:S(2)}) collective-permute-start(bf16[5,4,2304]{2,1,0:T(4,128)(2,1)S(1)} %get-tuple-element.72), channel_id=1, source_target_pairs={{0,24},{8,0},{16,8},{24,16},{1,25},{9,1},{17,9},{25,17},{2,26},{10... | collective-permute-start | bytes 276488 | tf_op jit(solution)/shard_map/ppermute | solution.py:22
  45.4 7.5 %collective-permute-start.15 = (bf16[5,8,2304]{2,1,0:T(8,128)(2,1)S(1)}, bf16[5,8,2304]{2,1,0:T(8,128)(2,1)S(1)}, u32[]{:S(2)}, u32[]{:S(2)}) collective-permute-start(bf16[5,8,2304]{2,1,0:T(8,128)(2,1)S(1)} %get-tuple-element.79), channel_id=1, source_target_pairs={{0,1},{1,0},{2,3},{3,2},{4,5},{5,4},{6,7},{7,6},{8,9},{9,8},{10,11... | collective-permute-start | bytes 552968 | tf_op jit(solution)/shard_map/ppermute | solution.py:22
  49.0 6.8 %collective-permute-start.14 = (bf16[5,8,2304]{2,1,0:T(8,128)(2,1)S(1)}, bf16[5,8,2304]{2,1,0:T(8,128)(2,1)S(1)}, u32[]{:S(2)}, u32[]{:S(2)}) collective-permute-start(bf16[5,8,2304]{2,1,0:T(8,128)(2,1)S(1)} %get-tuple-element.74), channel_id=1, source_target_pairs={{0,1},{1,0},{2,3},{3,2},{4,5},{5,4},{6,7},{7,6},{8,9},{9,8},{10,11... | collective-permute-start | bytes 552968 | tf_op jit(solution)/shard_map/ppermute | solution.py:22
  53.0 9.2 %collective-permute-start.16 = (bf16[5,4,2304]{2,1,0:T(4,128)(2,1)S(1)}, bf16[5,4,2304]{2,1,0:T(4,128)(2,1)S(1)}, u32[]{:S(2)}, u32[]{:S(2)}) collective-permute-start(bf16[5,4,2304]{2,1,0:T(4,128)(2,1)S(1)} %get-tuple-element.81), channel_id=1, source_target_pairs={{0,2},{2,0},{4,6},{6,4},{1,3},{3,1},{5,7},{7,5},{8,10},{10,8},{12,... | collective-permute-start | bytes 276488 | tf_op jit(solution)/shard_map/ppermute | solution.py:30
  53.1 9.1 %collective-permute-start.17 = (bf16[5,4,2304]{2,1,0:T(4,128)(2,1)S(1)}, bf16[5,4,2304]{2,1,0:T(4,128)(2,1)S(1)}, u32[]{:S(2)}, u32[]{:S(2)}) collective-permute-start(bf16[5,4,2304]{2,1,0:T(4,128)(2,1)S(1)} %get-tuple-element.82), channel_id=1, source_target_pairs={{0,6},{2,4},{4,2},{6,0},{1,7},{3,5},{5,3},{7,1},{8,14},{10,12},{12... | collective-permute-start | bytes 276488 | tf_op jit(solution)/shard_map/ppermute | solution.py:30
  58.4 6.5 %collective-permute-start.18 = (bf16[5,4,512]{2,1,0:T(4,128)(2,1)S(1)}, bf16[5,4,512]{2,1,0:T(4,128)(2,1)S(1)}, u32[]{:S(2)}, u32[]{:S(2)}) collective-permute-start(bf16[5,4,512]{2,1,0:T(4,128)(2,1)S(1)} %get-tuple-element.84), channel_id=1, source_target_pairs={{0,8},{8,16},{16,24},{24,0},{1,9},{9,17},{17,25},{25,1},{2,10},{10... | collective-permute-start | bytes 61448 | tf_op jit(solution)/shard_map/ppermute | solution.py:22
  58.4 6.5 %collective-permute-start.19 = (bf16[5,4,512]{2,1,0:T(4,128)(2,1)S(1)}, bf16[5,4,512]{2,1,0:T(4,128)(2,1)S(1)}, u32[]{:S(2)}, u32[]{:S(2)}) collective-permute-start(bf16[5,4,512]{2,1,0:T(4,128)(2,1)S(1)} %get-tuple-element.85), channel_id=1, source_target_pairs={{0,24},{8,0},{16,8},{24,16},{1,25},{9,1},{17,9},{25,17},{2,26},{10... | collective-permute-start | bytes 61448 | tf_op jit(solution)/shard_map/ppermute | solution.py:22
  64.8 1.2 %collective-permute-start.20 = (bf16[5,4,512]{2,1,0:T(4,128)(2,1)S(1)}, bf16[5,4,512]{2,1,0:T(4,128)(2,1)S(1)}, u32[]{:S(2)}, u32[]{:S(2)}) collective-permute-start(bf16[5,4,512]{2,1,0:T(4,128)(2,1)S(1)} %get-tuple-element.86), channel_id=1, source_target_pairs={{0,2},{2,0},{4,6},{6,4},{1,3},{3,1},{5,7},{7,5},{8,10},{10,8},{12,... | collective-permute-start | bytes 61448 | tf_op jit(solution)/shard_map/ppermute | solution.py:30
  64.8 3.2 %collective-permute-start.21 = (bf16[5,4,512]{2,1,0:T(4,128)(2,1)S(1)}, bf16[5,4,512]{2,1,0:T(4,128)(2,1)S(1)}, u32[]{:S(2)}, u32[]{:S(2)}) collective-permute-start(bf16[5,4,512]{2,1,0:T(4,128)(2,1)S(1)} %get-tuple-element.87), channel_id=1, source_target_pairs={{0,6},{2,4},{4,2},{6,0},{1,7},{3,5},{5,3},{7,1},{8,14},{10,12},{12... | collective-permute-start | bytes 61448 | tf_op jit(solution)/shard_map/ppermute | solution.py:30
